TPU v7x, 512 devices: a whole 4x8x8 slice. The times are simulated.
512 devices in a mesh: gy: 4 (over x), gx: 4 (over z_hi, core), probe: 32 (over y, z_lo).
Axes of the slice: x: 4, y: 8, z: 8 (z_hi: 2, z_lo: 4; z = z_hi * 4 + z_lo), core: 2. Of those that a mesh axis runs over, the one named last changes fastest.
Arguments:
- state: bfloat16 [4, 16, 16, 640], P(None, 'gy', 'gx'), may hold values from -6 to 6
- probe_signs: int32 [64, 4, 16, 16, 640], P('probe', None, 'gy', 'gx'), may hold values from -1 to 1, as said below
- timesteps: int32 [4], replicated, may hold values from 0 to 999
- time_table: float32 [1000, 640], replicated, may hold values from -4 to 4
- gn_gain: float32 [640], replicated, may hold values from 0.5 to 1.5
- gn_shift: float32 [640], replicated, may hold values from -3 to 3
- conv_weight: bfloat16 [9, 640, 640], P(None, 'probe'), may hold values from -0.078125 to 0.078125
- conv_bias: float32 [640], replicated, may hold values from -3 to 3
Outputs:
- next_state: bfloat16 [4, 16, 16, 640], P(None, 'gy', 'gx')
- logp_delta: float32 [4], replicated
Inputs may be any that keep to these rules, and one draw needn't show every extreme that they name: `probe_signs`: every entry is -1 or 1.
All inputs are finite; a program needn't handle non-finite values.
Results may differ from a plain program's by a relative error of at most 0.0034.
Values may be sent and summed in bfloat16 or wider, within the bound.
No kernel may reach another device: no remote copies, remote signals or barrier semaphores. Data moves between devices by JAX's collectives and lax.ppermute only.
A program may use at most 64 MiB of HBM per device.

v0:
```python
import jax
import jax.numpy as jnp
from jax import lax
from jax.sharding import Mesh
from jax.sharding import PartitionSpec as P

GROUPS = 32
GX = ("gx_0", "gx_1")
GY_GX = ("gy", "gx_0", "gx_1")
PROBE = ("probe_0", "probe_1")
GY_GX_PROBE = ("gy", "gx_0", "gx_1", "probe_0", "probe_1")


def packed_total(arrays, axis):
    flat, at, outs = (jnp.concatenate([a.reshape(-1) for a in arrays]), 0, [])
    total = lax.psum(flat, axis)
    for a in arrays:
        outs.append(total[at : at + a.size].reshape(a.shape))
        at += a.size
    return tuple(outs)


def with_halo(block, sides, width):
    for axis, dim in sides:
        count = lax.axis_size(axis)
        forward = [(i, i + 1) for i in range(count - 1)]
        backward = [(target, source) for source, target in forward]
        low = lax.ppermute(
            lax.slice_in_dim(block, block.shape[dim] - width, None, axis=dim), axis, forward
        )
        high = lax.ppermute(lax.slice_in_dim(block, 0, width, axis=dim), axis, backward)
        block = jnp.concatenate([low, block, high], axis=dim)
    return block


def gathered_by_axis(value, axes, dim):
    if not axes:
        return value
    nearer = lax.all_gather(value, axes[-1], axis=dim, tiled=True)
    return gathered_by_axis(nearer, axes[:-1], dim)


def one_axis_at_a_time(value, axes):
    for axis in axes:
        value = lax.psum(value, axis)
    return value


def local_conv(padded, weight, height, width):
    count = padded.shape[0]
    chans = padded.shape[3]
    total = jnp.zeros((count * height * width, weight.shape[2]), jnp.float32)
    for tap in range(9):
        row_off = tap // 3
        col_off = tap % 3
        window = padded[:, row_off : row_off + height, col_off : col_off + width, :].reshape(
            -1, chans
        )
        total = total + jnp.dot(window, weight[tap], preferred_element_type=jnp.float32)
    return total


def body(state, probe_signs, timesteps, time_table, gn_gain, gn_shift, conv_weight, conv_bias):
    batch, tile_h, tile_w, chans = state.shape
    probes_here = probe_signs.shape[0]
    group_width = chans // GROUPS
    count = tile_h * lax.axis_size("gy") * tile_w * lax.axis_size(GX) * group_width
    xf = state.astype(jnp.float32)
    signs = probe_signs.astype(jnp.float32)
    grouped = xf.reshape(batch, tile_h, tile_w, GROUPS, group_width)
    signs_grouped = signs.reshape(probes_here, batch, tile_h, tile_w, GROUPS, group_width)
    sum_x = jnp.sum(grouped, axis=(1, 2, 4))
    sum_xx = jnp.sum(grouped * grouped, axis=(1, 2, 4))
    sum_u = jnp.sum(signs_grouped, axis=(2, 3, 5))
    cross = jnp.sum(signs_grouped * grouped[None], axis=(2, 3, 5))
    sum_x, sum_xx, sum_u, cross = packed_total((sum_x, sum_xx, sum_u, cross), GY_GX)
    mean_x = sum_x / count
    centered = grouped - mean_x[:, None, None, :, None]
    sum_cu = cross - mean_x[None] * sum_u
    var_x = sum_xx / count - mean_x * mean_x
    sigma = jnp.sqrt(var_x + 1e-05)[:, None, None, :, None]
    normal = (centered / sigma).reshape(batch, tile_h, tile_w, chans)
    mean_u = (sum_u / count)[:, :, None, None, :, None]
    mean_cu = (sum_cu / count)[:, :, None, None, :, None]
    dnormal = (signs_grouped - mean_u) / sigma[None] - centered[None] * mean_cu / (
        sigma * sigma * sigma
    )[None]
    dnormal = dnormal.reshape(probes_here, batch, tile_h, tile_w, chans)
    onehot = (
        timesteps[:, None] == jnp.arange(time_table.shape[0], dtype=jnp.int32)[None, :]
    ).astype(jnp.float32)
    embed = jnp.dot(onehot, time_table, precision=lax.Precision.HIGHEST)
    pre = normal * gn_gain + gn_shift + embed[:, None, None, :]
    sig = jax.nn.sigmoid(pre)
    hidden = (pre * sig).astype(jnp.bfloat16)
    slope = sig * (1.0 + pre * (1.0 - sig)) * gn_gain
    dhidden = (slope[None] * dnormal).astype(jnp.bfloat16)
    flat_tangents = dhidden.reshape(probes_here * batch, tile_h, tile_w, chans)
    stacked = jnp.concatenate([hidden, flat_tangents], axis=0)
    items = stacked.shape[0]
    padded = with_halo(stacked, (("gy", 1), (GX, 2)), 1)
    summed = local_conv(padded, gathered_by_axis(conv_weight, PROBE, 1), tile_h, tile_w)
    conv_out = summed.reshape(items, tile_h, tile_w, chans)
    conv_primal = conv_out[:batch]
    tangent = conv_out[batch:].reshape(probes_here, batch, tile_h, tile_w, chans)
    partial_sum = jnp.sum(signs * tangent, axis=(0, 2, 3, 4))
    velocity = conv_primal + conv_bias
    next_state = (xf + 0.25 * velocity).astype(jnp.bfloat16)
    total = one_axis_at_a_time(partial_sum, GY_GX_PROBE)
    logp_delta = -0.25 / (probes_here * lax.axis_size(PROBE)) * total
    return (next_state, logp_delta)


def solution(mesh):
    split = Mesh(
        mesh.devices.reshape(mesh.shape["gy"], 2, 2, 8, 4),
        ("gy", "gx_0", "gx_1", "probe_0", "probe_1"),
    )
    return jax.shard_map(
        body,
        mesh=split,
        in_specs=(
            P(None, "gy", GX, None),
            P(PROBE, None, "gy", GX, None),
            P(),
            P(),
            P(),
            P(),
            P(None, PROBE, None),
            P(),
        ),
        out_specs=(P(None, "gy", GX, None), P()),
        check_vma=False,
    )
```

profile of v0, /device:TPU:8, one launch (start us, length us, event | category | flops | bytes accessed | tf_op | source)
XLA Modules:
  0.0 207.5 jit_solution(9103604304009968341)
XLA Ops:
  7.2 1.2 copy.11
  8.4 33.5 %all_gather.6 = bf16[9,80,640]{2,0,1:T(8,128)(2,1)S(1)} all-gather(bf16[9,20,640]{2,0,1:T(8,128)(2,1)S(1)} %copy.11), channel_id=1, replica_groups=mesh['gy'=4,'gx_0'=2,'gx_1'=2,'probe_0'=8,'probe_1'=4] {'probe_1'}, dimensions={1}, use_global_device_ids=true | all-gather | bytes 1152000 | tf_op jit(solution)/shard_map/all_gather | solution.py:39
  41.9 1.1 copy.12
  43.1 0.2 convert_reduce_fusion
  43.3 0.2 reduce_sum.83
  43.4 0.1 reduce_sum.84
  43.6 0.2 reduce_sum.80
  43.8 0.1 reduce_sum.81
  44.0 0.1 convert_reduce_fusion.1
  44.1 0.1 reduce_sum.61
  44.2 0.1 reduce_sum.62
  44.4 0.1 reduce_sum.55
  44.6 0.1 reduce_sum.59
  44.7 49.8 %psum.42 = f32[768]{0:T(1024)S(1)} all-reduce(f32[768]{0:T(1024)S(1)} %pad_maximum_fusion.7), channel_id=1, replica_groups=mesh['gy'=4,'gx_0'=2,'gx_1'=2,'probe_0'=8,'probe_1'=4] {'gy','gx_0','gx_1'}, use_global_device_ids=true, to_apply=%region_8.0 | all-reduce | flops 768 | bytes 6144 | tf_op jit(solution)/shard_map/psum | solution.py:16
  94.9 0.1 div.68
  95.2 0.1 mul.133
  95.3 0.1 mul.134
  95.5 0.1 div.59
  95.7 0.1 sub.60
  95.8 0.1 sub.65
  95.9 0.1 sub.66
  96.1 0.9 fusion.5
  97.0 0.2 multiply_convert_fusion.1
  97.2 0.2 multiply_convert_fusion
  97.5 1.3 collective-permute-start.1
  98.8 4.5 %collective-permute-start = (bf16[12,1,4,640]{3,2,1,0:T(4,128)(2,1)S(1)}, bf16[12,1,4,640]{3,2,1,0:T(4,128)(2,1)S(1)}, u32[]{:S(2)}, u32[]{:S(2)}) collective-permute-start(bf16[12,1,4,640]{3,2,1,0:T(4,128)(2,1)S(1)} %get-tuple-element.21), channel_id=1, source_target_pairs={{0,128},{128,256},{256,384},{1,129},{129,257},{257,385},{2,130},{1... | collective-permute-start | bytes 184328 | tf_op jit(solution)/shard_map/ppermute | solution.py:28
  103.4 0.3 collective-permute-done.1
  103.6 1.6 collective-permute-done
  105.2 0.3 pad_maximum_fusion.1
  105.5 1.0 fusion.9
  106.6 2.0 collective-permute-start.2
  108.5 1.3 collective-permute-start.3
  109.8 1.3 pad_maximum_fusion.3
  111.1 1.0 reshape.217
  112.1 1.7 reshape.220
  113.9 1.7 reshape.223
  115.6 1.8 maximum_maximum_fusion
  117.4 1.6 fusion.7
  119.0 1.0 reshape.224
  120.0 1.7 reshape.216
  121.7 1.7 reshape.218
  123.4 1.7 reshape.219
  125.1 1.7 reshape.221
  126.8 1.7 reshape.222
  128.5 3.0 %all-gather.2.cloned.1.call-done = bf16[9,640,640]{2,1,0:T(8,128)(2,1)} async-done(((bf16[9,80,640]{2,1,0:T(8,128)(2,1)}), bf16[9,640,640]{2,1,0:T(8,128)(2,1)}) %all-gather.2.cloned.1.call-update) | async-done | bytes 7372816 | tf_op jit(solution)/shard_map/all_gather | solution.py:39
  131.5 1.6 fusion.1
  133.1 1.6 fusion.2
  134.7 1.6 convolution_add_fusion.6
  136.3 1.6 convolution_add_fusion.5
  137.9 1.6 convolution_add_fusion.4
  139.5 1.6 convolution_add_fusion.3
  141.1 1.5 convolution_add_fusion.2
  142.7 1.5 convolution_add_fusion.1
  144.2 1.5 fusion
  145.8 0.7 slice.193
  146.5 1.8 reshape.225
  148.3 1.2 multiply_reduce_fusion
  149.5 10.4 %psum.43 = f32[4]{0:T(128)S(1)} all-reduce(f32[4]{0:T(128)S(1)} %multiply_reduce_fusion), channel_id=1, replica_groups=mesh['gy'=4,'gx_0'=2,'gx_1'=2,'probe_0'=8,'probe_1'=4] {'gy'}, use_global_device_ids=true, to_apply=%region_10.0 | all-reduce | flops 4 | bytes 32 | tf_op jit(solution)/shard_map/psum | solution.py:45
  159.9 9.0 %psum.44 = f32[4]{0:T(128)S(1)} all-reduce(f32[4]{0:T(128)S(1)} %psum.43), channel_id=1, replica_groups=mesh['gy'=4,'gx_0'=2,'gx_1'=2,'probe_0'=8,'probe_1'=4] {'gx_0'}, use_global_device_ids=true, to_apply=%region_11.12 | all-reduce | flops 4 | bytes 32 | tf_op jit(solution)/shard_map/psum | solution.py:45
  168.9 2.4 %psum.45 = f32[4]{0:T(128)S(1)} all-reduce(f32[4]{0:T(128)S(1)} %psum.44), channel_id=1, replica_groups=mesh['gy'=4,'gx_0'=2,'gx_1'=2,'probe_0'=8,'probe_1'=4] {'gx_1'}, use_global_device_ids=true, to_apply=%region_12.13 | all-reduce | flops 4 | bytes 32 | tf_op jit(solution)/shard_map/psum | solution.py:45
  171.3 16.1 %psum.46 = f32[4]{0:T(128)S(1)} all-reduce(f32[4]{0:T(128)S(1)} %psum.45), channel_id=1, replica_groups=mesh['gy'=4,'gx_0'=2,'gx_1'=2,'probe_0'=8,'probe_1'=4] {'probe_0'}, use_global_device_ids=true, to_apply=%region_13.14 | all-reduce | flops 4 | bytes 32 | tf_op jit(solution)/shard_map/psum | solution.py:45
  187.4 12.0 %psum.47 = f32[4]{0:T(128)S(1)} all-reduce(f32[4]{0:T(128)S(1)} %psum.46), channel_id=1, replica_groups=mesh['gy'=4,'gx_0'=2,'gx_1'=2,'probe_0'=8,'probe_1'=4] {'probe_1'}, use_global_device_ids=true, to_apply=%region_14.15 | all-reduce | flops 4 | bytes 32 | tf_op jit(solution)/shard_map/psum | solution.py:45
  199.4 0.5 broadcast_multiply_fusion.1
  200.0 0.7 add_convert_fusion
  (54 shorter events, 1.2 us)
Async XLA Ops:
  7.2 88.9 %copy-start = (f32[1000,640]{1,0:T(8,128)S(1)}, f32[1000,640]{1,0:T(8,128)}, u32[]{:S(2)}) copy-start(f32[1000,640]{1,0:T(8,128)} %param.11) | copy-start | bytes 7680004
  7.2 124.3 %all-gather.2.cloned.1.call-start = ((), (), s32[]{:S(2)}) async-start(), calls=%async_computation | async-start | bytes 8294400 | tf_op jit(solution)/shard_map/all_gather | solution.py:39
  8.4 34.6 %copy-start.2 = (bf16[4,4,4,640]{3,2,1,0:T(4,128)(2,1)S(1)}, bf16[4,4,4,640]{3,2,1,0:T(4,128)(2,1)}, u32[]{:S(2)}) copy-start(bf16[4,4,4,640]{3,2,1,0:T(4,128)(2,1)} %param.8) | copy-start | bytes 245764
  8.4 34.6 %copy-start.1 = (s32[2,4,4,4,640]{4,3,2,1,0:T(4,128)S(1)}, s32[2,4,4,4,640]{4,3,2,1,0:T(4,128)}, u32[]{:S(2)}) copy-start(s32[2,4,4,4,640]{4,3,2,1,0:T(4,128)} %param.9) | copy-start | bytes 983044
  41.9 54.2 %copy-start.14 = (s32[4]{0:T(128)S(1)}, s32[4]{0:T(128)}, u32[]{:S(2)}) copy-start(s32[4]{0:T(128)} %param.10) | copy-start | bytes 52
  43.0 54.0 %copy-start.11 = (f32[640]{0:T(1024)S(1)}, f32[640]{0:T(1024)}, u32[]{:S(2)}) copy-start(f32[640]{0:T(1024)} %param.13) | copy-start | bytes 7684
  43.1 54.0 %copy-start.12 = (f32[640]{0:T(1024)S(1)}, f32[640]{0:T(1024)}, u32[]{:S(2)}) copy-start(f32[640]{0:T(1024)} %param.12) | copy-start | bytes 7684
  97.5 6.1 %collective-permute-start.1 = (bf16[12,1,4,640]{3,2,1,0:T(4,128)(2,1)S(1)}, bf16[12,1,4,640]{3,2,1,0:T(4,128)(2,1)S(1)}, u32[]{:S(2)}, u32[]{:S(2)}) collective-permute-start(bf16[12,1,4,640]{3,2,1,0:T(4,128)(2,1)S(1)} %get-tuple-element.22), channel_id=1, source_target_pairs={{128,0},{256,128},{384,256},{129,1},{257,129},{385,257},{130,2},{2... | collective-permute-start | bytes 184328 | tf_op jit(solution)/shard_map/ppermute | solution.py:31
  98.8 6.4 %collective-permute-start = (bf16[12,1,4,640]{3,2,1,0:T(4,128)(2,1)S(1)}, bf16[12,1,4,640]{3,2,1,0:T(4,128)(2,1)S(1)}, u32[]{:S(2)}, u32[]{:S(2)}) collective-permute-start(bf16[12,1,4,640]{3,2,1,0:T(4,128)(2,1)S(1)} %get-tuple-element.21), channel_id=1, source_target_pairs={{0,128},{128,256},{256,384},{1,129},{129,257},{257,385},{2,130},{1... | collective-permute-start | bytes 184328 | tf_op jit(solution)/shard_map/ppermute | solution.py:28
  105.2 5.9 %copy-start.10 = (bf16[12,1,4,640]{3,2,1,0:T(4,128)(2,1)}, bf16[12,1,4,640]{3,2,1,0:T(4,128)(2,1)S(1)}, u32[]{:S(2)}) copy-start(bf16[12,1,4,640]{3,2,1,0:T(4,128)(2,1)S(1)} %collective-permute-done) | copy-start | bytes 184324
  106.6 9.0 %collective-permute-start.2 = (bf16[12,6,1,640]{3,2,1,0:T(2,128)(2,1)}, bf16[12,6,1,640]{3,2,1,0:T(2,128)(2,1)}, u32[]{:S(2)}, u32[]{:S(2)}) collective-permute-start(bf16[12,6,1,640]{3,2,1,0:T(2,128)(2,1)} %get-tuple-element.16), channel_id=1, source_target_pairs={{0,32},{32,64},{64,96},{1,33},{33,65},{65,97},{2,34},{34,66},{66,9... | collective-permute-start | bytes 276488 | tf_op jit(solution)/shard_map/ppermute | solution.py:28
  108.5 7.1 %collective-permute-start.3 = (bf16[12,6,1,640]{3,2,1,0:T(2,128)(2,1)}, bf16[12,6,1,640]{3,2,1,0:T(2,128)(2,1)}, u32[]{:S(2)}, u32[]{:S(2)}) collective-permute-start(bf16[12,6,1,640]{3,2,1,0:T(2,128)(2,1)} %get-tuple-element.17), channel_id=1, source_target_pairs={{32,0},{64,32},{96,64},{33,1},{65,33},{97,65},{34,2},{66,34},{98,6... | collective-permute-start | bytes 276488 | tf_op jit(solution)/shard_map/ppermute | solution.py:31
  131.5 3.2 %copy-start.9 = (bf16[192,640]{1,0:T(8,128)(2,1)S(1)}, bf16[192,640]{1,0:T(8,128)(2,1)}, u32[]{:S(2)}) copy-start(bf16[192,640]{1,0:T(8,128)(2,1)} %reshape.216) | copy-start | bytes 737284
  131.5 4.8 %copy-start.8 = (bf16[192,640]{1,0:T(8,128)(2,1)S(1)}, bf16[192,640]{1,0:T(8,128)(2,1)}, u32[]{:S(2)}) copy-start(bf16[192,640]{1,0:T(8,128)(2,1)} %reshape.218) | copy-start | bytes 737284
  133.1 4.8 %copy-start.7 = (bf16[192,640]{1,0:T(8,128)(2,1)S(1)}, bf16[192,640]{1,0:T(8,128)(2,1)}, u32[]{:S(2)}) copy-start(bf16[192,640]{1,0:T(8,128)(2,1)} %reshape.219) | copy-start | bytes 737284
  134.7 4.8 %copy-start.4 = (bf16[192,640]{1,0:T(8,128)(2,1)S(1)}, bf16[192,640]{1,0:T(8,128)(2,1)}, u32[]{:S(2)}) copy-start(bf16[192,640]{1,0:T(8,128)(2,1)} %reshape.220) | copy-start | bytes 737284
  136.3 4.8 %copy-start.5 = (bf16[192,640]{1,0:T(8,128)(2,1)S(1)}, bf16[192,640]{1,0:T(8,128)(2,1)}, u32[]{:S(2)}) copy-start(bf16[192,640]{1,0:T(8,128)(2,1)} %reshape.221) | copy-start | bytes 737284
  137.9 4.7 %copy-start.6 = (bf16[192,640]{1,0:T(8,128)(2,1)S(1)}, bf16[192,640]{1,0:T(8,128)(2,1)}, u32[]{:S(2)}) copy-start(bf16[192,640]{1,0:T(8,128)(2,1)} %reshape.222) | copy-start | bytes 737284
  139.5 4.7 %copy-start.3 = (bf16[192,640]{1,0:T(8,128)(2,1)S(1)}, bf16[192,640]{1,0:T(8,128)(2,1)}, u32[]{:S(2)}) copy-start(bf16[192,640]{1,0:T(8,128)(2,1)} %reshape.223) | copy-start | bytes 737284
  144.2 55.7 %copy-start.13 = (f32[640]{0:T(1024)S(1)}, f32[640]{0:T(1024)}, u32[]{:S(2)}) copy-start(f32[640]{0:T(1024)} %param.15) | copy-start | bytes 7684
Sparse Core Ops, SparseCore 0:
  43.1 88.3 all-gather.1
where the time goes:
time: 208 us
  blocking collectives  133 us (64%)
  local copies, waits for them, and re-layouts  23.8 us (11%)
  matrix products  15 us (7%)
  between operations  14.5 us (7%)
  starting transfers between devices  9.13 us (4%)
  other arithmetic  7.03 us (3%)
  waiting for transfers between devices  4.85 us (2%)
    psum x5, blocking collectives, one_axis_at_a_time(): value = lax.psum(value, axis)  49.9 us
    psum x1, blocking collectives, packed_total(): total = lax.psum(flat, axis)  49.8 us
    all_gather x1, blocking collectives, gathered_by_axis(): nearer = lax.all_gather(value, axes[-1], axis=dim, tiled=True)  33.5 us
    dot_general x9, matrix products, local_conv(): jnp.dot(window, weight[tap], preferred_element_type=jnp.float32)  14.1 us
    reshape x9, local copies, waits for them, and re-layouts, local_conv(): padded[:, row_off:row_off + height, col_off:col_off + width, :]  14 us
    ppermute x2, starting transfers between devices, with_halo(): lax.ppermute(lax.slice_in_dim(block, block.shape[dim] - width, None, axis...  6.52 us
  transfers between devices with their start and end apart: 5, of which 3 were waited for; matrix products, arithmetic and copies ran while one was open for 12% of the time, Pallas kernels for 0%

commit v1 on v0

v1 whole, which is shorter than its diff:
```python
import jax
import jax.numpy as jnp
from jax import lax
from jax.experimental import pallas as pl
from jax.experimental.pallas import tpu as pltpu
from jax.sharding import Mesh
from jax.sharding import PartitionSpec as P

GROUPS = 32
GX = ("gx_0", "gx_1")
PROBE = ("probe_0", "probe_1")
LANES = 128
PAIRS = 6
F32 = jnp.float32
BF16 = jnp.bfloat16
VMEM = pl.BlockSpec(memory_space=pltpu.VMEM)
SMEM = pl.BlockSpec(memory_space=pltpu.SMEM)
HBM = pl.BlockSpec(memory_space=pltpu.HBM)


def three_parts(value):
    high = value.astype(BF16)
    rest = value - high.astype(F32)
    mid = rest.astype(BF16)
    low = (rest - mid.astype(F32)).astype(BF16)
    return high, mid, low


def lane_block(index):
    return slice(index * LANES, (index + 1) * LANES)


def doubled_rows(rows):
    turned = pltpu.roll(rows, 4, axis=0)
    upper = lax.broadcasted_iota(jnp.int32, rows.shape, 0) < 4
    return jnp.where(upper, rows, turned), jnp.where(upper, turned, rows)


def pair_of(index):
    member = lax.axis_index("gy") * 2 + lax.axis_index("gx_1")
    number = member * PAIRS + index
    return lax.rem(number, 9), lax.div(number, 9)


def pack_kernel(
    signs_hbm, state_hbm, weight_hbm, wsend_ref, main_ref, rim_ref,
    signs_ref, state_ref, weight_ref, uf, xf, wf, rim, sums, arrived,
):
    blocks = uf.shape[0]
    loads = [
        pltpu.make_async_copy(src, dst, arrived.at[index])
        for index, (src, dst) in enumerate(
            ((weight_hbm, weight_ref), (state_hbm, state_ref), (signs_hbm, signs_ref))
        )
    ]
    for load in loads:
        load.start()
    loads[0].wait()
    for index in range(PAIRS):
        tap, ob = pair_of(index)
        rows = weight_ref[tap].astype(F32)
        picked = jnp.zeros((rows.shape[0], LANES), F32)
        for o in range(blocks):
            picked = picked + jnp.where(ob == o, rows[:, lane_block(o)], 0.0)
        wf[pl.ds(index, rows.shape[0], stride=PAIRS), :] = picked
    packed = wf[...].astype(BF16)
    for target in range(wsend_ref.shape[0]):
        wsend_ref[target] = packed

    loads[1].wait()
    loads[2].wait()
    for p in range(2):
        for b in range(4):
            for r in range(4):
                line = signs_ref[p, b, r].astype(F32)
                for o in range(blocks):
                    uf[o, pl.ds(r * 32 + p * 4 + b, 4, stride=8), :] = line[:, lane_block(o)]
    for b in range(4):
        for r in range(4):
            line = state_ref[b, r].astype(F32)
            for o in range(blocks):
                xf[o, pl.ds(r * 16 + b, 4, stride=4), :] = line[:, lane_block(o)]

    edge = jnp.where(lax.axis_index("gx_0") == 0, 3, 0)
    for o in range(blocks):
        sum_u = jnp.zeros((8, LANES), F32)
        cross = jnp.zeros((8, LANES), F32)
        sum_x = jnp.zeros((8, LANES), F32)
        sum_xx = jnp.zeros((8, LANES), F32)
        for two in range(8):
            pair = doubled_rows(xf[o, two * 8 : two * 8 + 8, :])
            for half in range(2):
                cell = two * 2 + half
                x = pair[half]
                u = uf[o, cell * 8 : cell * 8 + 8, :]
                sum_u, cross = sum_u + u, cross + u * x
                sum_x, sum_xx = sum_x + x, sum_xx + x * x
        for kind, part in enumerate((sum_u, cross, sum_x, sum_xx)):
            sums[kind * 8 : kind * 8 + 8, lane_block(o)] = part
        for r in range(4):
            rim[r * 8 : r * 8 + 8, lane_block(o)] = uf[o, pl.ds(pl.multiple_of((r * 4 + edge) * 8, 8), 8), :]
            rim[32 + r * 4 : 36 + r * 4, lane_block(o)] = xf[o, pl.ds((r * 4 + edge) * 4, 4), :]

    width = sums.shape[1] // GROUPS
    row = lax.broadcasted_iota(jnp.int32, (sums.shape[1], LANES), 0)
    first = lax.broadcasted_iota(jnp.int32, (sums.shape[1], LANES), 1) * width
    member = jnp.where((row >= first) & (row < first + width), 1.0, 0.0).astype(BF16)
    grouped = jnp.zeros((32, LANES), F32)
    for part in three_parts(sums[...]):
        grouped = grouped + jnp.dot(part, member, preferred_element_type=F32)
    stats = grouped[0:8]
    for kind in range(1, 4):
        stats = stats + pltpu.roll(grouped[kind * 8 : kind * 8 + 8], GROUPS * kind, axis=1)
    rim[48:56, :] = jnp.zeros((8, rim.shape[1]), F32)
    for index, part in enumerate(three_parts(stats)):
        rim[48:56, lane_block(index)] = part.astype(F32)

    for o in range(blocks):
        main_ref[0:128, lane_block(o)] = uf[o].astype(BF16)
        main_ref[128:192, lane_block(o)] = xf[o].astype(BF16)
    rim_ref[...] = rim[...].astype(BF16)


def mix_kernel(
    own0, own1, own2, own3, other0, other1, other2, other3, weight_ref, gain_ref, offset_ref,
    out_ref, ug, xg, embed, picked, lhs_ref, slope_ref, rows_ref, wf, wc, velocity,
):
    blocks = ug.shape[0]
    core = lax.axis_index("gx_1")
    half = lax.axis_index("gx_0")
    probe = lax.axis_index("probe_0") * lax.axis_size("probe_1") + lax.axis_index("probe_1")
    chans = own0.shape[1]
    ug[...] = jnp.zeros(ug.shape, F32)
    xg[...] = jnp.zeros(xg.shape, F32)

    def spot(row, col):
        return pl.multiple_of((row * 10 + col) * 8, 8)

    total = jnp.zeros((8, chans), F32)
    rim_here = core == 1 - half
    rim_col = jnp.where(half == 0, 9, 0)
    for back, (own_ref, other_ref) in enumerate(((own0, other0), (own1, other1), (own2, other2), (own3, other3))):
        tile = lax.rem(lax.axis_index("gy") + 4 - back, 4)
        for src, base in ((own_ref, 4 * core), (other_ref, 4 * (1 - core))):
            for r in range(4):
                at = spot(4 * tile + r + 1, base + 1)
                lines = src[r * 32 : r * 32 + 32, :].astype(F32)
                states = src[128 + r * 16 : 144 + r * 16, :].astype(F32)
                for o in range(blocks):
                    ug[o, pl.ds(at, 32), :] = lines[:, lane_block(o)]
                    for two in range(2):
                        pair = doubled_rows(states[two * 8 : two * 8 + 8, lane_block(o)])
                        xg[o, pl.ds(pl.multiple_of(at + two * 16, 8), 8), :] = pair[0]
                        xg[o, pl.ds(pl.multiple_of(at + two * 16 + 8, 8), 8), :] = pair[1]
        mine = own_ref[192:256, :].astype(F32)
        theirs = other_ref[192:256, :].astype(F32)
        total = total + mine[48:56] + mine[56:64] + theirs[48:56] + theirs[56:64]
        rim = jnp.where(rim_here, mine[0:48], theirs[0:48])
        for r in range(4):
            at = spot(4 * tile + r + 1, rim_col)
            for o in range(blocks):
                ug[o, pl.ds(at, 8), :] = rim[r * 8 : r * 8 + 8, lane_block(o)]
        for two in range(2):
            for o in range(blocks):
                pair = doubled_rows(rim[32 + two * 8 : 40 + two * 8, lane_block(o)])
                for one in range(2):
                    at = spot(4 * tile + two * 2 + one + 1, rim_col)
                    xg[o, pl.ds(at, 8), :] = pair[one]

    stats = total[:, lane_block(0)] + total[:, lane_block(1)] + total[:, lane_block(2)]
    width = chans // GROUPS
    lane = lax.broadcasted_iota(jnp.int32, (LANES, chans), 1)
    first = lax.broadcasted_iota(jnp.int32, (LANES, chans), 0) * width
    spread = jnp.where((lane >= first) & (lane < first + width), 1.0, 0.0).astype(BF16)

    def expanded(kind):
        turned = stats if kind == 0 else pltpu.roll(stats, LANES - GROUPS * kind, axis=1)
        out = jnp.zeros((8, chans), F32)
        for part in three_parts(turned):
            out = out + jnp.dot(part, spread, preferred_element_type=F32)
        return out

    count = 256 * width
    sum_u, cross, sum_x, sum_xx = (expanded(kind) for kind in range(4))
    mean = sum_x / count
    sigma = jnp.sqrt(sum_xx / count - mean * mean + 1e-05)
    inverse = 1.0 / sigma
    mean_u = sum_u / count
    mean_cu = (cross - mean * sum_u) / count
    bend = mean_cu / (sigma * sigma * sigma)
    for b in range(4):
        line = offset_ref[b : b + 1, :]
        embed[b : b + 1, :] = line
        embed[b + 4 : b + 5, :] = line
    offset = embed[...]
    gain = gain_ref[...]

    def fields(x, o):
        at = lane_block(o)
        centered = x - mean[:, at]
        pre = centered * inverse[:, at] * gain[:, at] + offset[:, at]
        sig = 1.0 / (1.0 + jnp.exp(-pre))
        return centered, pre, sig

    def grid_row(gr, carry):
        at = spot(gr + 1, 1)
        for o in range(blocks):
            ln = lane_block(o)
            x = xg[o, pl.ds(at, 64), :].reshape(8, 8, LANES)
            u = ug[o, pl.ds(at, 64), :].reshape(8, 8, LANES)
            centered, pre, sig = fields(x, o)
            xg[o, pl.ds(at, 64), :] = (pre * sig).reshape(64, LANES)
            slope = sig * (1.0 + pre * (1.0 - sig)) * gain[:, ln]
            direction = (u - mean_u[:, ln]) * inverse[:, ln] - centered * bend[:, ln]
            out = (slope * direction).reshape(64, LANES).astype(BF16)
            slope_ref[pl.ds(pl.multiple_of(gr * 64, 64), 64), ln] = out
            edge = spot(gr + 1, rim_col)
            _, pre, sig = fields(xg[o, pl.ds(edge, 8), :], o)
            xg[o, pl.ds(edge, 8), :] = pre * sig
        return carry

    lax.fori_loop(0, 16, grid_row, 0)

    taps = [pair_of(index) for index in range(PAIRS)]

    def lhs_row(gr, carry):
        for index, (tap, ob) in enumerate(taps):
            dy, dx = lax.div(tap, 3), lax.rem(tap, 3)
            at = spot(gr + 2 - dy, 2 - dx)
            value = ug[jnp.minimum(ob, blocks - 1), pl.ds(at, 64), :]
            lhs_ref[pl.ds(pl.multiple_of(gr * 64, 64), 64), lane_block(index)] = value.astype(BF16)
        return carry

    lax.fori_loop(0, 16, lhs_row, 0)

    latent, spots = lax.div(probe, 8), lax.rem(probe, 8)
    row, col = lax.div(spots, 2), 2 * lax.rem(spots, 2)
    for index, (tap, ob) in enumerate(taps):
        dy, dx = lax.div(tap, 3), lax.rem(tap, 3)
        for target in range(8):
            at = ((4 * (target // 2) + row + dy) * 10 + 4 * (target % 2) + col + dx) * 8 + latent
            for o in range(blocks):
                picked[o, index * 16 + target * 2 : index * 16 + target * 2 + 2, :] = xg[o, pl.ds(at, 2, stride=8), :]
    for o in range(blocks):
        rows_ref[:, lane_block(o)] = picked[o].astype(BF16)

    each = weight_ref.shape[1]
    for source in range(weight_ref.shape[0]):
        wf[source * each : (source + 1) * each, :] = weight_ref[source].astype(F32)
    for index in range(PAIRS):
        wc[:, lane_block(index)] = wf[pl.ds(index, chans, stride=PAIRS), :].astype(BF16)

    chunk = 256
    total = jnp.zeros((8, chans), F32)
    for start in range(0, lhs_ref.shape[0], chunk):
        value = lax.dot_general(
            lhs_ref[start : start + chunk, :], wc[...], (((1,), (1,)), ((), ())), preferred_element_type=F32
        )
        value = value * slope_ref[start : start + chunk, :].astype(F32)
        total = total + jnp.sum(value.reshape(chunk // 8, 8, chans), axis=0)
    lanes = total[:, lane_block(0)]
    for o in range(1, blocks):
        lanes = lanes + total[:, lane_block(o)]
    lanes = lanes + pltpu.roll(lanes, 4, axis=0)

    velocity[...] = jnp.zeros(velocity.shape, F32)
    for index in range(PAIRS):
        ob = jnp.minimum(taps[index][1], blocks - 1)
        part = jnp.dot(rows_ref[index * 16 : index * 16 + 16, :], wc[:, lane_block(index)], preferred_element_type=F32)
        velocity[ob] = velocity[ob] + part
    for o in range(blocks):
        for j in range(2):
            out_ref[pl.ds(o * 2 + j, 8, stride=16), :] = velocity[o, pl.ds(j, 8, stride=2), :]
    for b in range(4):
        out_ref[pl.ds(10 + b, 8, stride=16), :] = jnp.broadcast_to(lanes[b : b + 1, :], (8, LANES))
    for b in range(2):
        out_ref[pl.ds(14 + b, 8, stride=16), :] = jnp.zeros((8, LANES), F32)


def step_kernel(parts_ref, state_ref, bias_ref, out_ref, lines, message):
    blocks = bias_ref.shape[1] // LANES
    probe = lax.axis_index("probe_0") * lax.axis_size("probe_1") + lax.axis_index("probe_1")
    latent, spots = lax.div(probe, 8), lax.rem(probe, 8)
    row, col = lax.div(spots, 2), 2 * lax.rem(spots, 2)
    total = parts_ref[0:16, :]
    for source in range(1, 8):
        total = total + parts_ref[source * 16 : source * 16 + 16, :]
    here = state_ref[latent, row].astype(F32)
    for o in range(blocks):
        lines[o] = here[:, lane_block(o)]
    for o in range(blocks):
        x = lines[o, pl.ds(col, 2), :]
        message[o * 2 : o * 2 + 2, :] = x + 0.25 * (total[o * 2 : o * 2 + 2, :] + bias_ref[:, lane_block(o)])
    mass = jnp.sum(total[10:14, :], axis=1, keepdims=True)
    lane = lax.broadcasted_iota(jnp.int32, (4, LANES), 1)
    coded = jnp.zeros((4, LANES), F32)
    for index, part in enumerate(three_parts(jnp.broadcast_to(mass, (4, LANES)))):
        coded = jnp.where(lane == index, part.astype(F32), coded)
    message[10:14, :] = coded
    message[14:16, :] = jnp.zeros((2, LANES), F32)
    packed = message[...].astype(BF16)
    for target in range(out_ref.shape[0]):
        out_ref[target] = packed


def final_kernel(scale, parts_ref, next_ref, mass_ref, wide, lines):
    blocks = lines.shape[0]
    total = jnp.zeros((16, LANES), F32)
    for source in range(64):
        value = parts_ref[source].astype(F32)
        wide[source * 16 : source * 16 + 16, :] = value
        total = total + value
    for b in range(4):
        mass_ref[b] = scale * jnp.sum(total[10 + b : 11 + b, :])
    start = lax.axis_index("gx_0") * 512
    for o in range(blocks):
        for j in range(2):
            lines[o, pl.ds(j, 32, stride=2), :] = wide[pl.ds(start + o * 2 + j, 32, stride=16), :]
    for o in range(blocks):
        for b in range(4):
            for r in range(4):
                at = b * 16 + r * 4
                next_ref[b, r, :, lane_block(o)] = lines[o, at : at + 4, :].astype(BF16)


def shape(dims, kind):
    return jax.ShapeDtypeStruct(dims, kind)


def body(state, probe_signs, timesteps, time_table, gn_gain, gn_shift, conv_weight, conv_bias):
    chans = state.shape[3]
    blocks = chans // LANES
    each = conv_weight.shape[1] * PAIRS
    params = pltpu.CompilerParams(vmem_limit_bytes=40 * 1024 * 1024)
    wsend, main, rim = pl.pallas_call(
        pack_kernel,
        out_shape=(shape((32, each, LANES), BF16), shape((192, chans), BF16), shape((56, chans), BF16)),
        in_specs=[HBM] * 3,
        out_specs=(VMEM,) * 3,
        scratch_shapes=[
            pltpu.VMEM(probe_signs.shape, jnp.int32),
            pltpu.VMEM(state.shape, BF16),
            pltpu.VMEM(conv_weight.shape, BF16),
            pltpu.VMEM((blocks, 128, LANES), F32),
            pltpu.VMEM((blocks, 64, LANES), F32),
            pltpu.VMEM((each, LANES), F32),
            pltpu.VMEM((56, chans), F32),
            pltpu.VMEM((32, chans), F32),
            pltpu.SemaphoreType.DMA((3,)),
        ],
        compiler_params=params,
        name="pack",
    )(probe_signs, state, conv_weight)

    across = [(a * 2 + b, (1 - a) * 2 + 1 - b) for a in range(2) for b in range(2)]
    with jax.named_scope("facing"):
        facing = lax.ppermute(rim, GX, across)
    with jax.named_scope("spread"):
        weights = lax.all_to_all(wsend, PROBE, 0, 0, tiled=True)
    block = jnp.concatenate([main, facing, rim[48:56]], axis=0)
    own = [block] + [None] * 3
    with jax.named_scope("column"):
        for back in (1, 3, 2):
            own[back] = lax.ppermute(block, "gy", [(i, (i + back) % 4) for i in range(4)])
    with jax.named_scope("partner"):
        other = [lax.ppermute(tile, "gx_1", [(0, 1), (1, 0)]) for tile in own]

    lines = [lax.dynamic_slice(time_table, (timesteps[b], jnp.int32(0)), (1, chans), allow_negative_indices=False) for b in range(4)]
    offset = jnp.concatenate(lines, axis=0) + gn_shift[None]
    partial = pl.pallas_call(
        mix_kernel,
        out_shape=shape((128, LANES), F32),
        in_specs=[VMEM] * 11,
        out_specs=VMEM,
        scratch_shapes=[
            pltpu.VMEM((blocks, 1440, LANES), F32),
            pltpu.VMEM((blocks, 1440, LANES), F32),
            pltpu.VMEM((8, chans), F32),
            pltpu.VMEM((blocks, PAIRS * 16, LANES), F32),
            pltpu.VMEM((1024, PAIRS * LANES), BF16),
            pltpu.VMEM((1024, chans), BF16),
            pltpu.VMEM((PAIRS * 16, chans), BF16),
            pltpu.VMEM((32 * each, LANES), F32),
            pltpu.VMEM((chans, PAIRS * LANES), BF16),
            pltpu.VMEM((blocks, 16, LANES), F32),
        ],
        compiler_params=params,
        name="mix",
    )(*own, *other, weights, gn_gain[None], offset)

    partial = lax.all_to_all(partial.reshape(8, 16, LANES), ("gy", "gx_1"), 0, 0, tiled=True)
    message = pl.pallas_call(
        step_kernel,
        out_shape=shape((64, 16, LANES), BF16),
        in_specs=[VMEM] * 3,
        out_specs=VMEM,
        scratch_shapes=[pltpu.VMEM((blocks, 4, LANES), F32), pltpu.VMEM((16, LANES), F32)],
        compiler_params=params,
        name="step",
    )(partial.reshape(128, LANES), state, conv_bias[None])
    parts = lax.all_to_all(message, ("gx_0",) + PROBE, 0, 0, tiled=True)
    scale = -0.25 / (probe_signs.shape[0] * lax.axis_size(PROBE))
    following, mass = pl.pallas_call(
        lambda *refs: final_kernel(scale, *refs),
        out_shape=(shape(state.shape, BF16), shape((4,), F32)),
        in_specs=[VMEM],
        out_specs=(VMEM, SMEM),
        scratch_shapes=[pltpu.VMEM((1024, LANES), F32), pltpu.VMEM((blocks, 64, LANES), F32)],
        compiler_params=params,
        name="final",
    )(parts)
    return following, mass


def solution(mesh):
    split = Mesh(
        mesh.devices.reshape(mesh.shape["gy"], 2, 2, 8, 4),
        ("gy", "gx_0", "gx_1", "probe_0", "probe_1"),
    )
    return jax.shard_map(
        body,
        mesh=split,
        in_specs=(
            P(None, "gy", GX, None),
            P(PROBE, None, "gy", GX, None),
            P(),
            P(),
            P(),
            P(),
            P(None, PROBE, None),
            P(),
        ),
        out_specs=(P(None, "gy", GX, None), P()),
        check_vma=False,
    )
```

time: 208 us -> 123 us (0.59)
  blocking collectives: 133 us -> 32 us
  starting transfers between devices: 9.13 us -> 50.9 us
  local copies, waits for them, and re-layouts: 23.8 us -> 8.47 us
  matrix products: 15 us -> 0 us
  waiting for transfers between devices: 4.85 us -> 18.9 us
  between operations: 14.5 us -> 0.87 us
  Pallas kernels: 0 us -> 11.3 us
  other arithmetic: 7.03 us -> 0.05 us
    psum x6 -> x0, blocking collectives: 99.7 us -> none  [the longest x5 49.9 us: one_axis_at_a_time(): value = lax.psum(value, axis)]
    all_gather x1 -> x0, blocking collectives: 33.5 us -> none  [gathered_by_axis(): nearer = lax.all_gather(value, axes[-1], axis=dim, tiled=True)]
    all_to_all x0 -> x1, blocking collectives: none -> 32 us  [body(): parts = lax.all_to_all(message, ('gx_0',) + PROBE, 0, 0, tiled=True)]
    ppermute x4 -> x8, starting transfers between devices: 9.09 us -> 34.1 us  [the longest x4 16.7 us: body(): other = [lax.ppermute(tile, 'gx_1', [(0, 1), (1, 0)]) for tile in own]]
    all_to_all x0 -> x2, starting transfers between devices: none -> 16.8 us  [the longest x1 13.1 us: body(): weights = lax.all_to_all(wsend, PROBE, 0, 0, tiled=True)]
    reshape x16 -> x0, local copies, waits for them, and re-layouts: 16.3 us -> none  [the longest x9 14 us: local_conv(): padded[:, row_off:row_off + height, col_off:col_off + width, :]]
    dot_general x10 -> x0, matrix products: 15 us -> none  [the longest x9 14.1 us: local_conv(): jnp.dot(window, weight[tap], preferred_element_type=jnp.float32)]
    ppermute x4 -> x8, waiting for transfers between devices: 1.85 us -> 13.3 us  [the longest x1 13.3 us: body(): facing = lax.ppermute(rim, GX, across)]
  transfers between devices with their start and end apart: 5 -> 10, of which waited for: 3 -> 2; matrix products, arithmetic and copies ran while one was open for 12% -> 3% of each run, Pallas kernels for 0% -> 0%
where the time goes in v1:
time: 123 us; the launch traced here: 122 us
  starting transfers between devices  50.9 us (41%)
  blocking collectives  32 us (26%)
  waiting for transfers between devices  18.9 us (15%)
  Pallas kernels  11.3 us (9%)
  local copies, waits for them, and re-layouts  8.47 us (7%)
    all_to_all x1, blocking collectives, body(): parts = lax.all_to_all(message, ('gx_0',) + PROBE, 0, 0, tiled=True)  32 us
    ppermute x4, starting transfers between devices, body(): other = [lax.ppermute(tile, 'gx_1', [(0, 1), (1, 0)]) for tile in own]  16.7 us
    ppermute x1, waiting for transfers between devices, body(): facing = lax.ppermute(rim, GX, across)  13.3 us
    all_to_all x1, starting transfers between devices, body(): weights = lax.all_to_all(wsend, PROBE, 0, 0, tiled=True)  13.1 us
    ppermute x3, starting transfers between devices, body(): lax.ppermute(block, 'gy', [(i, (i + back) % 4) for i in range(4)])  10.2 us
    pallas_call x1, Pallas kernels, body(): pl.pallas_call(mix_kernel, out_shape=shape((128, LANES), F32), in_specs=[...  8.74 us
    ppermute x1, starting transfers between devices, body(): facing = lax.ppermute(rim, GX, across)  7.23 us
    all_to_all x1, waiting for transfers between devices, body(): lax.all_to_all(partial.reshape(8, 16, LANES), ('gy', 'gx_1'), 0, 0, tiled...  5.61 us
  transfers between devices with their start and end apart: 10, of which 2 were waited for; matrix products, arithmetic and copies ran while one was open for 3% of the time, Pallas kernels for 0%

profile of v1, /device:TPU:8, one launch (start us, length us, event | category | flops | bytes accessed | tf_op | source)
XLA Modules:
  0.0 122.4 jit_solution(8453531173941762828)
XLA Ops:
  0.6 0.0 copy-start.2
  0.6 1.0 copy-done.2
  1.6 0.0 copy-start.3
  1.6 0.9 copy-done.3
  2.5 0.0 copy-start.5
  2.5 1.0 copy-done.5
  3.4 0.0 copy-start.7
  3.5 0.0 copy-start.6
  3.5 0.0 copy-start.9
  3.5 1.6 %pack.1 = (bf16[32,120,128]{2,1,0:T(8,128)(2,1)}, bf16[192,640]{1,0:T(8,128)(2,1)S(1)}, bf16[56,640]{1,0:T(8,128)(2,1)S(1)}) custom-call(s32[2,4,4,4,640]{4,3,2,1,0:T(4,128)S(1)} %copy-done.2, bf16[4,4,4,640]{3,2,1,0:T(4,128)(2,1)S(1)} %copy-done.3, bf16[9,20,640]{2,1,0:T(8,128)(2,1)S(1)} %copy-done.5), custom_call_target="tpu_custom_call" | custom-call | tf_op jit(solution)/shard_map/pack/pallas_call | solution.py:335
  5.1 13.1 %all-to-all-start = ((bf16[32,120,128]{2,1,0:T(8,128)(2,1)}), bf16[32,120,128]{2,1,0:T(8,128)(2,1)S(1)}, u32[]{:S(2)}, u32[]{:S(2)}) async-start(bf16[32,120,128]{2,1,0:T(8,128)(2,1)} %get-tuple-element.7), calls=%async_computation | async-start | bytes 1966080 | tf_op jit(solution)/shard_map/spread/all_to_all | solution.py:359
  18.2 0.0 copy-start.8
  18.3 0.0 copy-start.4
  18.3 7.2 %collective-permute-start = (bf16[56,640]{1,0:T(8,128)(2,1)S(1)}, bf16[56,640]{1,0:T(8,128)(2,1)S(1)}, u32[]{:S(2)}, u32[]{:S(2)}) collective-permute-start(bf16[56,640]{1,0:T(8,128)(2,1)S(1)} %get-tuple-element.6), channel_id=1, source_target_pairs={{0,96},{32,64},{64,32},{96,0},{1,97},{33,65},{65,33},{97,1},{2,98}... | collective-permute-start | bytes 215048 | tf_op jit(solution)/shard_map/facing/ppermute | solution.py:357
  25.5 13.3 %collective-permute-done = bf16[56,640]{1,0:T(8,128)(2,1)S(1)} collective-permute-done((bf16[56,640]{1,0:T(8,128)(2,1)S(1)}, bf16[56,640]{1,0:T(8,128)(2,1)S(1)}, u32[]{:S(2)}, u32[]{:S(2)}) %collective-permute-start) | collective-permute-done | bytes 71712 | tf_op jit(solution)/shard_map/facing/ppermute | solution.py:357
  38.8 4.7 %collective-permute-start.3 = (bf16[256,640]{1,0:T(8,128)(2,1)S(1)}, bf16[256,640]{1,0:T(8,128)(2,1)S(1)}, u32[]{:S(2)}, u32[]{:S(2)}) collective-permute-start(bf16[256,640]{1,0:T(8,128)(2,1)S(1)} %pad_maximum_fusion.own0), channel_id=1, source_target_pairs={{0,384},{128,0},{256,128},{384,256},{1,385},{129,1},{257,129},{385... | collective-permute-start | bytes 983048 | tf_op jit(solution)/shard_map/column/ppermute | solution.py:364
  43.5 2.7 %collective-permute-start.2 = (bf16[256,640]{1,0:T(8,128)(2,1)S(1)}, bf16[256,640]{1,0:T(8,128)(2,1)S(1)}, u32[]{:S(2)}, u32[]{:S(2)}) collective-permute-start(bf16[256,640]{1,0:T(8,128)(2,1)S(1)} %pad_maximum_fusion.own0), channel_id=1, source_target_pairs={{0,256},{128,384},{256,0},{384,128},{1,257},{129,385},{257,1},{385... | collective-permute-start | bytes 983048 | tf_op jit(solution)/shard_map/column/ppermute | solution.py:364
  46.2 2.8 %collective-permute-start.1 = (bf16[256,640]{1,0:T(8,128)(2,1)S(1)}, bf16[256,640]{1,0:T(8,128)(2,1)S(1)}, u32[]{:S(2)}, u32[]{:S(2)}) collective-permute-start(bf16[256,640]{1,0:T(8,128)(2,1)S(1)} %pad_maximum_fusion.own0), channel_id=1, source_target_pairs={{0,128},{128,256},{256,384},{384,0},{1,129},{129,257},{257,385},{3... | collective-permute-start | bytes 983048 | tf_op jit(solution)/shard_map/column/ppermute | solution.py:364
  49.0 0.0 copy-done.7
  49.0 0.0 copy-done.6
  49.0 0.7 fusion
  49.7 9.5 %collective-permute-start.4 = (bf16[256,640]{1,0:T(8,128)(2,1)S(1)}, bf16[256,640]{1,0:T(8,128)(2,1)S(1)}, u32[]{:S(2)}, u32[]{:S(2)}) collective-permute-start(bf16[256,640]{1,0:T(8,128)(2,1)S(1)} %pad_maximum_fusion.own0), channel_id=1, source_target_pairs={{0,32},{32,0},{1,33},{33,1},{2,34},{34,2},{3,35},{35,3},{4,36},{36... | collective-permute-start | bytes 983048 | tf_op jit(solution)/shard_map/partner/ppermute | solution.py:366
  59.2 0.0 collective-permute-done.3.own3
  59.2 1.9 %collective-permute-start.7 = (bf16[256,640]{1,0:T(8,128)(2,1)S(1)}, bf16[256,640]{1,0:T(8,128)(2,1)S(1)}, u32[]{:S(2)}, u32[]{:S(2)}) collective-permute-start(bf16[256,640]{1,0:T(8,128)(2,1)S(1)} %collective-permute-done.3.own3), channel_id=1, source_target_pairs={{0,32},{32,0},{1,33},{33,1},{2,34},{34,2},{3,35},{35,3},{4,36},{36... | collective-permute-start | bytes 983048 | tf_op jit(solution)/shard_map/partner/ppermute | solution.py:366
  61.2 0.0 collective-permute-done.2.own2
  61.2 2.4 %collective-permute-start.6 = (bf16[256,640]{1,0:T(8,128)(2,1)S(1)}, bf16[256,640]{1,0:T(8,128)(2,1)S(1)}, u32[]{:S(2)}, u32[]{:S(2)}) collective-permute-start(bf16[256,640]{1,0:T(8,128)(2,1)S(1)} %collective-permute-done.2.own2), channel_id=1, source_target_pairs={{0,32},{32,0},{1,33},{33,1},{2,34},{34,2},{3,35},{35,3},{4,36},{36... | collective-permute-start | bytes 983048 | tf_op jit(solution)/shard_map/partner/ppermute | solution.py:366
  63.6 0.0 collective-permute-done.1.own1
  63.6 2.8 %collective-permute-start.5 = (bf16[256,640]{1,0:T(8,128)(2,1)S(1)}, bf16[256,640]{1,0:T(8,128)(2,1)S(1)}, u32[]{:S(2)}, u32[]{:S(2)}) collective-permute-start(bf16[256,640]{1,0:T(8,128)(2,1)S(1)} %collective-permute-done.1.own1), channel_id=1, source_target_pairs={{0,32},{32,0},{1,33},{33,1},{2,34},{34,2},{3,35},{35,3},{4,36},{36... | collective-permute-start | bytes 983048 | tf_op jit(solution)/shard_map/partner/ppermute | solution.py:366
  66.4 3.3 %constant_dynamic-slice_fusion.3 = (f32[1,640]{1,0:T(1,128)S(1)}, f32[1,640]{1,0:T(1,128)S(1)}, f32[1,640]{1,0:T(1,128)S(1)}, f32[1,640]{1,0:T(1,128)S(1)}) fusion(f32[1000,640]{1,0:T(8,128)} %param.11, s32[]{:T(128)} %bitcast, s32[]{:T(128)} %bitcast.1, s32[]{:T(128)} %bitcast.3, s32[]{:T(128)} %bitcast.2), kind=kLoop, calls=%fused_computation.5 | loop fusion | bytes 20496 | tf_op jit(solution)/shard_map/dynamic_slice | solution.py:368
  69.7 0.0 copy-done.9
  69.7 0.0 collective-permute-done.4.other0
  69.7 0.0 collective-permute-done.7.other3
  69.7 0.0 collective-permute-done.6.other2
  69.8 0.0 collective-permute-done.5.other1
  69.8 0.0 copy-start
  69.8 0.7 copy-done
  70.5 0.0 all-to-all-done.weight_ref
  70.5 0.0 copy-start.1
  70.5 1.0 copy-done.1
  71.5 8.7 %mix.1 = f32[128,128]{1,0:T(8,128)} custom-call(bf16[256,640]{1,0:T(8,128)(2,1)S(1)} %pad_maximum_fusion.own0, bf16[256,640]{1,0:T(8,128)(2,1)S(1)} %collective-permute-done.1.own1, bf16[256,640]{1,0:T(8,128)(2,1)S(1)} %collective-permute-done.2.own2, bf16[256,640]{1,0:T(8,128)(2,1)S(1)} %collective-permute-done.3.own3, ...), custom_call_target="tpu_custom_call" | custom-call | tf_op jit(solution)/shard_map/mix/pallas_call | solution.py:370
  80.2 3.7 %all-to-all-start.1 = ((f32[8,16,128]{2,1,0:T(8,128)}), f32[8,16,128]{2,1,0:T(8,128)S(1)}, u32[]{:S(2)}, u32[]{:S(2)}) async-start(f32[8,16,128]{2,1,0:T(8,128)} %bitcast.4), calls=%async_computation.1 | async-start | bytes 131072 | tf_op jit(solution)/shard_map/all_to_all | solution.py:391
  83.9 0.0 copy-done.8
  83.9 5.6 %all-to-all-done.1 = f32[8,16,128]{2,1,0:T(8,128)S(1)} async-done(((f32[8,16,128]{2,1,0:T(8,128)}), f32[8,16,128]{2,1,0:T(8,128)S(1)}, u32[]{:S(2)}, u32[]{:S(2)}) %all-to-all-start.1) | async-done | bytes 65568 | tf_op jit(solution)/shard_map/all_to_all | solution.py:391
  89.6 0.0 copy-done.4
  89.6 0.1 step.1
  89.7 32.0 %all_to_all.15.refs_0_ = bf16[64,16,128]{2,1,0:T(8,128)(2,1)S(1)} all-to-all(bf16[64,16,128]{2,1,0:T(8,128)(2,1)S(1)} %step.1), channel_id=1, replica_groups=mesh['gy'=4,'gx_0'=2,'gx_1'=2,'probe_0'=8,'probe_1'=4] {'gx_0','probe_0'..., dimensions={0} | all-to-all | bytes 524288 | tf_op jit(solution)/shard_map/all_to_all | solution.py:401
  121.7 0.8 final.1
  (5 shorter events, 0.1 us)
Async XLA Ops:
  0.6 1.0 copy-start.2
  1.6 0.9 copy-start.3
  2.5 1.0 copy-start.5
  3.4 45.6 %copy-start.7 = (f32[640]{0:T(1024)S(1)}, f32[640]{0:T(1024)}, u32[]{:S(2)}) copy-start(f32[640]{0:T(1024)} %param.12) | copy-start | bytes 7684
  3.5 45.6 %copy-start.6 = (s32[4]{0:T(128)S(1)}, s32[4]{0:T(128)}, u32[]{:S(2)}) copy-start(s32[4]{0:T(128)} %param.10) | copy-start | bytes 52
  3.5 66.2 %copy-start.9 = (f32[640]{0:T(1024)S(1)}, f32[640]{0:T(1024)}, u32[]{:S(2)}) copy-start(f32[640]{0:T(1024)} %param.13) | copy-start | bytes 7684
  5.1 65.4 %all-to-all-start = ((bf16[32,120,128]{2,1,0:T(8,128)(2,1)}), bf16[32,120,128]{2,1,0:T(8,128)(2,1)S(1)}, u32[]{:S(2)}, u32[]{:S(2)}) async-start(bf16[32,120,128]{2,1,0:T(8,128)(2,1)} %get-tuple-element.7), calls=%async_computation | async-start | bytes 1966080 | tf_op jit(solution)/shard_map/spread/all_to_all | solution.py:359
  18.2 65.7 %copy-start.8 = (f32[640]{0:T(1024)S(1)}, f32[640]{0:T(1024)}, u32[]{:S(2)}) copy-start(f32[640]{0:T(1024)} %param.15) | copy-start | bytes 7684
  18.3 71.3 %copy-start.4 = (bf16[4,4,4,640]{3,2,1,0:T(4,128)(2,1)S(1)}, bf16[4,4,4,640]{3,2,1,0:T(4,128)(2,1)}, u32[]{:S(2)}) copy-start(bf16[4,4,4,640]{3,2,1,0:T(4,128)(2,1)} %state_ref.1) | copy-start | bytes 245764
  18.3 20.5 %collective-permute-start = (bf16[56,640]{1,0:T(8,128)(2,1)S(1)}, bf16[56,640]{1,0:T(8,128)(2,1)S(1)}, u32[]{:S(2)}, u32[]{:S(2)}) collective-permute-start(bf16[56,640]{1,0:T(8,128)(2,1)S(1)} %get-tuple-element.6), channel_id=1, source_target_pairs={{0,96},{32,64},{64,32},{96,0},{1,97},{33,65},{65,33},{97,1},{2,98}... | collective-permute-start | bytes 215048 | tf_op jit(solution)/shard_map/facing/ppermute | solution.py:357
  38.8 20.4 %collective-permute-start.3 = (bf16[256,640]{1,0:T(8,128)(2,1)S(1)}, bf16[256,640]{1,0:T(8,128)(2,1)S(1)}, u32[]{:S(2)}, u32[]{:S(2)}) collective-permute-start(bf16[256,640]{1,0:T(8,128)(2,1)S(1)} %pad_maximum_fusion.own0), channel_id=1, source_target_pairs={{0,384},{128,0},{256,128},{384,256},{1,385},{129,1},{257,129},{385... | collective-permute-start | bytes 983048 | tf_op jit(solution)/shard_map/column/ppermute | solution.py:364
  43.5 17.7 %collective-permute-start.2 = (bf16[256,640]{1,0:T(8,128)(2,1)S(1)}, bf16[256,640]{1,0:T(8,128)(2,1)S(1)}, u32[]{:S(2)}, u32[]{:S(2)}) collective-permute-start(bf16[256,640]{1,0:T(8,128)(2,1)S(1)} %pad_maximum_fusion.own0), channel_id=1, source_target_pairs={{0,256},{128,384},{256,0},{384,128},{1,257},{129,385},{257,1},{385... | collective-permute-start | bytes 983048 | tf_op jit(solution)/shard_map/column/ppermute | solution.py:364
  46.2 17.4 %collective-permute-start.1 = (bf16[256,640]{1,0:T(8,128)(2,1)S(1)}, bf16[256,640]{1,0:T(8,128)(2,1)S(1)}, u32[]{:S(2)}, u32[]{:S(2)}) collective-permute-start(bf16[256,640]{1,0:T(8,128)(2,1)S(1)} %pad_maximum_fusion.own0), channel_id=1, source_target_pairs={{0,128},{128,256},{256,384},{384,0},{1,129},{129,257},{257,385},{3... | collective-permute-start | bytes 983048 | tf_op jit(solution)/shard_map/column/ppermute | solution.py:364
  49.7 20.0 %collective-permute-start.4 = (bf16[256,640]{1,0:T(8,128)(2,1)S(1)}, bf16[256,640]{1,0:T(8,128)(2,1)S(1)}, u32[]{:S(2)}, u32[]{:S(2)}) collective-permute-start(bf16[256,640]{1,0:T(8,128)(2,1)S(1)} %pad_maximum_fusion.own0), channel_id=1, source_target_pairs={{0,32},{32,0},{1,33},{33,1},{2,34},{34,2},{3,35},{35,3},{4,36},{36... | collective-permute-start | bytes 983048 | tf_op jit(solution)/shard_map/partner/ppermute | solution.py:366
  59.2 10.5 %collective-permute-start.7 = (bf16[256,640]{1,0:T(8,128)(2,1)S(1)}, bf16[256,640]{1,0:T(8,128)(2,1)S(1)}, u32[]{:S(2)}, u32[]{:S(2)}) collective-permute-start(bf16[256,640]{1,0:T(8,128)(2,1)S(1)} %collective-permute-done.3.own3), channel_id=1, source_target_pairs={{0,32},{32,0},{1,33},{33,1},{2,34},{34,2},{3,35},{35,3},{4,36},{36... | collective-permute-start | bytes 983048 | tf_op jit(solution)/shard_map/partner/ppermute | solution.py:366
  61.2 8.6 %collective-permute-start.6 = (bf16[256,640]{1,0:T(8,128)(2,1)S(1)}, bf16[256,640]{1,0:T(8,128)(2,1)S(1)}, u32[]{:S(2)}, u32[]{:S(2)}) collective-permute-start(bf16[256,640]{1,0:T(8,128)(2,1)S(1)} %collective-permute-done.2.own2), channel_id=1, source_target_pairs={{0,32},{32,0},{1,33},{33,1},{2,34},{34,2},{3,35},{35,3},{4,36},{36... | collective-permute-start | bytes 983048 | tf_op jit(solution)/shard_map/partner/ppermute | solution.py:366
  63.6 6.2 %collective-permute-start.5 = (bf16[256,640]{1,0:T(8,128)(2,1)S(1)}, bf16[256,640]{1,0:T(8,128)(2,1)S(1)}, u32[]{:S(2)}, u32[]{:S(2)}) collective-permute-start(bf16[256,640]{1,0:T(8,128)(2,1)S(1)} %collective-permute-done.1.own1), channel_id=1, source_target_pairs={{0,32},{32,0},{1,33},{33,1},{2,34},{34,2},{3,35},{35,3},{4,36},{36... | collective-permute-start | bytes 983048 | tf_op jit(solution)/shard_map/partner/ppermute | solution.py:366
  69.8 0.7 copy-start
  70.5 1.0 copy-start.1
  80.2 9.3 %all-to-all-start.1 = ((f32[8,16,128]{2,1,0:T(8,128)}), f32[8,16,128]{2,1,0:T(8,128)S(1)}, u32[]{:S(2)}, u32[]{:S(2)}) async-start(f32[8,16,128]{2,1,0:T(8,128)} %bitcast.4), calls=%async_computation.1 | async-start | bytes 131072 | tf_op jit(solution)/shard_map/all_to_all | solution.py:391

commit v2 on v1

--- a/solution.py
+++ b/solution.py
@@ -5,6 +5,7 @@
 from jax.experimental.pallas import tpu as pltpu
 from jax.sharding import Mesh
 from jax.sharding import PartitionSpec as P
+
 
 GROUPS = 32
 GX = ("gx_0", "gx_1")
@@ -36,6 +37,10 @@
     return jnp.where(upper, rows, turned), jnp.where(upper, turned, rows)
 
 
+def quarter():
+    return 2 * lax.rem(lax.axis_index("probe_0"), 2) + lax.rem(lax.axis_index("probe_1"), 2)
+
+
 def pair_of(index):
     member = lax.axis_index("gy") * 2 + lax.axis_index("gx_1")
     number = member * PAIRS + index
@@ -43,8 +48,8 @@
 
 
 def pack_kernel(
-    signs_hbm, state_hbm, weight_hbm, wsend_ref, main_ref, rim_ref,
-    signs_ref, state_ref, weight_ref, uf, xf, wf, rim, sums, arrived,
+    step_ref, signs_hbm, state_hbm, weight_hbm, table_hbm, shift_ref, wsend_ref, main_ref, rim_ref, offset_ref,
+    signs_ref, state_ref, weight_ref, table, uf, xf, wf, rim, sums, arrived, found,
 ):
     blocks = uf.shape[0]
     loads = [
@@ -55,6 +60,15 @@
     ]
     for load in loads:
         load.start()
+    steps = [step_ref[b] for b in range(4)]
+    finds = [
+        pltpu.make_async_copy(
+            table_hbm.at[pl.ds(pl.multiple_of(lax.div(steps[b], 8) * 8, 8), 8), :], table.at[b], found.at[b]
+        )
+        for b in range(4)
+    ]
+    for find in finds:
+        find.start()
     loads[0].wait()
     for index in range(PAIRS):
         tap, ob = pair_of(index)
@@ -119,16 +133,20 @@
         main_ref[0:128, lane_block(o)] = uf[o].astype(BF16)
         main_ref[128:192, lane_block(o)] = xf[o].astype(BF16)
     rim_ref[...] = rim[...].astype(BF16)
+    for b in range(4):
+        finds[b].wait()
+        line = table[b, pl.ds(lax.rem(steps[b], 8), 1), :] + shift_ref[...]
+        offset_ref[b : b + 1, :] = line
+        offset_ref[b + 4 : b + 5, :] = line
 
 
 def mix_kernel(
-    own0, own1, own2, own3, other0, other1, other2, other3, weight_ref, gain_ref, offset_ref,
-    out_ref, ug, xg, embed, picked, lhs_ref, slope_ref, rows_ref, wf, wc, velocity,
+    own0, own1, own3, own2a, own2b, other0, other1, other3, other2a, other2b, weight_ref, gain_ref, offset_ref,
+    out_ref, ug, xg, picked, lhs_ref, slope_ref, rows_ref, wf, wc, velocity,
 ):
     blocks = ug.shape[0]
     core = lax.axis_index("gx_1")
     half = lax.axis_index("gx_0")
-    probe = lax.axis_index("probe_0") * lax.axis_size("probe_1") + lax.axis_index("probe_1")
     chans = own0.shape[1]
     ug[...] = jnp.zeros(ug.shape, F32)
     xg[...] = jnp.zeros(xg.shape, F32)
@@ -139,21 +157,28 @@
     total = jnp.zeros((8, chans), F32)
     rim_here = core == 1 - half
     rim_col = jnp.where(half == 0, 9, 0)
-    for back, (own_ref, other_ref) in enumerate(((own0, other0), (own1, other1), (own2, other2), (own3, other3))):
+    whole = lambda ref: (ref.at[0:128], ref.at[128:256])
+    sources = (
+        (0, whole(own0), whole(other0)),
+        (1, whole(own1), whole(other1)),
+        (3, whole(own3), whole(other3)),
+        (2, (own2a, own2b), (other2a, other2b)),
+    )
+    for back, own_ref, other_ref in sources:
         tile = lax.rem(lax.axis_index("gy") + 4 - back, 4)
-        for src, base in ((own_ref, 4 * core), (other_ref, 4 * (1 - core))):
+        for (upper, lower), base in ((own_ref, 4 * core), (other_ref, 4 * (1 - core))):
             for r in range(4):
                 at = spot(4 * tile + r + 1, base + 1)
-                lines = src[r * 32 : r * 32 + 32, :].astype(F32)
-                states = src[128 + r * 16 : 144 + r * 16, :].astype(F32)
+                lines = upper[r * 32 : r * 32 + 32, :].astype(F32)
+                states = lower[r * 16 : r * 16 + 16, :].astype(F32)
                 for o in range(blocks):
                     ug[o, pl.ds(at, 32), :] = lines[:, lane_block(o)]
                     for two in range(2):
                         pair = doubled_rows(states[two * 8 : two * 8 + 8, lane_block(o)])
                         xg[o, pl.ds(pl.multiple_of(at + two * 16, 8), 8), :] = pair[0]
                         xg[o, pl.ds(pl.multiple_of(at + two * 16 + 8, 8), 8), :] = pair[1]
-        mine = own_ref[192:256, :].astype(F32)
-        theirs = other_ref[192:256, :].astype(F32)
+        mine = own_ref[1][64:128, :].astype(F32)
+        theirs = other_ref[1][64:128, :].astype(F32)
         total = total + mine[48:56] + mine[56:64] + theirs[48:56] + theirs[56:64]
         rim = jnp.where(rim_here, mine[0:48], theirs[0:48])
         for r in range(4):
@@ -188,11 +213,7 @@
     mean_u = sum_u / count
     mean_cu = (cross - mean * sum_u) / count
     bend = mean_cu / (sigma * sigma * sigma)
-    for b in range(4):
-        line = offset_ref[b : b + 1, :]
-        embed[b : b + 1, :] = line
-        embed[b + 4 : b + 5, :] = line
-    offset = embed[...]
+    offset = offset_ref[...]
     gain = gain_ref[...]
 
     def fields(x, o):
@@ -233,14 +254,19 @@
 
     lax.fori_loop(0, 16, lhs_row, 0)
 
-    latent, spots = lax.div(probe, 8), lax.rem(probe, 8)
-    row, col = lax.div(spots, 2), 2 * lax.rem(spots, 2)
+    row = quarter()
+    early = lax.broadcasted_iota(jnp.int32, (8, LANES), 0) < 4
     for index, (tap, ob) in enumerate(taps):
         dy, dx = lax.div(tap, 3), lax.rem(tap, 3)
         for target in range(8):
-            at = ((4 * (target // 2) + row + dy) * 10 + 4 * (target % 2) + col + dx) * 8 + latent
+            at = spot(4 * (target // 2) + row + dy, 4 * (target % 2) + dx)
+            to = index * 128 + target * 16
             for o in range(blocks):
-                picked[o, index * 16 + target * 2 : index * 16 + target * 2 + 2, :] = xg[o, pl.ds(at, 2, stride=8), :]
+                for two in range(2):
+                    first = xg[o, pl.ds(pl.multiple_of(at + two * 16, 8), 8), :]
+                    second = xg[o, pl.ds(pl.multiple_of(at + two * 16 + 8, 8), 8), :]
+                    both = jnp.where(early, first, pltpu.roll(second, 4, axis=0))
+                    picked[o, to + two * 8 : to + two * 8 + 8, :] = both
     for o in range(blocks):
         rows_ref[:, lane_block(o)] = picked[o].astype(BF16)
 
@@ -266,61 +292,50 @@
     velocity[...] = jnp.zeros(velocity.shape, F32)
     for index in range(PAIRS):
         ob = jnp.minimum(taps[index][1], blocks - 1)
-        part = jnp.dot(rows_ref[index * 16 : index * 16 + 16, :], wc[:, lane_block(index)], preferred_element_type=F32)
+        part = jnp.dot(
+            rows_ref[index * 128 : index * 128 + 128, :], wc[:, lane_block(index)], preferred_element_type=F32
+        )
         velocity[ob] = velocity[ob] + part
+    for target in range(8):
+        for o in range(blocks):
+            out_ref[target, o * 16 : o * 16 + 16, :] = velocity[o, target * 16 : target * 16 + 16, :]
+        out_ref[target, blocks * 16 : blocks * 16 + 8, :] = lanes
+
+
+def step_kernel(parts_ref, state_ref, bias_ref, rows_ref, mass_ref, lines):
+    blocks = bias_ref.shape[1] // LANES
+    total = parts_ref[0]
+    for source in range(1, 8):
+        total = total + parts_ref[source]
+    mass = jnp.sum(total[blocks * 16 : blocks * 16 + 8, :], axis=1, keepdims=True)
+    lane = lax.broadcasted_iota(jnp.int32, (8, LANES), 1)
+    latents = lax.broadcasted_iota(jnp.int32, (8, LANES), 0)
+    line = jnp.sum(jnp.where(lane == latents, mass, 0.0), axis=0, keepdims=True)
+    mass_ref[...] = jnp.broadcast_to(line, mass_ref.shape)
+    row = quarter()
+    for b in range(4):
+        here = state_ref[b, row].astype(F32)
+        for o in range(blocks):
+            lines[o, pl.ds(b, 4, stride=4), :] = here[:, lane_block(o)]
     for o in range(blocks):
-        for j in range(2):
-            out_ref[pl.ds(o * 2 + j, 8, stride=16), :] = velocity[o, pl.ds(j, 8, stride=2), :]
+        value = lines[o] + 0.25 * (total[o * 16 : o * 16 + 16, :] + bias_ref[:, lane_block(o)])
+        rows_ref[:, lane_block(o)] = value.astype(BF16)
+
+
+def final_kernel(scale, mass_ref, rows0, rows1, rows2, rows3, next_ref, out_ref, lines):
+    blocks = lines.shape[0]
+    total = jnp.sum(mass_ref[...], axis=0, keepdims=True)
+    lane = lax.broadcasted_iota(jnp.int32, (1, LANES), 1)
     for b in range(4):
-        out_ref[pl.ds(10 + b, 8, stride=16), :] = jnp.broadcast_to(lanes[b : b + 1, :], (8, LANES))
-    for b in range(2):
-        out_ref[pl.ds(14 + b, 8, stride=16), :] = jnp.zeros((8, LANES), F32)
-
-
-def step_kernel(parts_ref, state_ref, bias_ref, out_ref, lines, message):
-    blocks = bias_ref.shape[1] // LANES
-    probe = lax.axis_index("probe_0") * lax.axis_size("probe_1") + lax.axis_index("probe_1")
-    latent, spots = lax.div(probe, 8), lax.rem(probe, 8)
-    row, col = lax.div(spots, 2), 2 * lax.rem(spots, 2)
-    total = parts_ref[0:16, :]
-    for source in range(1, 8):
-        total = total + parts_ref[source * 16 : source * 16 + 16, :]
-    here = state_ref[latent, row].astype(F32)
-    for o in range(blocks):
-        lines[o] = here[:, lane_block(o)]
-    for o in range(blocks):
-        x = lines[o, pl.ds(col, 2), :]
-        message[o * 2 : o * 2 + 2, :] = x + 0.25 * (total[o * 2 : o * 2 + 2, :] + bias_ref[:, lane_block(o)])
-    mass = jnp.sum(total[10:14, :], axis=1, keepdims=True)
-    lane = lax.broadcasted_iota(jnp.int32, (4, LANES), 1)
-    coded = jnp.zeros((4, LANES), F32)
-    for index, part in enumerate(three_parts(jnp.broadcast_to(mass, (4, LANES)))):
-        coded = jnp.where(lane == index, part.astype(F32), coded)
-    message[10:14, :] = coded
-    message[14:16, :] = jnp.zeros((2, LANES), F32)
-    packed = message[...].astype(BF16)
-    for target in range(out_ref.shape[0]):
-        out_ref[target] = packed
-
-
-def final_kernel(scale, parts_ref, next_ref, mass_ref, wide, lines):
-    blocks = lines.shape[0]
-    total = jnp.zeros((16, LANES), F32)
-    for source in range(64):
-        value = parts_ref[source].astype(F32)
-        wide[source * 16 : source * 16 + 16, :] = value
-        total = total + value
-    for b in range(4):
-        mass_ref[b] = scale * jnp.sum(total[10 + b : 11 + b, :])
-    start = lax.axis_index("gx_0") * 512
-    for o in range(blocks):
-        for j in range(2):
-            lines[o, pl.ds(j, 32, stride=2), :] = wide[pl.ds(start + o * 2 + j, 32, stride=16), :]
-    for o in range(blocks):
-        for b in range(4):
-            for r in range(4):
-                at = b * 16 + r * 4
-                next_ref[b, r, :, lane_block(o)] = lines[o, at : at + 4, :].astype(BF16)
+        out_ref[b] = scale * jnp.sum(jnp.where(lane == b, total, 0.0))
+    for code, rows in enumerate((rows0, rows1, rows2, rows3)):
+        tall, wide = lax.axis_index("probe_0") + code // 2, lax.axis_index("probe_1") + code % 2
+        row = 2 * lax.rem(tall, 2) + lax.rem(wide, 2)
+        for o in range(blocks):
+            lines[o] = rows[:, lane_block(o)].astype(F32)
+        for o in range(blocks):
+            for b in range(4):
+                next_ref[b, row, :, lane_block(o)] = lines[o, pl.ds(b, 4, stride=4), :].astype(BF16)
 
 
 def shape(dims, kind):
@@ -332,84 +347,93 @@
     blocks = chans // LANES
     each = conv_weight.shape[1] * PAIRS
     params = pltpu.CompilerParams(vmem_limit_bytes=40 * 1024 * 1024)
-    wsend, main, rim = pl.pallas_call(
+    far = lambda array: pltpu.with_memory_space_constraint(array, pltpu.HBM)
+    wsend, main, rim, offset = pl.pallas_call(
         pack_kernel,
-        out_shape=(shape((32, each, LANES), BF16), shape((192, chans), BF16), shape((56, chans), BF16)),
-        in_specs=[HBM] * 3,
-        out_specs=(VMEM,) * 3,
+        out_shape=(
+            shape((32, each, LANES), BF16),
+            shape((192, chans), BF16),
+            shape((56, chans), BF16),
+            shape((8, chans), F32),
+        ),
+        in_specs=[SMEM] + [HBM] * 4 + [VMEM],
+        out_specs=(VMEM,) * 4,
         scratch_shapes=[
             pltpu.VMEM(probe_signs.shape, jnp.int32),
             pltpu.VMEM(state.shape, BF16),
             pltpu.VMEM(conv_weight.shape, BF16),
+            pltpu.VMEM((4, 8, chans), F32),
             pltpu.VMEM((blocks, 128, LANES), F32),
             pltpu.VMEM((blocks, 64, LANES), F32),
             pltpu.VMEM((each, LANES), F32),
             pltpu.VMEM((56, chans), F32),
             pltpu.VMEM((32, chans), F32),
             pltpu.SemaphoreType.DMA((3,)),
+            pltpu.SemaphoreType.DMA((4,)),
         ],
         compiler_params=params,
         name="pack",
-    )(probe_signs, state, conv_weight)
+    )(timesteps, far(probe_signs), far(state), far(conv_weight), far(time_table), gn_shift[None])
 
     across = [(a * 2 + b, (1 - a) * 2 + 1 - b) for a in range(2) for b in range(2)]
-    with jax.named_scope("facing"):
-        facing = lax.ppermute(rim, GX, across)
-    with jax.named_scope("spread"):
-        weights = lax.all_to_all(wsend, PROBE, 0, 0, tiled=True)
+    facing = lax.ppermute(rim, GX, across)
+    weights = lax.all_to_all(wsend, PROBE, 0, 0, tiled=True)
     block = jnp.concatenate([main, facing, rim[48:56]], axis=0)
-    own = [block] + [None] * 3
-    with jax.named_scope("column"):
-        for back in (1, 3, 2):
-            own[back] = lax.ppermute(block, "gy", [(i, (i + back) % 4) for i in range(4)])
-    with jax.named_scope("partner"):
-        other = [lax.ppermute(tile, "gx_1", [(0, 1), (1, 0)]) for tile in own]
-
-    lines = [lax.dynamic_slice(time_table, (timesteps[b], jnp.int32(0)), (1, chans), allow_negative_indices=False) for b in range(4)]
-    offset = jnp.concatenate(lines, axis=0) + gn_shift[None]
+    down = [(i, (i + 1) % 4) for i in range(4)]
+    up = [(i, (i + 3) % 4) for i in range(4)]
+    above = lax.ppermute(block, "gy", down)
+    below = lax.ppermute(block, "gy", up)
+    upper = lax.ppermute(above[:128], "gy", down)
+    lower = lax.ppermute(below[128:], "gy", up)
+    own = [block, above, below, upper, lower]
+    other = [lax.ppermute(tile, "gx_1", [(0, 1), (1, 0)]) for tile in own]
+
     partial = pl.pallas_call(
         mix_kernel,
-        out_shape=shape((128, LANES), F32),
-        in_specs=[VMEM] * 11,
+        out_shape=shape((8, blocks * 16 + 8, LANES), F32),
+        in_specs=[VMEM] * 13,
         out_specs=VMEM,
         scratch_shapes=[
             pltpu.VMEM((blocks, 1440, LANES), F32),
             pltpu.VMEM((blocks, 1440, LANES), F32),
-            pltpu.VMEM((8, chans), F32),
-            pltpu.VMEM((blocks, PAIRS * 16, LANES), F32),
+            pltpu.VMEM((blocks, PAIRS * 128, LANES), F32),
             pltpu.VMEM((1024, PAIRS * LANES), BF16),
             pltpu.VMEM((1024, chans), BF16),
-            pltpu.VMEM((PAIRS * 16, chans), BF16),
+            pltpu.VMEM((PAIRS * 128, chans), BF16),
             pltpu.VMEM((32 * each, LANES), F32),
             pltpu.VMEM((chans, PAIRS * LANES), BF16),
-            pltpu.VMEM((blocks, 16, LANES), F32),
+            pltpu.VMEM((blocks, 128, LANES), F32),
         ],
         compiler_params=params,
         name="mix",
     )(*own, *other, weights, gn_gain[None], offset)
 
-    partial = lax.all_to_all(partial.reshape(8, 16, LANES), ("gy", "gx_1"), 0, 0, tiled=True)
-    message = pl.pallas_call(
+    partial = lax.all_to_all(partial, ("gy", "gx_1"), 0, 0, tiled=True)
+    rows, mass = pl.pallas_call(
         step_kernel,
-        out_shape=shape((64, 16, LANES), BF16),
+        out_shape=(shape((16, chans), BF16), shape((64, LANES), F32)),
         in_specs=[VMEM] * 3,
-        out_specs=VMEM,
-        scratch_shapes=[pltpu.VMEM((blocks, 4, LANES), F32), pltpu.VMEM((16, LANES), F32)],
+        out_specs=(VMEM,) * 2,
+        scratch_shapes=[pltpu.VMEM((blocks, 16, LANES), F32)],
         compiler_params=params,
         name="step",
-    )(partial.reshape(128, LANES), state, conv_bias[None])
-    parts = lax.all_to_all(message, ("gx_0",) + PROBE, 0, 0, tiled=True)
+    )(partial, state, conv_bias[None])
+    mass = lax.all_to_all(mass.reshape(64, 1, LANES), ("gx_0",) + PROBE, 0, 0, tiled=True)
+    quarters = [rows]
+    tall, wide = lax.axis_size("probe_0"), lax.axis_size("probe_1")
+    for code in (1, 2, 3):
+        swap = [(y * wide + z, (y ^ (code // 2)) * wide + (z ^ (code % 2))) for y in range(tall) for z in range(wide)]
+        quarters.append(lax.ppermute(rows, PROBE, swap))
     scale = -0.25 / (probe_signs.shape[0] * lax.axis_size(PROBE))
-    following, mass = pl.pallas_call(
+    return pl.pallas_call(
         lambda *refs: final_kernel(scale, *refs),
         out_shape=(shape(state.shape, BF16), shape((4,), F32)),
-        in_specs=[VMEM],
+        in_specs=[VMEM] * 5,
         out_specs=(VMEM, SMEM),
-        scratch_shapes=[pltpu.VMEM((1024, LANES), F32), pltpu.VMEM((blocks, 64, LANES), F32)],
+        scratch_shapes=[pltpu.VMEM((blocks, 16, LANES), F32)],
         compiler_params=params,
         name="final",
-    )(parts)
-    return following, mass
+    )(mass.reshape(64, LANES), *quarters)
 
 
 def solution(mesh):

time: 123 us -> 126 us (1.024)
  blocking collectives: 32 us -> 0 us
  starting transfers between devices: 50.9 us -> 75.2 us
  waiting for transfers between devices: 18.9 us -> 31.9 us
  local copies, waits for them, and re-layouts: 8.47 us -> 2.99 us
  Pallas kernels: 11.3 us -> 13.7 us
    all_to_all x1 -> x0, blocking collectives: 32 us -> none  [body(): parts = lax.all_to_all(message, ('gx_0',) + PROBE, 0, 0, tiled=True)]
    all_to_all x1 -> x2, starting transfers between devices: 3.71 us -> 17.4 us  [the longest x1 13.2 us: body(): lax.all_to_all(mass.reshape(64, 1, LANES), ('gx_0',) + PROBE, 0, 0, tiled...]
    ppermute x3 -> x7, starting transfers between devices: 10.2 us -> 23 us  [the longest x3 9.21 us: body(): quarters.append(lax.ppermute(rows, PROBE, swap))]
    ppermute x1, waiting for transfers between devices: 13.3 us -> 19 us  [body(): facing = lax.ppermute(rim, GX, across)]
    ppermute x3 -> x7, waiting for transfers between devices: 0.01 us -> 3.29 us  [the longest x3 3.18 us: body(): quarters.append(lax.ppermute(rows, PROBE, swap))]
    dynamic_slice x1 -> x0, local copies, waits for them, and re-layouts: 3.27 us -> none  [body(): lax.dynamic_slice(time_table, (timesteps[b], jnp.int32(0)), (1, chans), a...]
    all_to_all x1 -> x2, waiting for transfers between devices: 5.61 us -> 8.55 us  [the longest x1 8.54 us: body(): partial = lax.all_to_all(partial, ('gy', 'gx_1'), 0, 0, tiled=True)]
    unnamed x20 -> x12, local copies, waits for them, and re-layouts: 4.53 us -> 2.26 us
  transfers between devices with their start and end apart: 10 -> 16, of which waited for: 2 -> 5; matrix products, arithmetic and copies ran while one was open for 3% -> 0% of each run, Pallas kernels for 0% -> 0%
where the time goes in v2:
time: 126 us; the launch traced here: 125 us
  starting transfers between devices  75.2 us (60%)
  waiting for transfers between devices  31.9 us (25%)
  Pallas kernels  13.7 us (11%)
  local copies, waits for them, and re-layouts  2.99 us (2%)
    ppermute x1, waiting for transfers between devices, body(): facing = lax.ppermute(rim, GX, across)  19 us
    ppermute x5, starting transfers between devices, body(): other = [lax.ppermute(tile, 'gx_1', [(0, 1), (1, 0)]) for tile in own]  14.5 us
    all_to_all x1, starting transfers between devices, body(): lax.all_to_all(mass.reshape(64, 1, LANES), ('gx_0',) + PROBE, 0, 0, tiled...  13.2 us
    all_to_all x1, starting transfers between devices, body(): weights = lax.all_to_all(wsend, PROBE, 0, 0, tiled=True)  13.1 us
    ppermute x3, starting transfers between devices, body(): quarters.append(lax.ppermute(rows, PROBE, swap))  9.21 us
    pallas_call x1, Pallas kernels, body(): pl.pallas_call(mix_kernel, out_shape=shape((8, blocks * 16 + 8, LANES), F...  9.05 us
    all_to_all x1, waiting for transfers between devices, body(): partial = lax.all_to_all(partial, ('gy', 'gx_1'), 0, 0, tiled=True)  8.54 us
    ppermute x1, starting transfers between devices, body(): facing = lax.ppermute(rim, GX, across)  7.09 us
  transfers between devices with their start and end apart: 16, of which 5 were waited for; matrix products, arithmetic and copies ran while one was open for 0% of the time, Pallas kernels for 0%

profile of v2, /device:TPU:8, one launch (start us, length us, event | category | flops | bytes accessed | tf_op | source)
XLA Modules:
  0.0 124.8 jit_solution(2986026562475143501)
XLA Ops:
  0.6 0.7 broadcast_in_dim.9.shift_ref
  1.3 0.0 copy-start.3
  1.3 0.7 copy-done.3
  2.0 0.0 copy-start.4
  2.0 3.3 %pack.1 = (bf16[32,120,128]{2,1,0:T(8,128)(2,1)}, bf16[192,640]{1,0:T(8,128)(2,1)S(1)}, bf16[56,640]{1,0:T(8,128)(2,1)S(1)}, f32[8,640]{1,0:T(8,128)S(1)}) custom-call(s32[4]{0:T(128)S(1)} %copy-done.3, s32[2,4,4,4,640]{4,3,2,1,0:T(4,128)} %signs_hbm.1, bf16[4,4,4,640]{3,2,1,0:T(4,128)(2,1)} %state_ref.1, bf16[9,20,640]{2,1,0:T(8,128)(2,1)} %weight_hbm.1, ...), custom_call_target="tpu_custom_call" | custom-call | tf_op jit(solution)/shard_map/pack/pallas_call | solution.py:351
  5.3 13.1 %all-to-all-start = ((bf16[32,120,128]{2,1,0:T(8,128)(2,1)}), bf16[32,120,128]{2,1,0:T(8,128)(2,1)S(1)}, u32[]{:S(2)}, u32[]{:S(2)}) async-start(bf16[32,120,128]{2,1,0:T(8,128)(2,1)} %get-tuple-element.10), calls=%async_computation | async-start | bytes 1966080 | tf_op jit(solution)/shard_map/all_to_all | solution.py:380
  18.4 7.1 %collective-permute-start = (bf16[56,640]{1,0:T(8,128)(2,1)S(1)}, bf16[56,640]{1,0:T(8,128)(2,1)S(1)}, u32[]{:S(2)}, u32[]{:S(2)}) collective-permute-start(bf16[56,640]{1,0:T(8,128)(2,1)S(1)} %get-tuple-element.9), channel_id=1, source_target_pairs={{0,96},{32,64},{64,32},{96,0},{1,97},{33,65},{65,33},{97,1},{2,98}... | collective-permute-start | bytes 215048 | tf_op jit(solution)/shard_map/ppermute | solution.py:379
  25.5 19.0 %collective-permute-done = bf16[56,640]{1,0:T(8,128)(2,1)S(1)} collective-permute-done((bf16[56,640]{1,0:T(8,128)(2,1)S(1)}, bf16[56,640]{1,0:T(8,128)(2,1)S(1)}, u32[]{:S(2)}, u32[]{:S(2)}) %collective-permute-start) | collective-permute-done | bytes 71712 | tf_op jit(solution)/shard_map/ppermute | solution.py:379
  44.5 4.7 %collective-permute-start.2 = (bf16[256,640]{1,0:T(8,128)(2,1)S(1)}, bf16[256,640]{1,0:T(8,128)(2,1)S(1)}, u32[]{:S(2)}, u32[]{:S(2)}) collective-permute-start(bf16[256,640]{1,0:T(8,128)(2,1)S(1)} %pad_maximum_fusion.own0), channel_id=1, source_target_pairs={{0,384},{128,0},{256,128},{384,256},{1,385},{129,1},{257,129},{385... | collective-permute-start | bytes 983048 | tf_op jit(solution)/shard_map/ppermute | solution.py:385
  49.2 1.9 %collective-permute-start.1 = (bf16[256,640]{1,0:T(8,128)(2,1)S(1)}, bf16[256,640]{1,0:T(8,128)(2,1)S(1)}, u32[]{:S(2)}, u32[]{:S(2)}) collective-permute-start(bf16[256,640]{1,0:T(8,128)(2,1)S(1)} %pad_maximum_fusion.own0), channel_id=1, source_target_pairs={{0,128},{128,256},{256,384},{384,0},{1,129},{129,257},{257,385},{3... | collective-permute-start | bytes 983048 | tf_op jit(solution)/shard_map/ppermute | solution.py:384
  51.1 4.6 %collective-permute-start.5 = (bf16[256,640]{1,0:T(8,128)(2,1)S(1)}, bf16[256,640]{1,0:T(8,128)(2,1)S(1)}, u32[]{:S(2)}, u32[]{:S(2)}) collective-permute-start(bf16[256,640]{1,0:T(8,128)(2,1)S(1)} %pad_maximum_fusion.own0), channel_id=1, source_target_pairs={{0,32},{32,0},{1,33},{33,1},{2,34},{34,2},{3,35},{35,3},{4,36},{36... | collective-permute-start | bytes 983048 | tf_op jit(solution)/shard_map/ppermute | solution.py:389
  55.7 0.0 collective-permute-done.2.own3
  55.7 0.0 copy-start.5
  55.8 0.0 copy-start
  55.8 5.3 %collective-permute-start.4 = (bf16[128,640]{1,0:T(8,128)(2,1)S(1)}, bf16[128,640]{1,0:T(8,128)(2,1)S(1)}, u32[]{:S(2)}, u32[]{:S(2)}) collective-permute-start(bf16[128,640]{1,0:T(8,128)(2,1)S(1)} %slice.13), channel_id=1, source_target_pairs={{0,384},{128,0},{256,128},{384,256},{1,385},{129,1},{257,129},{385... | collective-permute-start | bytes 491528 | tf_op jit(solution)/shard_map/ppermute | solution.py:387
  61.1 0.1 collective-permute-done.1.own1
  61.2 1.9 %collective-permute-start.3 = (bf16[128,640]{1,0:T(8,128)(2,1)S(1)}, bf16[128,640]{1,0:T(8,128)(2,1)S(1)}, u32[]{:S(2)}, u32[]{:S(2)}) collective-permute-start(bf16[128,640]{1,0:T(8,128)(2,1)S(1)} %slice.12), channel_id=1, source_target_pairs={{0,128},{128,256},{256,384},{384,0},{1,129},{129,257},{257,385},{3... | collective-permute-start | bytes 491528 | tf_op jit(solution)/shard_map/ppermute | solution.py:386
  63.2 3.4 %collective-permute-start.7 = (bf16[256,640]{1,0:T(8,128)(2,1)S(1)}, bf16[256,640]{1,0:T(8,128)(2,1)S(1)}, u32[]{:S(2)}, u32[]{:S(2)}) collective-permute-start(bf16[256,640]{1,0:T(8,128)(2,1)S(1)} %collective-permute-done.2.own3), channel_id=1, source_target_pairs={{0,32},{32,0},{1,33},{33,1},{2,34},{34,2},{3,35},{35,3},{4,36},{36... | collective-permute-start | bytes 983048 | tf_op jit(solution)/shard_map/ppermute | solution.py:389
  66.6 1.9 %collective-permute-start.6 = (bf16[256,640]{1,0:T(8,128)(2,1)S(1)}, bf16[256,640]{1,0:T(8,128)(2,1)S(1)}, u32[]{:S(2)}, u32[]{:S(2)}) collective-permute-start(bf16[256,640]{1,0:T(8,128)(2,1)S(1)} %collective-permute-done.1.own1), channel_id=1, source_target_pairs={{0,32},{32,0},{1,33},{33,1},{2,34},{34,2},{3,35},{35,3},{4,36},{36... | collective-permute-start | bytes 983048 | tf_op jit(solution)/shard_map/ppermute | solution.py:389
  68.5 0.0 collective-permute-done.4.own2b
  68.5 2.4 %collective-permute-start.9 = (bf16[128,640]{1,0:T(8,128)(2,1)S(1)}, bf16[128,640]{1,0:T(8,128)(2,1)S(1)}, u32[]{:S(2)}, u32[]{:S(2)}) collective-permute-start(bf16[128,640]{1,0:T(8,128)(2,1)S(1)} %collective-permute-done.4.own2b), channel_id=1, source_target_pairs={{0,32},{32,0},{1,33},{33,1},{2,34},{34,2},{3,35},{35,3},{4,36},{36... | collective-permute-start | bytes 491528 | tf_op jit(solution)/shard_map/ppermute | solution.py:389
  70.9 0.0 collective-permute-done.3.own2a
  70.9 2.2 %collective-permute-start.8 = (bf16[128,640]{1,0:T(8,128)(2,1)S(1)}, bf16[128,640]{1,0:T(8,128)(2,1)S(1)}, u32[]{:S(2)}, u32[]{:S(2)}) collective-permute-start(bf16[128,640]{1,0:T(8,128)(2,1)S(1)} %collective-permute-done.3.own2a), channel_id=1, source_target_pairs={{0,32},{32,0},{1,33},{33,1},{2,34},{34,2},{3,35},{35,3},{4,36},{36... | collective-permute-start | bytes 491528 | tf_op jit(solution)/shard_map/ppermute | solution.py:389
  73.1 0.0 copy-done.4
  73.1 0.0 collective-permute-done.5.other0
  73.2 0.0 collective-permute-done.9.other2b
  73.2 1.1 collective-permute-done.8.other2a
  74.2 0.0 copy-start.1
  74.2 0.7 copy-done.1
  74.9 0.0 collective-permute-done.7.other3
  74.9 0.0 collective-permute-done.6.other1
  74.9 0.0 all-to-all-done.weight_ref
  74.9 0.0 copy-start.2
  74.9 0.9 copy-done.2
  75.8 9.1 %mix.1 = f32[8,88,128]{2,1,0:T(8,128)} custom-call(bf16[256,640]{1,0:T(8,128)(2,1)S(1)} %pad_maximum_fusion.own0, bf16[256,640]{1,0:T(8,128)(2,1)S(1)} %collective-permute-done.1.own1, bf16[256,640]{1,0:T(8,128)(2,1)S(1)} %collective-permute-done.2.own3, bf16[128,640]{1,0:T(8,128)(2,1)S(1)} %collective-permute-done.3.own2a, ...), custom_call_target="tpu_custom_call" | custom-call | tf_op jit(solution)/shard_map/mix/pallas_call | solution.py:391
  84.9 4.2 %all-to-all-start.1 = ((f32[8,88,128]{2,1,0:T(8,128)}), f32[8,88,128]{2,1,0:T(8,128)S(1)}, u32[]{:S(2)}, u32[]{:S(2)}) async-start(f32[8,88,128]{2,1,0:T(8,128)} %mix.1), calls=%async_computation.1 | async-start | bytes 720896 | tf_op jit(solution)/shard_map/all_to_all | solution.py:411
  89.1 0.0 copy-done.5
  89.1 8.5 %all-to-all-done.1.parts_ref = f32[8,88,128]{2,1,0:T(8,128)S(1)} async-done(((f32[8,88,128]{2,1,0:T(8,128)}), f32[8,88,128]{2,1,0:T(8,128)S(1)}, u32[]{:S(2)}, u32[]{:S(2)}) %all-to-all-start.1) | async-done | bytes 360480 | tf_op jit(solution)/shard_map/all_to_all | solution.py:411
  97.7 0.0 copy-done
  97.7 0.7 step.1
  98.4 13.2 %all-to-all-start.2 = ((f32[64,1,128]{2,1,0:T(1,128)}), f32[64,1,128]{2,1,0:T(1,128)S(1)}, u32[]{:S(2)}, u32[]{:S(2)}) async-start(f32[64,1,128]{2,1,0:T(1,128)} %bitcast.1), calls=%async_computation.2 | async-start | bytes 65536 | tf_op jit(solution)/shard_map/all_to_all | solution.py:421
  111.6 3.4 %collective-permute-start.12 = (bf16[16,640]{1,0:T(8,128)(2,1)S(1)}, bf16[16,640]{1,0:T(8,128)(2,1)S(1)}, u32[]{:S(2)}, u32[]{:S(2)}) collective-permute-start(bf16[16,640]{1,0:T(8,128)(2,1)S(1)} %get-tuple-element.13.refs_1_), channel_id=1, source_target_pairs={{0,5},{1,4},{2,7},{3,6},{4,1},{5,0},{6,3},{7,2},{8,13},{9,12},{10,... | collective-permute-start | bytes 61448 | tf_op jit(solution)/shard_map/ppermute | solution.py:426
  115.0 3.4 %collective-permute-start.11 = (bf16[16,640]{1,0:T(8,128)(2,1)S(1)}, bf16[16,640]{1,0:T(8,128)(2,1)S(1)}, u32[]{:S(2)}, u32[]{:S(2)}) collective-permute-start(bf16[16,640]{1,0:T(8,128)(2,1)S(1)} %get-tuple-element.13.refs_1_), channel_id=1, source_target_pairs={{0,4},{1,5},{2,6},{3,7},{4,0},{5,1},{6,2},{7,3},{8,12},{9,13},{10,... | collective-permute-start | bytes 61448 | tf_op jit(solution)/shard_map/ppermute | solution.py:426
  118.4 2.5 %collective-permute-start.10 = (bf16[16,640]{1,0:T(8,128)(2,1)S(1)}, bf16[16,640]{1,0:T(8,128)(2,1)S(1)}, u32[]{:S(2)}, u32[]{:S(2)}) collective-permute-start(bf16[16,640]{1,0:T(8,128)(2,1)S(1)} %get-tuple-element.13.refs_1_), channel_id=1, source_target_pairs={{0,1},{1,0},{2,3},{3,2},{4,5},{5,4},{6,7},{7,6},{8,9},{9,8},{10,11... | collective-permute-start | bytes 61448 | tf_op jit(solution)/shard_map/ppermute | solution.py:426
  120.8 0.0 collective-permute-done.12.refs_4_
  120.9 0.0 collective-permute-done.11.refs_3_
  120.9 3.2 %collective-permute-done.10.refs_2_ = bf16[16,640]{1,0:T(8,128)(2,1)S(1)} collective-permute-done((bf16[16,640]{1,0:T(8,128)(2,1)S(1)}, bf16[16,640]{1,0:T(8,128)(2,1)S(1)}, u32[]{:S(2)}, u32[]{:S(2)}) %collective-permute-start.10) | collective-permute-done | bytes 20512 | tf_op jit(solution)/shard_map/ppermute | solution.py:426
  124.0 0.0 all-to-all-done.2
  124.0 0.7 final.1
  (6 shorter events, 0.1 us)
Async XLA Ops:
  1.3 0.7 copy-start.3
  2.0 71.2 %copy-start.4 = (f32[640]{0:T(1024)S(1)}, f32[640]{0:T(1024)}, u32[]{:S(2)}) copy-start(f32[640]{0:T(1024)} %param.12) | copy-start | bytes 7684
  5.3 69.7 %all-to-all-start = ((bf16[32,120,128]{2,1,0:T(8,128)(2,1)}), bf16[32,120,128]{2,1,0:T(8,128)(2,1)S(1)}, u32[]{:S(2)}, u32[]{:S(2)}) async-start(bf16[32,120,128]{2,1,0:T(8,128)(2,1)} %get-tuple-element.10), calls=%async_computation | async-start | bytes 1966080 | tf_op jit(solution)/shard_map/all_to_all | solution.py:380
  18.4 26.1 %collective-permute-start = (bf16[56,640]{1,0:T(8,128)(2,1)S(1)}, bf16[56,640]{1,0:T(8,128)(2,1)S(1)}, u32[]{:S(2)}, u32[]{:S(2)}) collective-permute-start(bf16[56,640]{1,0:T(8,128)(2,1)S(1)} %get-tuple-element.9), channel_id=1, source_target_pairs={{0,96},{32,64},{64,32},{96,0},{1,97},{33,65},{65,33},{97,1},{2,98}... | collective-permute-start | bytes 215048 | tf_op jit(solution)/shard_map/ppermute | solution.py:379
  44.5 11.2 %collective-permute-start.2 = (bf16[256,640]{1,0:T(8,128)(2,1)S(1)}, bf16[256,640]{1,0:T(8,128)(2,1)S(1)}, u32[]{:S(2)}, u32[]{:S(2)}) collective-permute-start(bf16[256,640]{1,0:T(8,128)(2,1)S(1)} %pad_maximum_fusion.own0), channel_id=1, source_target_pairs={{0,384},{128,0},{256,128},{384,256},{1,385},{129,1},{257,129},{385... | collective-permute-start | bytes 983048 | tf_op jit(solution)/shard_map/ppermute | solution.py:385
  49.2 12.0 %collective-permute-start.1 = (bf16[256,640]{1,0:T(8,128)(2,1)S(1)}, bf16[256,640]{1,0:T(8,128)(2,1)S(1)}, u32[]{:S(2)}, u32[]{:S(2)}) collective-permute-start(bf16[256,640]{1,0:T(8,128)(2,1)S(1)} %pad_maximum_fusion.own0), channel_id=1, source_target_pairs={{0,128},{128,256},{256,384},{384,0},{1,129},{129,257},{257,385},{3... | collective-permute-start | bytes 983048 | tf_op jit(solution)/shard_map/ppermute | solution.py:384
  51.1 22.0 %collective-permute-start.5 = (bf16[256,640]{1,0:T(8,128)(2,1)S(1)}, bf16[256,640]{1,0:T(8,128)(2,1)S(1)}, u32[]{:S(2)}, u32[]{:S(2)}) collective-permute-start(bf16[256,640]{1,0:T(8,128)(2,1)S(1)} %pad_maximum_fusion.own0), channel_id=1, source_target_pairs={{0,32},{32,0},{1,33},{33,1},{2,34},{34,2},{3,35},{35,3},{4,36},{36... | collective-permute-start | bytes 983048 | tf_op jit(solution)/shard_map/ppermute | solution.py:389
  55.7 33.4 %copy-start.5 = (f32[640]{0:T(1024)S(1)}, f32[640]{0:T(1024)}, u32[]{:S(2)}) copy-start(f32[640]{0:T(1024)} %param.15) | copy-start | bytes 7684
  55.8 41.9 %copy-start = (bf16[4,4,4,640]{3,2,1,0:T(4,128)(2,1)S(1)}, bf16[4,4,4,640]{3,2,1,0:T(4,128)(2,1)}, u32[]{:S(2)}) copy-start(bf16[4,4,4,640]{3,2,1,0:T(4,128)(2,1)} %state_ref.1) | copy-start | bytes 245764
  55.8 12.7 %collective-permute-start.4 = (bf16[128,640]{1,0:T(8,128)(2,1)S(1)}, bf16[128,640]{1,0:T(8,128)(2,1)S(1)}, u32[]{:S(2)}, u32[]{:S(2)}) collective-permute-start(bf16[128,640]{1,0:T(8,128)(2,1)S(1)} %slice.13), channel_id=1, source_target_pairs={{0,384},{128,0},{256,128},{384,256},{1,385},{129,1},{257,129},{385... | collective-permute-start | bytes 491528 | tf_op jit(solution)/shard_map/ppermute | solution.py:387
  61.2 9.7 %collective-permute-start.3 = (bf16[128,640]{1,0:T(8,128)(2,1)S(1)}, bf16[128,640]{1,0:T(8,128)(2,1)S(1)}, u32[]{:S(2)}, u32[]{:S(2)}) collective-permute-start(bf16[128,640]{1,0:T(8,128)(2,1)S(1)} %slice.12), channel_id=1, source_target_pairs={{0,128},{128,256},{256,384},{384,0},{1,129},{129,257},{257,385},{3... | collective-permute-start | bytes 491528 | tf_op jit(solution)/shard_map/ppermute | solution.py:386
  63.2 11.8 %collective-permute-start.7 = (bf16[256,640]{1,0:T(8,128)(2,1)S(1)}, bf16[256,640]{1,0:T(8,128)(2,1)S(1)}, u32[]{:S(2)}, u32[]{:S(2)}) collective-permute-start(bf16[256,640]{1,0:T(8,128)(2,1)S(1)} %collective-permute-done.2.own3), channel_id=1, source_target_pairs={{0,32},{32,0},{1,33},{33,1},{2,34},{34,2},{3,35},{35,3},{4,36},{36... | collective-permute-start | bytes 983048 | tf_op jit(solution)/shard_map/ppermute | solution.py:389
  66.6 8.3 %collective-permute-start.6 = (bf16[256,640]{1,0:T(8,128)(2,1)S(1)}, bf16[256,640]{1,0:T(8,128)(2,1)S(1)}, u32[]{:S(2)}, u32[]{:S(2)}) collective-permute-start(bf16[256,640]{1,0:T(8,128)(2,1)S(1)} %collective-permute-done.1.own1), channel_id=1, source_target_pairs={{0,32},{32,0},{1,33},{33,1},{2,34},{34,2},{3,35},{35,3},{4,36},{36... | collective-permute-start | bytes 983048 | tf_op jit(solution)/shard_map/ppermute | solution.py:389
  68.5 4.6 %collective-permute-start.9 = (bf16[128,640]{1,0:T(8,128)(2,1)S(1)}, bf16[128,640]{1,0:T(8,128)(2,1)S(1)}, u32[]{:S(2)}, u32[]{:S(2)}) collective-permute-start(bf16[128,640]{1,0:T(8,128)(2,1)S(1)} %collective-permute-done.4.own2b), channel_id=1, source_target_pairs={{0,32},{32,0},{1,33},{33,1},{2,34},{34,2},{3,35},{35,3},{4,36},{36... | collective-permute-start | bytes 491528 | tf_op jit(solution)/shard_map/ppermute | solution.py:389
  70.9 3.3 %collective-permute-start.8 = (bf16[128,640]{1,0:T(8,128)(2,1)S(1)}, bf16[128,640]{1,0:T(8,128)(2,1)S(1)}, u32[]{:S(2)}, u32[]{:S(2)}) collective-permute-start(bf16[128,640]{1,0:T(8,128)(2,1)S(1)} %collective-permute-done.3.own2a), channel_id=1, source_target_pairs={{0,32},{32,0},{1,33},{33,1},{2,34},{34,2},{3,35},{35,3},{4,36},{36... | collective-permute-start | bytes 491528 | tf_op jit(solution)/shard_map/ppermute | solution.py:389
  74.2 0.7 copy-start.1
  74.9 0.9 copy-start.2
  84.9 12.8 %all-to-all-start.1 = ((f32[8,88,128]{2,1,0:T(8,128)}), f32[8,88,128]{2,1,0:T(8,128)S(1)}, u32[]{:S(2)}, u32[]{:S(2)}) async-start(f32[8,88,128]{2,1,0:T(8,128)} %mix.1), calls=%async_computation.1 | async-start | bytes 720896 | tf_op jit(solution)/shard_map/all_to_all | solution.py:411
  98.4 25.7 %all-to-all-start.2 = ((f32[64,1,128]{2,1,0:T(1,128)}), f32[64,1,128]{2,1,0:T(1,128)S(1)}, u32[]{:S(2)}, u32[]{:S(2)}) async-start(f32[64,1,128]{2,1,0:T(1,128)} %bitcast.1), calls=%async_computation.2 | async-start | bytes 65536 | tf_op jit(solution)/shard_map/all_to_all | solution.py:421
  111.6 9.2 %collective-permute-start.12 = (bf16[16,640]{1,0:T(8,128)(2,1)S(1)}, bf16[16,640]{1,0:T(8,128)(2,1)S(1)}, u32[]{:S(2)}, u32[]{:S(2)}) collective-permute-start(bf16[16,640]{1,0:T(8,128)(2,1)S(1)} %get-tuple-element.13.refs_1_), channel_id=1, source_target_pairs={{0,5},{1,4},{2,7},{3,6},{4,1},{5,0},{6,3},{7,2},{8,13},{9,12},{10,... | collective-permute-start | bytes 61448 | tf_op jit(solution)/shard_map/ppermute | solution.py:426
  115.0 5.9 %collective-permute-start.11 = (bf16[16,640]{1,0:T(8,128)(2,1)S(1)}, bf16[16,640]{1,0:T(8,128)(2,1)S(1)}, u32[]{:S(2)}, u32[]{:S(2)}) collective-permute-start(bf16[16,640]{1,0:T(8,128)(2,1)S(1)} %get-tuple-element.13.refs_1_), channel_id=1, source_target_pairs={{0,4},{1,5},{2,6},{3,7},{4,0},{5,1},{6,2},{7,3},{8,12},{9,13},{10,... | collective-permute-start | bytes 61448 | tf_op jit(solution)/shard_map/ppermute | solution.py:426
  118.4 5.7 %collective-permute-start.10 = (bf16[16,640]{1,0:T(8,128)(2,1)S(1)}, bf16[16,640]{1,0:T(8,128)(2,1)S(1)}, u32[]{:S(2)}, u32[]{:S(2)}) collective-permute-start(bf16[16,640]{1,0:T(8,128)(2,1)S(1)} %get-tuple-element.13.refs_1_), channel_id=1, source_target_pairs={{0,1},{1,0},{2,3},{3,2},{4,5},{5,4},{6,7},{7,6},{8,9},{9,8},{10,11... | collective-permute-start | bytes 61448 | tf_op jit(solution)/shard_map/ppermute | solution.py:426

commit v3 on v2

--- a/solution.py
+++ b/solution.py
@@ -37,8 +37,12 @@
     return jnp.where(upper, rows, turned), jnp.where(upper, turned, rows)
 
 
-def quarter():
-    return 2 * lax.rem(lax.axis_index("probe_0"), 2) + lax.rem(lax.axis_index("probe_1"), 2)
+def half_rows():
+    return 2 * lax.rem(lax.axis_index("probe_0"), 2)
+
+
+def first_block(member):
+    return member * PAIRS // 9
 
 
 def pair_of(index):
@@ -47,19 +51,20 @@
     return lax.rem(number, 9), lax.div(number, 9)
 
 
-def pack_kernel(
-    step_ref, signs_hbm, state_hbm, weight_hbm, table_hbm, shift_ref, wsend_ref, main_ref, rim_ref, offset_ref,
-    signs_ref, state_ref, weight_ref, table, uf, xf, wf, rim, sums, arrived, found,
-):
-    blocks = uf.shape[0]
-    loads = [
-        pltpu.make_async_copy(src, dst, arrived.at[index])
-        for index, (src, dst) in enumerate(
-            ((weight_hbm, weight_ref), (state_hbm, state_ref), (signs_hbm, signs_ref))
-        )
-    ]
-    for load in loads:
-        load.start()
+def spread_kernel(weight_ref, wsend_ref, wf):
+    for index in range(PAIRS):
+        tap, ob = pair_of(index)
+        rows = weight_ref[tap].astype(F32)
+        picked = jnp.zeros((rows.shape[0], LANES), F32)
+        for o in range(rows.shape[1] // LANES):
+            picked = picked + jnp.where(ob == o, rows[:, lane_block(o)], 0.0)
+        wf[pl.ds(index, rows.shape[0], stride=PAIRS), :] = picked
+    packed = wf[...].astype(BF16)
+    for target in range(wsend_ref.shape[0]):
+        wsend_ref[target] = packed
+
+
+def lookup_kernel(step_ref, table_hbm, shift_ref, offset_ref, table, found):
     steps = [step_ref[b] for b in range(4)]
     finds = [
         pltpu.make_async_copy(
@@ -69,20 +74,23 @@
     ]
     for find in finds:
         find.start()
-    loads[0].wait()
-    for index in range(PAIRS):
-        tap, ob = pair_of(index)
-        rows = weight_ref[tap].astype(F32)
-        picked = jnp.zeros((rows.shape[0], LANES), F32)
-        for o in range(blocks):
-            picked = picked + jnp.where(ob == o, rows[:, lane_block(o)], 0.0)
-        wf[pl.ds(index, rows.shape[0], stride=PAIRS), :] = picked
-    packed = wf[...].astype(BF16)
-    for target in range(wsend_ref.shape[0]):
-        wsend_ref[target] = packed
-
-    loads[1].wait()
-    loads[2].wait()
+    for b in range(4):
+        finds[b].wait()
+        line = table[b, pl.ds(lax.rem(steps[b], 8), 1), :] + shift_ref[...]
+        offset_ref[b : b + 1, :] = line
+        offset_ref[b + 4 : b + 5, :] = line
+
+
+def pack_kernel(signs_hbm, state_hbm, main_ref, rim_ref, signs_ref, state_ref, uf, xf, rim, sums, arrived):
+    blocks = uf.shape[0]
+    loads = [
+        pltpu.make_async_copy(src, dst, arrived.at[index])
+        for index, (src, dst) in enumerate(((signs_hbm, signs_ref), (state_hbm, state_ref)))
+    ]
+    for load in loads:
+        load.start()
+    for load in loads:
+        load.wait()
     for p in range(2):
         for b in range(4):
             for r in range(4):
@@ -133,17 +141,14 @@
         main_ref[0:128, lane_block(o)] = uf[o].astype(BF16)
         main_ref[128:192, lane_block(o)] = xf[o].astype(BF16)
     rim_ref[...] = rim[...].astype(BF16)
-    for b in range(4):
-        finds[b].wait()
-        line = table[b, pl.ds(lax.rem(steps[b], 8), 1), :] + shift_ref[...]
-        offset_ref[b : b + 1, :] = line
-        offset_ref[b + 4 : b + 5, :] = line
 
 
 def mix_kernel(
-    own0, own1, own3, own2a, own2b, other0, other1, other3, other2a, other2b, weight_ref, gain_ref, offset_ref,
-    out_ref, ug, xg, picked, lhs_ref, slope_ref, rows_ref, wf, wc, velocity,
+    own0, own1, own3, own2, other0, other1, other3, other2, weight_hbm, gain_ref, offset_ref,
+    out_ref, ug, xg, picked, lhs_ref, slope_ref, rows_ref, weight_ref, wf, wc, velocity, arrived,
 ):
+    load = pltpu.make_async_copy(weight_hbm, weight_ref, arrived)
+    load.start()
     blocks = ug.shape[0]
     core = lax.axis_index("gx_1")
     half = lax.axis_index("gx_0")
@@ -157,28 +162,22 @@
     total = jnp.zeros((8, chans), F32)
     rim_here = core == 1 - half
     rim_col = jnp.where(half == 0, 9, 0)
-    whole = lambda ref: (ref.at[0:128], ref.at[128:256])
-    sources = (
-        (0, whole(own0), whole(other0)),
-        (1, whole(own1), whole(other1)),
-        (3, whole(own3), whole(other3)),
-        (2, (own2a, own2b), (other2a, other2b)),
-    )
+    sources = ((0, own0, other0), (1, own1, other1), (3, own3, other3), (2, own2, other2))
     for back, own_ref, other_ref in sources:
         tile = lax.rem(lax.axis_index("gy") + 4 - back, 4)
-        for (upper, lower), base in ((own_ref, 4 * core), (other_ref, 4 * (1 - core))):
+        for src, base in ((own_ref, 4 * core), (other_ref, 4 * (1 - core))):
             for r in range(4):
                 at = spot(4 * tile + r + 1, base + 1)
-                lines = upper[r * 32 : r * 32 + 32, :].astype(F32)
-                states = lower[r * 16 : r * 16 + 16, :].astype(F32)
+                lines = src[r * 32 : r * 32 + 32, :].astype(F32)
+                states = src[128 + r * 16 : 144 + r * 16, :].astype(F32)
                 for o in range(blocks):
                     ug[o, pl.ds(at, 32), :] = lines[:, lane_block(o)]
                     for two in range(2):
                         pair = doubled_rows(states[two * 8 : two * 8 + 8, lane_block(o)])
                         xg[o, pl.ds(pl.multiple_of(at + two * 16, 8), 8), :] = pair[0]
                         xg[o, pl.ds(pl.multiple_of(at + two * 16 + 8, 8), 8), :] = pair[1]
-        mine = own_ref[1][64:128, :].astype(F32)
-        theirs = other_ref[1][64:128, :].astype(F32)
+        mine = own_ref[192:256, :].astype(F32)
+        theirs = other_ref[192:256, :].astype(F32)
         total = total + mine[48:56] + mine[56:64] + theirs[48:56] + theirs[56:64]
         rim = jnp.where(rim_here, mine[0:48], theirs[0:48])
         for r in range(4):
@@ -254,22 +253,23 @@
 
     lax.fori_loop(0, 16, lhs_row, 0)
 
-    row = quarter()
     early = lax.broadcasted_iota(jnp.int32, (8, LANES), 0) < 4
     for index, (tap, ob) in enumerate(taps):
         dy, dx = lax.div(tap, 3), lax.rem(tap, 3)
         for target in range(8):
-            at = spot(4 * (target // 2) + row + dy, 4 * (target % 2) + dx)
-            to = index * 128 + target * 16
-            for o in range(blocks):
-                for two in range(2):
-                    first = xg[o, pl.ds(pl.multiple_of(at + two * 16, 8), 8), :]
-                    second = xg[o, pl.ds(pl.multiple_of(at + two * 16 + 8, 8), 8), :]
-                    both = jnp.where(early, first, pltpu.roll(second, 4, axis=0))
-                    picked[o, to + two * 8 : to + two * 8 + 8, :] = both
+            for line in range(2):
+                at = spot(4 * (target // 2) + half_rows() + line + dy, 4 * (target % 2) + dx)
+                to = index * 256 + target * 32 + line * 16
+                for o in range(blocks):
+                    for two in range(2):
+                        first = xg[o, pl.ds(pl.multiple_of(at + two * 16, 8), 8), :]
+                        second = xg[o, pl.ds(pl.multiple_of(at + two * 16 + 8, 8), 8), :]
+                        both = jnp.where(early, first, pltpu.roll(second, 4, axis=0))
+                        picked[o, to + two * 8 : to + two * 8 + 8, :] = both
     for o in range(blocks):
         rows_ref[:, lane_block(o)] = picked[o].astype(BF16)
 
+    load.wait()
     each = weight_ref.shape[1]
     for source in range(weight_ref.shape[0]):
         wf[source * each : (source + 1) * each, :] = weight_ref[source].astype(F32)
@@ -291,51 +291,56 @@
 
     velocity[...] = jnp.zeros(velocity.shape, F32)
     for index in range(PAIRS):
-        ob = jnp.minimum(taps[index][1], blocks - 1)
+        slot = taps[index][1] - lax.div((lax.axis_index("gy") * 2 + lax.axis_index("gx_1")) * PAIRS, 9)
         part = jnp.dot(
-            rows_ref[index * 128 : index * 128 + 128, :], wc[:, lane_block(index)], preferred_element_type=F32
+            rows_ref[index * 256 : index * 256 + 256, :], wc[:, lane_block(index)], preferred_element_type=F32
         )
-        velocity[ob] = velocity[ob] + part
+        velocity[slot] = velocity[slot] + part
     for target in range(8):
-        for o in range(blocks):
-            out_ref[target, o * 16 : o * 16 + 16, :] = velocity[o, target * 16 : target * 16 + 16, :]
-        out_ref[target, blocks * 16 : blocks * 16 + 8, :] = lanes
+        for slot in range(2):
+            out_ref[target, slot * 32 : slot * 32 + 32, :] = velocity[slot, target * 32 : target * 32 + 32, :]
+        out_ref[target, 64:72, :] = lanes
 
 
 def step_kernel(parts_ref, state_ref, bias_ref, rows_ref, mass_ref, lines):
     blocks = bias_ref.shape[1] // LANES
-    total = parts_ref[0]
+    total = parts_ref[0, 64:72, :]
     for source in range(1, 8):
-        total = total + parts_ref[source]
-    mass = jnp.sum(total[blocks * 16 : blocks * 16 + 8, :], axis=1, keepdims=True)
+        total = total + parts_ref[source, 64:72, :]
+    mass = jnp.sum(total, axis=1, keepdims=True)
     lane = lax.broadcasted_iota(jnp.int32, (8, LANES), 1)
     latents = lax.broadcasted_iota(jnp.int32, (8, LANES), 0)
     line = jnp.sum(jnp.where(lane == latents, mass, 0.0), axis=0, keepdims=True)
     mass_ref[...] = jnp.broadcast_to(line, mass_ref.shape)
-    row = quarter()
     for b in range(4):
-        here = state_ref[b, row].astype(F32)
-        for o in range(blocks):
-            lines[o, pl.ds(b, 4, stride=4), :] = here[:, lane_block(o)]
+        for r in range(2):
+            here = state_ref[b, half_rows() + r].astype(F32)
+            for o in range(blocks):
+                lines[o, pl.ds(r * 16 + b, 4, stride=4), :] = here[:, lane_block(o)]
+    velocity = [jnp.broadcast_to(bias_ref[:, lane_block(o)], (32, LANES)) for o in range(blocks)]
+    for source in range(8):
+        for slot in range(2):
+            o = first_block(source) + slot
+            if o < blocks:
+                velocity[o] = velocity[o] + parts_ref[source, slot * 32 : slot * 32 + 32, :]
     for o in range(blocks):
-        value = lines[o] + 0.25 * (total[o * 16 : o * 16 + 16, :] + bias_ref[:, lane_block(o)])
-        rows_ref[:, lane_block(o)] = value.astype(BF16)
-
-
-def final_kernel(scale, mass_ref, rows0, rows1, rows2, rows3, next_ref, out_ref, lines):
+        rows_ref[:, lane_block(o)] = (lines[o] + 0.25 * velocity[o]).astype(BF16)
+
+
+def final_kernel(scale, mass_ref, rows0, rows1, next_ref, out_ref, lines):
     blocks = lines.shape[0]
     total = jnp.sum(mass_ref[...], axis=0, keepdims=True)
     lane = lax.broadcasted_iota(jnp.int32, (1, LANES), 1)
     for b in range(4):
         out_ref[b] = scale * jnp.sum(jnp.where(lane == b, total, 0.0))
-    for code, rows in enumerate((rows0, rows1, rows2, rows3)):
-        tall, wide = lax.axis_index("probe_0") + code // 2, lax.axis_index("probe_1") + code % 2
-        row = 2 * lax.rem(tall, 2) + lax.rem(wide, 2)
+    for start, rows in ((half_rows(), rows0), (2 - half_rows(), rows1)):
         for o in range(blocks):
             lines[o] = rows[:, lane_block(o)].astype(F32)
         for o in range(blocks):
             for b in range(4):
-                next_ref[b, row, :, lane_block(o)] = lines[o, pl.ds(b, 4, stride=4), :].astype(BF16)
+                for r in range(2):
+                    value = lines[o, pl.ds(r * 16 + b, 4, stride=4), :].astype(BF16)
+                    next_ref[b, start + r, :, lane_block(o)] = value
 
 
 def shape(dims, kind):
@@ -348,32 +353,41 @@
     each = conv_weight.shape[1] * PAIRS
     params = pltpu.CompilerParams(vmem_limit_bytes=40 * 1024 * 1024)
     far = lambda array: pltpu.with_memory_space_constraint(array, pltpu.HBM)
-    wsend, main, rim, offset = pl.pallas_call(
+    main, rim = pl.pallas_call(
         pack_kernel,
-        out_shape=(
-            shape((32, each, LANES), BF16),
-            shape((192, chans), BF16),
-            shape((56, chans), BF16),
-            shape((8, chans), F32),
-        ),
-        in_specs=[SMEM] + [HBM] * 4 + [VMEM],
-        out_specs=(VMEM,) * 4,
+        out_shape=(shape((192, chans), BF16), shape((56, chans), BF16)),
+        in_specs=[HBM] * 2,
+        out_specs=(VMEM,) * 2,
         scratch_shapes=[
             pltpu.VMEM(probe_signs.shape, jnp.int32),
             pltpu.VMEM(state.shape, BF16),
-            pltpu.VMEM(conv_weight.shape, BF16),
-            pltpu.VMEM((4, 8, chans), F32),
             pltpu.VMEM((blocks, 128, LANES), F32),
             pltpu.VMEM((blocks, 64, LANES), F32),
-            pltpu.VMEM((each, LANES), F32),
             pltpu.VMEM((56, chans), F32),
             pltpu.VMEM((32, chans), F32),
-            pltpu.SemaphoreType.DMA((3,)),
-            pltpu.SemaphoreType.DMA((4,)),
+            pltpu.SemaphoreType.DMA((2,)),
         ],
         compiler_params=params,
         name="pack",
-    )(timesteps, far(probe_signs), far(state), far(conv_weight), far(time_table), gn_shift[None])
+    )(far(probe_signs), far(state))
+    wsend = pl.pallas_call(
+        spread_kernel,
+        out_shape=shape((32, each, LANES), BF16),
+        in_specs=[VMEM],
+        out_specs=VMEM,
+        scratch_shapes=[pltpu.VMEM((each, LANES), F32)],
+        compiler_params=params,
+        name="deal",
+    )(conv_weight)
+    offset = pl.pallas_call(
+        lookup_kernel,
+        out_shape=shape((8, chans), F32),
+        in_specs=[SMEM, HBM, VMEM],
+        out_specs=VMEM,
+        scratch_shapes=[pltpu.VMEM((4, 8, chans), F32), pltpu.SemaphoreType.DMA((4,))],
+        compiler_params=params,
+        name="lookup",
+    )(timesteps, far(time_table), gn_shift[None])
 
     across = [(a * 2 + b, (1 - a) * 2 + 1 - b) for a in range(2) for b in range(2)]
     facing = lax.ppermute(rim, GX, across)
@@ -383,57 +397,56 @@
     up = [(i, (i + 3) % 4) for i in range(4)]
     above = lax.ppermute(block, "gy", down)
     below = lax.ppermute(block, "gy", up)
-    upper = lax.ppermute(above[:128], "gy", down)
-    lower = lax.ppermute(below[128:], "gy", up)
-    own = [block, above, below, upper, lower]
+    onward = [(x * 2 + c, (x + 1 - 2 * c) % 4 * 2 + c) for x in range(4) for c in range(2)]
+    beyond = lax.ppermute(jnp.where(lax.axis_index("gx_1") == 0, above, below), ("gy", "gx_1"), onward)
+    own = [block, above, below, beyond]
     other = [lax.ppermute(tile, "gx_1", [(0, 1), (1, 0)]) for tile in own]
 
     partial = pl.pallas_call(
         mix_kernel,
-        out_shape=shape((8, blocks * 16 + 8, LANES), F32),
-        in_specs=[VMEM] * 13,
+        out_shape=shape((8, 72, LANES), F32),
+        in_specs=[VMEM] * 8 + [HBM] + [VMEM] * 2,
         out_specs=VMEM,
         scratch_shapes=[
             pltpu.VMEM((blocks, 1440, LANES), F32),
             pltpu.VMEM((blocks, 1440, LANES), F32),
-            pltpu.VMEM((blocks, PAIRS * 128, LANES), F32),
+            pltpu.VMEM((blocks, PAIRS * 256, LANES), F32),
             pltpu.VMEM((1024, PAIRS * LANES), BF16),
             pltpu.VMEM((1024, chans), BF16),
-            pltpu.VMEM((PAIRS * 128, chans), BF16),
+            pltpu.VMEM((PAIRS * 256, chans), BF16),
+            pltpu.VMEM((32, each, LANES), BF16),
             pltpu.VMEM((32 * each, LANES), F32),
             pltpu.VMEM((chans, PAIRS * LANES), BF16),
-            pltpu.VMEM((blocks, 128, LANES), F32),
+            pltpu.VMEM((2, 256, LANES), F32),
+            pltpu.SemaphoreType.DMA,
         ],
         compiler_params=params,
         name="mix",
-    )(*own, *other, weights, gn_gain[None], offset)
+    )(*own, *other, far(weights), gn_gain[None], offset)
 
     partial = lax.all_to_all(partial, ("gy", "gx_1"), 0, 0, tiled=True)
     rows, mass = pl.pallas_call(
         step_kernel,
-        out_shape=(shape((16, chans), BF16), shape((64, LANES), F32)),
+        out_shape=(shape((32, chans), BF16), shape((64, LANES), F32)),
         in_specs=[VMEM] * 3,
         out_specs=(VMEM,) * 2,
-        scratch_shapes=[pltpu.VMEM((blocks, 16, LANES), F32)],
+        scratch_shapes=[pltpu.VMEM((blocks, 32, LANES), F32)],
         compiler_params=params,
         name="step",
     )(partial, state, conv_bias[None])
     mass = lax.all_to_all(mass.reshape(64, 1, LANES), ("gx_0",) + PROBE, 0, 0, tiled=True)
-    quarters = [rows]
-    tall, wide = lax.axis_size("probe_0"), lax.axis_size("probe_1")
-    for code in (1, 2, 3):
-        swap = [(y * wide + z, (y ^ (code // 2)) * wide + (z ^ (code % 2))) for y in range(tall) for z in range(wide)]
-        quarters.append(lax.ppermute(rows, PROBE, swap))
+    tall = lax.axis_size("probe_0")
+    facing_rows = lax.ppermute(rows, "probe_0", [(y, y ^ 1) for y in range(tall)])
     scale = -0.25 / (probe_signs.shape[0] * lax.axis_size(PROBE))
     return pl.pallas_call(
         lambda *refs: final_kernel(scale, *refs),
         out_shape=(shape(state.shape, BF16), shape((4,), F32)),
-        in_specs=[VMEM] * 5,
+        in_specs=[VMEM] * 3,
         out_specs=(VMEM, SMEM),
-        scratch_shapes=[pltpu.VMEM((blocks, 16, LANES), F32)],
+        scratch_shapes=[pltpu.VMEM((blocks, 32, LANES), F32)],
         compiler_params=params,
         name="final",
-    )(mass.reshape(64, LANES), *quarters)
+    )(mass.reshape(64, LANES), rows, facing_rows)
 
 
 def solution(mesh):

time: 126 us -> 119 us (0.944)
  the two profiles are of different devices: /device:TPU:8 before, /device:TPU:2 now
where the time goes in v3:
time: 119 us; the launch traced here: 118 us
  starting transfers between devices  56.2 us (47%)
  waiting for transfers between devices  44.8 us (38%)
  Pallas kernels  15.1 us (13%)
    ppermute x1, waiting for transfers between devices, body(): facing = lax.ppermute(rim, GX, across)  20.6 us
    all_to_all x1, starting transfers between devices, body(): weights = lax.all_to_all(wsend, PROBE, 0, 0, tiled=True)  13 us
    pallas_call x1, Pallas kernels, body(): pl.pallas_call(mix_kernel, out_shape=shape((8, 72, LANES), F32), in_specs...  9.69 us
    all_to_all x1, starting transfers between devices, body(): lax.all_to_all(mass.reshape(64, 1, LANES), ('gx_0',) + PROBE, 0, 0, tiled...  9.69 us
    ppermute x4, starting transfers between devices, body(): other = [lax.ppermute(tile, 'gx_1', [(0, 1), (1, 0)]) for tile in own]  8.65 us
    ppermute x1, starting transfers between devices, body(): facing = lax.ppermute(rim, GX, across)  7.38 us
    all_to_all x1, waiting for transfers between devices, body(): partial = lax.all_to_all(partial, ('gy', 'gx_1'), 0, 0, tiled=True)  6.39 us
    all_to_all x1, waiting for transfers between devices, body(): lax.all_to_all(mass.reshape(64, 1, LANES), ('gx_0',) + PROBE, 0, 0, tiled...  6.15 us
  transfers between devices with their start and end apart: 12, of which 6 were waited for; matrix products, arithmetic and copies ran while one was open for 0% of the time, Pallas kernels for 2%

profile of v3, /device:TPU:2, one launch (start us, length us, event | category | flops | bytes accessed | tf_op | source)
XLA Modules:
  0.0 118.0 jit_solution(10210066162568380085)
XLA Ops:
  0.6 0.0 copy-start.1
  0.6 0.9 copy-done.1
  1.6 0.0 copy-start.3
  1.6 0.0 copy-start.4
  1.6 0.0 copy-start.2
  1.6 1.1 deal.1
  2.7 13.0 %all-to-all-start = ((bf16[32,120,128]{2,1,0:T(8,128)(2,1)}), bf16[32,120,128]{2,1,0:T(8,128)(2,1)}, u32[]{:S(2)}, u32[]{:S(2)}) async-start(bf16[32,120,128]{2,1,0:T(8,128)(2,1)} %deal.1), calls=%async_computation | async-start | bytes 1966080 | tf_op jit(solution)/shard_map/all_to_all | solution.py:394
  15.7 1.5 %pack.1 = (bf16[192,640]{1,0:T(8,128)(2,1)S(1)}, bf16[56,640]{1,0:T(8,128)(2,1)S(1)}) custom-call(s32[2,4,4,4,640]{4,3,2,1,0:T(4,128)} %signs_hbm.1, bf16[4,4,4,640]{3,2,1,0:T(4,128)(2,1)} %state_ref.1), custom_call_target="tpu_custom_call" | custom-call | tf_op jit(solution)/shard_map/pack/pallas_call | solution.py:356
  17.3 7.4 %collective-permute-start = (bf16[56,640]{1,0:T(8,128)(2,1)S(1)}, bf16[56,640]{1,0:T(8,128)(2,1)S(1)}, u32[]{:S(2)}, u32[]{:S(2)}) collective-permute-start(bf16[56,640]{1,0:T(8,128)(2,1)S(1)} %get-tuple-element.7), channel_id=1, source_target_pairs={{0,96},{32,64},{64,32},{96,0},{1,97},{33,65},{65,33},{97,1},{2,98}... | collective-permute-start | bytes 215048 | tf_op jit(solution)/shard_map/ppermute | solution.py:393
  24.7 20.6 %collective-permute-done = bf16[56,640]{1,0:T(8,128)(2,1)S(1)} collective-permute-done((bf16[56,640]{1,0:T(8,128)(2,1)S(1)}, bf16[56,640]{1,0:T(8,128)(2,1)S(1)}, u32[]{:S(2)}, u32[]{:S(2)}) %collective-permute-start) | collective-permute-done | bytes 71712 | tf_op jit(solution)/shard_map/ppermute | solution.py:393
  45.3 3.4 %collective-permute-start.1 = (bf16[256,640]{1,0:T(8,128)(2,1)S(1)}, bf16[256,640]{1,0:T(8,128)(2,1)S(1)}, u32[]{:S(2)}, u32[]{:S(2)}) collective-permute-start(bf16[256,640]{1,0:T(8,128)(2,1)S(1)} %pad_maximum_fusion.own0), channel_id=1, source_target_pairs={{0,128},{128,256},{256,384},{384,0},{1,129},{129,257},{257,385},{3... | collective-permute-start | bytes 983048 | tf_op jit(solution)/shard_map/ppermute | solution.py:398
  48.7 2.4 %collective-permute-start.2 = (bf16[256,640]{1,0:T(8,128)(2,1)S(1)}, bf16[256,640]{1,0:T(8,128)(2,1)S(1)}, u32[]{:S(2)}, u32[]{:S(2)}) collective-permute-start(bf16[256,640]{1,0:T(8,128)(2,1)S(1)} %pad_maximum_fusion.own0), channel_id=1, source_target_pairs={{0,384},{128,0},{256,128},{384,256},{1,385},{129,1},{257,129},{385... | collective-permute-start | bytes 983048 | tf_op jit(solution)/shard_map/ppermute | solution.py:399
  51.2 6.1 %collective-permute-done.1.own1 = bf16[256,640]{1,0:T(8,128)(2,1)S(1)} collective-permute-done((bf16[256,640]{1,0:T(8,128)(2,1)S(1)}, bf16[256,640]{1,0:T(8,128)(2,1)S(1)}, u32[]{:S(2)}, u32[]{:S(2)}) %collective-permute-start.1) | collective-permute-done | bytes 327712 | tf_op jit(solution)/shard_map/ppermute | solution.py:398
  57.2 3.1 %collective-permute-done.2.own3 = bf16[256,640]{1,0:T(8,128)(2,1)S(1)} collective-permute-done((bf16[256,640]{1,0:T(8,128)(2,1)S(1)}, bf16[256,640]{1,0:T(8,128)(2,1)S(1)}, u32[]{:S(2)}, u32[]{:S(2)}) %collective-permute-start.2) | collective-permute-done | bytes 327712 | tf_op jit(solution)/shard_map/ppermute | solution.py:399
  60.4 3.1 %collective-permute-start.3 = (bf16[256,640]{1,0:T(8,128)(2,1)S(1)}, bf16[256,640]{1,0:T(8,128)(2,1)S(1)}, u32[]{:S(2)}, u32[]{:S(2)}) collective-permute-start(bf16[256,640]{1,0:T(8,128)(2,1)S(1)} %broadcast_select_fusion), channel_id=1, source_target_pairs={{0,128},{32,416},{128,256},{160,32},{256,384},{288,160},{384,0},{4... | collective-permute-start | bytes 983048 | tf_op jit(solution)/shard_map/ppermute | solution.py:401
  63.5 1.9 %collective-permute-start.4 = (bf16[256,640]{1,0:T(8,128)(2,1)S(1)}, bf16[256,640]{1,0:T(8,128)(2,1)S(1)}, u32[]{:S(2)}, u32[]{:S(2)}) collective-permute-start(bf16[256,640]{1,0:T(8,128)(2,1)S(1)} %pad_maximum_fusion.own0), channel_id=1, source_target_pairs={{0,32},{32,0},{1,33},{33,1},{2,34},{34,2},{3,35},{35,3},{4,36},{36... | collective-permute-start | bytes 983048 | tf_op jit(solution)/shard_map/ppermute | solution.py:403
  65.5 2.4 %collective-permute-start.5 = (bf16[256,640]{1,0:T(8,128)(2,1)S(1)}, bf16[256,640]{1,0:T(8,128)(2,1)S(1)}, u32[]{:S(2)}, u32[]{:S(2)}) collective-permute-start(bf16[256,640]{1,0:T(8,128)(2,1)S(1)} %collective-permute-done.1.own1), channel_id=1, source_target_pairs={{0,32},{32,0},{1,33},{33,1},{2,34},{34,2},{3,35},{35,3},{4,36},{36... | collective-permute-start | bytes 983048 | tf_op jit(solution)/shard_map/ppermute | solution.py:403
  67.9 1.9 %collective-permute-start.6 = (bf16[256,640]{1,0:T(8,128)(2,1)S(1)}, bf16[256,640]{1,0:T(8,128)(2,1)S(1)}, u32[]{:S(2)}, u32[]{:S(2)}) collective-permute-start(bf16[256,640]{1,0:T(8,128)(2,1)S(1)} %collective-permute-done.2.own3), channel_id=1, source_target_pairs={{0,32},{32,0},{1,33},{33,1},{2,34},{34,2},{3,35},{35,3},{4,36},{36... | collective-permute-start | bytes 983048 | tf_op jit(solution)/shard_map/ppermute | solution.py:403
  69.8 0.0 collective-permute-done.3.own2
  69.8 2.4 %collective-permute-start.7 = (bf16[256,640]{1,0:T(8,128)(2,1)S(1)}, bf16[256,640]{1,0:T(8,128)(2,1)S(1)}, u32[]{:S(2)}, u32[]{:S(2)}) collective-permute-start(bf16[256,640]{1,0:T(8,128)(2,1)S(1)} %collective-permute-done.3.own2), channel_id=1, source_target_pairs={{0,32},{32,0},{1,33},{33,1},{2,34},{34,2},{3,35},{35,3},{4,36},{36... | collective-permute-start | bytes 983048 | tf_op jit(solution)/shard_map/ppermute | solution.py:403
  72.2 0.0 copy-done.3
  72.2 0.0 copy-done.4
  72.3 0.0 copy-done.2
  72.3 1.4 %lookup.1.offset_ref = f32[8,640]{1,0:T(8,128)S(1)} custom-call(s32[4]{0:T(128)S(1)} %copy-done.2, f32[1000,640]{1,0:T(8,128)} %table_hbm.1, f32[1,640]{1,0:T(1,128)S(1)} %broadcast_in_dim.10.shift_ref), custom_call_target="tpu_custom_call" | custom-call | tf_op jit(solution)/shard_map/lookup/pallas_call | solution.py:382
  73.6 0.0 copy-start.5
  73.7 0.0 copy-start
  73.7 0.0 collective-permute-done.4.other0
  73.7 0.0 collective-permute-done.5.other1
  73.7 0.0 collective-permute-done.6.other3
  73.7 0.0 collective-permute-done.7.other2
  73.7 0.0 all-to-all-done.weight_hbm
  73.7 9.7 %mix.1 = f32[8,72,128]{2,1,0:T(8,128)} custom-call(bf16[256,640]{1,0:T(8,128)(2,1)S(1)} %pad_maximum_fusion.own0, bf16[256,640]{1,0:T(8,128)(2,1)S(1)} %collective-permute-done.1.own1, bf16[256,640]{1,0:T(8,128)(2,1)S(1)} %collective-permute-done.2.own3, bf16[256,640]{1,0:T(8,128)(2,1)S(1)} %collective-permute-done.3.own2, ...), custom_call_target="tpu_custom_call" | custom-call | tf_op jit(solution)/shard_map/mix/pallas_call | solution.py:405
  83.4 5.0 %all-to-all-start.1 = ((f32[8,72,128]{2,1,0:T(8,128)}), f32[8,72,128]{2,1,0:T(8,128)S(1)}, u32[]{:S(2)}, u32[]{:S(2)}) async-start(f32[8,72,128]{2,1,0:T(8,128)} %mix.1), calls=%async_computation.1 | async-start | bytes 589824 | tf_op jit(solution)/shard_map/all_to_all | solution.py:427
  88.5 0.0 copy-done.5
  88.5 6.4 %all-to-all-done.1.parts_ref = f32[8,72,128]{2,1,0:T(8,128)S(1)} async-done(((f32[8,72,128]{2,1,0:T(8,128)}), f32[8,72,128]{2,1,0:T(8,128)S(1)}, u32[]{:S(2)}, u32[]{:S(2)}) %all-to-all-start.1) | async-done | bytes 294944 | tf_op jit(solution)/shard_map/all_to_all | solution.py:427
  94.9 0.0 copy-done
  94.9 0.7 step.1
  95.6 9.7 %all-to-all-start.2 = ((f32[64,1,128]{2,1,0:T(1,128)}), f32[64,1,128]{2,1,0:T(1,128)S(1)}, u32[]{:S(2)}, u32[]{:S(2)}) async-start(f32[64,1,128]{2,1,0:T(1,128)} %bitcast.1), calls=%async_computation.2 | async-start | bytes 65536 | tf_op jit(solution)/shard_map/all_to_all | solution.py:437
  105.3 3.5 %collective-permute-start.8 = (bf16[32,640]{1,0:T(8,128)(2,1)S(1)}, bf16[32,640]{1,0:T(8,128)(2,1)S(1)}, u32[]{:S(2)}, u32[]{:S(2)}) collective-permute-start(bf16[32,640]{1,0:T(8,128)(2,1)S(1)} %get-tuple-element.9.refs_1_), channel_id=1, source_target_pairs={{0,4},{4,0},{8,12},{12,8},{16,20},{20,16},{24,28},{28,24},{1,5},{5... | collective-permute-start | bytes 122888 | tf_op jit(solution)/shard_map/ppermute | solution.py:439
  108.8 2.4 %collective-permute-done.8.refs_2_ = bf16[32,640]{1,0:T(8,128)(2,1)S(1)} collective-permute-done((bf16[32,640]{1,0:T(8,128)(2,1)S(1)}, bf16[32,640]{1,0:T(8,128)(2,1)S(1)}, u32[]{:S(2)}, u32[]{:S(2)}) %collective-permute-start.8) | collective-permute-done | bytes 40992 | tf_op jit(solution)/shard_map/ppermute | solution.py:439
  111.2 6.2 %all-to-all-done.2 = f32[64,1,128]{2,1,0:T(1,128)S(1)} async-done(((f32[64,1,128]{2,1,0:T(1,128)}), f32[64,1,128]{2,1,0:T(1,128)S(1)}, u32[]{:S(2)}, u32[]{:S(2)}) %all-to-all-start.2) | async-done | bytes 32800 | tf_op jit(solution)/shard_map/all_to_all | solution.py:437
  117.3 0.7 final.1
  (6 shorter events, 0.1 us)
Async XLA Ops:
  0.6 1.0 copy-start.1
  1.6 70.6 %copy-start.3 = (f32[640]{0:T(1024)S(1)}, f32[640]{0:T(1024)}, u32[]{:S(2)}) copy-start(f32[640]{0:T(1024)} %param.13) | copy-start | bytes 7684
  1.6 70.7 %copy-start.4 = (f32[640]{0:T(1024)S(1)}, f32[640]{0:T(1024)}, u32[]{:S(2)}) copy-start(f32[640]{0:T(1024)} %param.12) | copy-start | bytes 7684
  1.6 70.7 %copy-start.2 = (s32[4]{0:T(128)S(1)}, s32[4]{0:T(128)}, u32[]{:S(2)}) copy-start(s32[4]{0:T(128)} %step_ref.1) | copy-start | bytes 52
  2.7 71.0 %all-to-all-start = ((bf16[32,120,128]{2,1,0:T(8,128)(2,1)}), bf16[32,120,128]{2,1,0:T(8,128)(2,1)}, u32[]{:S(2)}, u32[]{:S(2)}) async-start(bf16[32,120,128]{2,1,0:T(8,128)(2,1)} %deal.1), calls=%async_computation | async-start | bytes 1966080 | tf_op jit(solution)/shard_map/all_to_all | solution.py:394
  17.3 28.0 %collective-permute-start = (bf16[56,640]{1,0:T(8,128)(2,1)S(1)}, bf16[56,640]{1,0:T(8,128)(2,1)S(1)}, u32[]{:S(2)}, u32[]{:S(2)}) collective-permute-start(bf16[56,640]{1,0:T(8,128)(2,1)S(1)} %get-tuple-element.7), channel_id=1, source_target_pairs={{0,96},{32,64},{64,32},{96,0},{1,97},{33,65},{65,33},{97,1},{2,98}... | collective-permute-start | bytes 215048 | tf_op jit(solution)/shard_map/ppermute | solution.py:393
  45.3 11.9 %collective-permute-start.1 = (bf16[256,640]{1,0:T(8,128)(2,1)S(1)}, bf16[256,640]{1,0:T(8,128)(2,1)S(1)}, u32[]{:S(2)}, u32[]{:S(2)}) collective-permute-start(bf16[256,640]{1,0:T(8,128)(2,1)S(1)} %pad_maximum_fusion.own0), channel_id=1, source_target_pairs={{0,128},{128,256},{256,384},{384,0},{1,129},{129,257},{257,385},{3... | collective-permute-start | bytes 983048 | tf_op jit(solution)/shard_map/ppermute | solution.py:398
  48.7 11.6 %collective-permute-start.2 = (bf16[256,640]{1,0:T(8,128)(2,1)S(1)}, bf16[256,640]{1,0:T(8,128)(2,1)S(1)}, u32[]{:S(2)}, u32[]{:S(2)}) collective-permute-start(bf16[256,640]{1,0:T(8,128)(2,1)S(1)} %pad_maximum_fusion.own0), channel_id=1, source_target_pairs={{0,384},{128,0},{256,128},{384,256},{1,385},{129,1},{257,129},{385... | collective-permute-start | bytes 983048 | tf_op jit(solution)/shard_map/ppermute | solution.py:399
  60.4 9.4 %collective-permute-start.3 = (bf16[256,640]{1,0:T(8,128)(2,1)S(1)}, bf16[256,640]{1,0:T(8,128)(2,1)S(1)}, u32[]{:S(2)}, u32[]{:S(2)}) collective-permute-start(bf16[256,640]{1,0:T(8,128)(2,1)S(1)} %broadcast_select_fusion), channel_id=1, source_target_pairs={{0,128},{32,416},{128,256},{160,32},{256,384},{288,160},{384,0},{4... | collective-permute-start | bytes 983048 | tf_op jit(solution)/shard_map/ppermute | solution.py:401
  63.5 10.2 %collective-permute-start.4 = (bf16[256,640]{1,0:T(8,128)(2,1)S(1)}, bf16[256,640]{1,0:T(8,128)(2,1)S(1)}, u32[]{:S(2)}, u32[]{:S(2)}) collective-permute-start(bf16[256,640]{1,0:T(8,128)(2,1)S(1)} %pad_maximum_fusion.own0), channel_id=1, source_target_pairs={{0,32},{32,0},{1,33},{33,1},{2,34},{34,2},{3,35},{35,3},{4,36},{36... | collective-permute-start | bytes 983048 | tf_op jit(solution)/shard_map/ppermute | solution.py:403
  65.5 8.2 %collective-permute-start.5 = (bf16[256,640]{1,0:T(8,128)(2,1)S(1)}, bf16[256,640]{1,0:T(8,128)(2,1)S(1)}, u32[]{:S(2)}, u32[]{:S(2)}) collective-permute-start(bf16[256,640]{1,0:T(8,128)(2,1)S(1)} %collective-permute-done.1.own1), channel_id=1, source_target_pairs={{0,32},{32,0},{1,33},{33,1},{2,34},{34,2},{3,35},{35,3},{4,36},{36... | collective-permute-start | bytes 983048 | tf_op jit(solution)/shard_map/ppermute | solution.py:403
  67.9 5.8 %collective-permute-start.6 = (bf16[256,640]{1,0:T(8,128)(2,1)S(1)}, bf16[256,640]{1,0:T(8,128)(2,1)S(1)}, u32[]{:S(2)}, u32[]{:S(2)}) collective-permute-start(bf16[256,640]{1,0:T(8,128)(2,1)S(1)} %collective-permute-done.2.own3), channel_id=1, source_target_pairs={{0,32},{32,0},{1,33},{33,1},{2,34},{34,2},{3,35},{35,3},{4,36},{36... | collective-permute-start | bytes 983048 | tf_op jit(solution)/shard_map/ppermute | solution.py:403
  69.8 3.9 %collective-permute-start.7 = (bf16[256,640]{1,0:T(8,128)(2,1)S(1)}, bf16[256,640]{1,0:T(8,128)(2,1)S(1)}, u32[]{:S(2)}, u32[]{:S(2)}) collective-permute-start(bf16[256,640]{1,0:T(8,128)(2,1)S(1)} %collective-permute-done.3.own2), channel_id=1, source_target_pairs={{0,32},{32,0},{1,33},{33,1},{2,34},{34,2},{3,35},{35,3},{4,36},{36... | collective-permute-start | bytes 983048 | tf_op jit(solution)/shard_map/ppermute | solution.py:403
  73.6 14.8 %copy-start.5 = (f32[640]{0:T(1024)S(1)}, f32[640]{0:T(1024)}, u32[]{:S(2)}) copy-start(f32[640]{0:T(1024)} %param.15) | copy-start | bytes 7684
  73.7 21.2 %copy-start = (bf16[4,4,4,640]{3,2,1,0:T(4,128)(2,1)S(1)}, bf16[4,4,4,640]{3,2,1,0:T(4,128)(2,1)}, u32[]{:S(2)}) copy-start(bf16[4,4,4,640]{3,2,1,0:T(4,128)(2,1)} %state_ref.1) | copy-start | bytes 245764
  83.4 11.4 %all-to-all-start.1 = ((f32[8,72,128]{2,1,0:T(8,128)}), f32[8,72,128]{2,1,0:T(8,128)S(1)}, u32[]{:S(2)}, u32[]{:S(2)}) async-start(f32[8,72,128]{2,1,0:T(8,128)} %mix.1), calls=%async_computation.1 | async-start | bytes 589824 | tf_op jit(solution)/shard_map/all_to_all | solution.py:427
  95.6 21.7 %all-to-all-start.2 = ((f32[64,1,128]{2,1,0:T(1,128)}), f32[64,1,128]{2,1,0:T(1,128)S(1)}, u32[]{:S(2)}, u32[]{:S(2)}) async-start(f32[64,1,128]{2,1,0:T(1,128)} %bitcast.1), calls=%async_computation.2 | async-start | bytes 65536 | tf_op jit(solution)/shard_map/all_to_all | solution.py:437
  105.3 5.9 %collective-permute-start.8 = (bf16[32,640]{1,0:T(8,128)(2,1)S(1)}, bf16[32,640]{1,0:T(8,128)(2,1)S(1)}, u32[]{:S(2)}, u32[]{:S(2)}) collective-permute-start(bf16[32,640]{1,0:T(8,128)(2,1)S(1)} %get-tuple-element.9.refs_1_), channel_id=1, source_target_pairs={{0,4},{4,0},{8,12},{12,8},{16,20},{20,16},{24,28},{28,24},{1,5},{5... | collective-permute-start | bytes 122888 | tf_op jit(solution)/shard_map/ppermute | solution.py:439

commit v4 on v3

--- a/solution.py
+++ b/solution.py
@@ -64,7 +64,7 @@
         wsend_ref[target] = packed
 
 
-def lookup_kernel(step_ref, table_hbm, shift_ref, offset_ref, table, found):
+def lookup_kernel(step_ref, table_hbm, shift_ref, bias_ref, base_ref, offset_ref, start_ref, table, found):
     steps = [step_ref[b] for b in range(4)]
     finds = [
         pltpu.make_async_copy(
@@ -74,6 +74,7 @@
     ]
     for find in finds:
         find.start()
+    start_ref[...] = base_ref[...] + 0.25 * bias_ref[...]
     for b in range(4):
         finds[b].wait()
         line = table[b, pl.ds(lax.rem(steps[b], 8), 1), :] + shift_ref[...]
@@ -81,7 +82,7 @@
         offset_ref[b + 4 : b + 5, :] = line
 
 
-def pack_kernel(signs_hbm, state_hbm, main_ref, rim_ref, signs_ref, state_ref, uf, xf, rim, sums, arrived):
+def pack_kernel(signs_hbm, state_hbm, main_ref, rim_ref, base_ref, signs_ref, state_ref, uf, xf, rim, sums, arrived):
     blocks = uf.shape[0]
     loads = [
         pltpu.make_async_copy(src, dst, arrived.at[index])
@@ -103,6 +104,8 @@
             for o in range(blocks):
                 xf[o, pl.ds(r * 16 + b, 4, stride=4), :] = line[:, lane_block(o)]
 
+    for o in range(blocks):
+        base_ref[:, lane_block(o)] = xf[o, pl.ds(pl.multiple_of(half_rows() * 16, 8), 32), :]
     edge = jnp.where(lax.axis_index("gx_0") == 0, 3, 0)
     for o in range(blocks):
         sum_u = jnp.zeros((8, LANES), F32)
@@ -145,7 +148,7 @@
 
 def mix_kernel(
     own0, own1, own3, own2, other0, other1, other3, other2, weight_hbm, gain_ref, offset_ref,
-    out_ref, ug, xg, picked, lhs_ref, slope_ref, rows_ref, weight_ref, wf, wc, velocity, arrived,
+    out_ref, ug, xg, lhs_ref, slope_ref, rows_ref, weight_ref, wf, wc, velocity, arrived,
 ):
     load = pltpu.make_async_copy(weight_hbm, weight_ref, arrived)
     load.start()
@@ -153,11 +156,21 @@
     core = lax.axis_index("gx_1")
     half = lax.axis_index("gx_0")
     chans = own0.shape[1]
-    ug[...] = jnp.zeros(ug.shape, F32)
-    xg[...] = jnp.zeros(xg.shape, F32)
 
     def spot(row, col):
         return pl.multiple_of((row * 10 + col) * 8, 8)
+
+    def small(row, col):
+        return pl.multiple_of((row * 10 + col) * 4, 4)
+
+    for o in range(blocks):
+        for row in (0, 17):
+            ug[o, row * 80 : row * 80 + 80, :] = jnp.zeros((80, LANES), F32)
+            xg[o, row * 40 : row * 40 + 40, :] = jnp.zeros((40, LANES), F32)
+        for row in range(1, 17):
+            for col in (0, 9):
+                ug[o, row * 80 + col * 8 : row * 80 + col * 8 + 8, :] = jnp.zeros((8, LANES), F32)
+                xg[o, row * 40 + col * 4 : row * 40 + col * 4 + 4, :] = jnp.zeros((4, LANES), F32)
 
     total = jnp.zeros((8, chans), F32)
     rim_here = core == 1 - half
@@ -172,10 +185,7 @@
                 states = src[128 + r * 16 : 144 + r * 16, :].astype(F32)
                 for o in range(blocks):
                     ug[o, pl.ds(at, 32), :] = lines[:, lane_block(o)]
-                    for two in range(2):
-                        pair = doubled_rows(states[two * 8 : two * 8 + 8, lane_block(o)])
-                        xg[o, pl.ds(pl.multiple_of(at + two * 16, 8), 8), :] = pair[0]
-                        xg[o, pl.ds(pl.multiple_of(at + two * 16 + 8, 8), 8), :] = pair[1]
+                    xg[o, pl.ds(small(4 * tile + r + 1, base + 1), 16), :] = states[:, lane_block(o)]
         mine = own_ref[192:256, :].astype(F32)
         theirs = other_ref[192:256, :].astype(F32)
         total = total + mine[48:56] + mine[56:64] + theirs[48:56] + theirs[56:64]
@@ -184,12 +194,7 @@
             at = spot(4 * tile + r + 1, rim_col)
             for o in range(blocks):
                 ug[o, pl.ds(at, 8), :] = rim[r * 8 : r * 8 + 8, lane_block(o)]
-        for two in range(2):
-            for o in range(blocks):
-                pair = doubled_rows(rim[32 + two * 8 : 40 + two * 8, lane_block(o)])
-                for one in range(2):
-                    at = spot(4 * tile + two * 2 + one + 1, rim_col)
-                    xg[o, pl.ds(at, 8), :] = pair[one]
+                xg[o, pl.ds(small(4 * tile + r + 1, rim_col), 4), :] = rim[32 + r * 4 : 36 + r * 4, lane_block(o)]
 
     stats = total[:, lane_block(0)] + total[:, lane_block(1)] + total[:, lane_block(2)]
     width = chans // GROUPS
@@ -215,28 +220,37 @@
     offset = offset_ref[...]
     gain = gain_ref[...]
 
-    def fields(x, o):
+    scale = inverse * gain
+    tilt = gain * inverse
+
+    def fields(x, o, rows):
         at = lane_block(o)
-        centered = x - mean[:, at]
-        pre = centered * inverse[:, at] * gain[:, at] + offset[:, at]
+        centered = x - mean[:rows, at]
+        pre = centered * scale[:rows, at] + offset[:rows, at]
         sig = 1.0 / (1.0 + jnp.exp(-pre))
         return centered, pre, sig
 
     def grid_row(gr, carry):
         at = spot(gr + 1, 1)
+        near = small(gr + 1, 1)
+        edge = small(gr + 1, rim_col)
         for o in range(blocks):
             ln = lane_block(o)
-            x = xg[o, pl.ds(at, 64), :].reshape(8, 8, LANES)
-            u = ug[o, pl.ds(at, 64), :].reshape(8, 8, LANES)
-            centered, pre, sig = fields(x, o)
-            xg[o, pl.ds(at, 64), :] = (pre * sig).reshape(64, LANES)
-            slope = sig * (1.0 + pre * (1.0 - sig)) * gain[:, ln]
-            direction = (u - mean_u[:, ln]) * inverse[:, ln] - centered * bend[:, ln]
-            out = (slope * direction).reshape(64, LANES).astype(BF16)
-            slope_ref[pl.ds(pl.multiple_of(gr * 64, 64), 64), ln] = out
-            edge = spot(gr + 1, rim_col)
-            _, pre, sig = fields(xg[o, pl.ds(edge, 8), :], o)
-            xg[o, pl.ds(edge, 8), :] = pre * sig
+            x = xg[o, pl.ds(near, 32), :].reshape(4, 8, LANES)
+            centered, pre, sig = fields(x, o, 8)
+            xg[o, pl.ds(near, 32), :] = (pre * sig).reshape(32, LANES)
+            slope = sig * (1.0 + pre * (1.0 - sig))
+            along = slope * tilt[:, ln]
+            across = slope * gain[:, ln] * centered
+            for two in range(4):
+                spans = zip(doubled_rows(along[two]), doubled_rows(across[two]))
+                for half_cell, (first, second) in enumerate(spans):
+                    cell = two * 2 + half_cell
+                    u = ug[o, pl.ds(pl.multiple_of(at + cell * 8, 8), 8), :]
+                    out = first * (u - mean_u[:, ln]) - second * bend[:, ln]
+                    slope_ref[pl.ds(pl.multiple_of(gr * 64 + cell * 8, 8), 8), ln] = out
+            _, pre, sig = fields(xg[o, pl.ds(edge, 4), :], o, 4)
+            xg[o, pl.ds(edge, 4), :] = pre * sig
         return carry
 
     lax.fori_loop(0, 16, grid_row, 0)
@@ -253,21 +267,14 @@
 
     lax.fori_loop(0, 16, lhs_row, 0)
 
-    early = lax.broadcasted_iota(jnp.int32, (8, LANES), 0) < 4
     for index, (tap, ob) in enumerate(taps):
         dy, dx = lax.div(tap, 3), lax.rem(tap, 3)
         for target in range(8):
             for line in range(2):
-                at = spot(4 * (target // 2) + half_rows() + line + dy, 4 * (target % 2) + dx)
+                at = small(4 * (target // 2) + half_rows() + line + dy, 4 * (target % 2) + dx)
                 to = index * 256 + target * 32 + line * 16
                 for o in range(blocks):
-                    for two in range(2):
-                        first = xg[o, pl.ds(pl.multiple_of(at + two * 16, 8), 8), :]
-                        second = xg[o, pl.ds(pl.multiple_of(at + two * 16 + 8, 8), 8), :]
-                        both = jnp.where(early, first, pltpu.roll(second, 4, axis=0))
-                        picked[o, to + two * 8 : to + two * 8 + 8, :] = both
-    for o in range(blocks):
-        rows_ref[:, lane_block(o)] = picked[o].astype(BF16)
+                    rows_ref[to : to + 16, lane_block(o)] = xg[o, pl.ds(at, 16), :].astype(BF16)
 
     load.wait()
     each = weight_ref.shape[1]
@@ -282,7 +289,7 @@
         value = lax.dot_general(
             lhs_ref[start : start + chunk, :], wc[...], (((1,), (1,)), ((), ())), preferred_element_type=F32
         )
-        value = value * slope_ref[start : start + chunk, :].astype(F32)
+        value = value * slope_ref[start : start + chunk, :]
         total = total + jnp.sum(value.reshape(chunk // 8, 8, chans), axis=0)
     lanes = total[:, lane_block(0)]
     for o in range(1, blocks):
@@ -302,8 +309,8 @@
         out_ref[target, 64:72, :] = lanes
 
 
-def step_kernel(parts_ref, state_ref, bias_ref, rows_ref, mass_ref, lines):
-    blocks = bias_ref.shape[1] // LANES
+def step_kernel(parts_ref, start_ref, rows_ref, mass_ref):
+    blocks = start_ref.shape[1] // LANES
     total = parts_ref[0, 64:72, :]
     for source in range(1, 8):
         total = total + parts_ref[source, 64:72, :]
@@ -312,19 +319,14 @@
     latents = lax.broadcasted_iota(jnp.int32, (8, LANES), 0)
     line = jnp.sum(jnp.where(lane == latents, mass, 0.0), axis=0, keepdims=True)
     mass_ref[...] = jnp.broadcast_to(line, mass_ref.shape)
-    for b in range(4):
-        for r in range(2):
-            here = state_ref[b, half_rows() + r].astype(F32)
-            for o in range(blocks):
-                lines[o, pl.ds(r * 16 + b, 4, stride=4), :] = here[:, lane_block(o)]
-    velocity = [jnp.broadcast_to(bias_ref[:, lane_block(o)], (32, LANES)) for o in range(blocks)]
+    velocity = [jnp.zeros((32, LANES), F32) for _ in range(blocks)]
     for source in range(8):
         for slot in range(2):
             o = first_block(source) + slot
             if o < blocks:
                 velocity[o] = velocity[o] + parts_ref[source, slot * 32 : slot * 32 + 32, :]
     for o in range(blocks):
-        rows_ref[:, lane_block(o)] = (lines[o] + 0.25 * velocity[o]).astype(BF16)
+        rows_ref[:, lane_block(o)] = (start_ref[:, lane_block(o)] + 0.25 * velocity[o]).astype(BF16)
 
 
 def final_kernel(scale, mass_ref, rows0, rows1, next_ref, out_ref, lines):
@@ -353,11 +355,11 @@
     each = conv_weight.shape[1] * PAIRS
     params = pltpu.CompilerParams(vmem_limit_bytes=40 * 1024 * 1024)
     far = lambda array: pltpu.with_memory_space_constraint(array, pltpu.HBM)
-    main, rim = pl.pallas_call(
+    main, rim, base = pl.pallas_call(
         pack_kernel,
-        out_shape=(shape((192, chans), BF16), shape((56, chans), BF16)),
+        out_shape=(shape((192, chans), BF16), shape((56, chans), BF16), shape((32, chans), F32)),
         in_specs=[HBM] * 2,
-        out_specs=(VMEM,) * 2,
+        out_specs=(VMEM,) * 3,
         scratch_shapes=[
             pltpu.VMEM(probe_signs.shape, jnp.int32),
             pltpu.VMEM(state.shape, BF16),
@@ -379,15 +381,15 @@
         compiler_params=params,
         name="deal",
     )(conv_weight)
-    offset = pl.pallas_call(
+    offset, start = pl.pallas_call(
         lookup_kernel,
-        out_shape=shape((8, chans), F32),
-        in_specs=[SMEM, HBM, VMEM],
-        out_specs=VMEM,
+        out_shape=(shape((8, chans), F32), shape((32, chans), F32)),
+        in_specs=[SMEM, HBM, VMEM, VMEM, VMEM],
+        out_specs=(VMEM,) * 2,
         scratch_shapes=[pltpu.VMEM((4, 8, chans), F32), pltpu.SemaphoreType.DMA((4,))],
         compiler_params=params,
         name="lookup",
-    )(timesteps, far(time_table), gn_shift[None])
+    )(timesteps, far(time_table), gn_shift[None], conv_bias[None], base)
 
     across = [(a * 2 + b, (1 - a) * 2 + 1 - b) for a in range(2) for b in range(2)]
     facing = lax.ppermute(rim, GX, across)
@@ -400,7 +402,9 @@
     onward = [(x * 2 + c, (x + 1 - 2 * c) % 4 * 2 + c) for x in range(4) for c in range(2)]
     beyond = lax.ppermute(jnp.where(lax.axis_index("gx_1") == 0, above, below), ("gy", "gx_1"), onward)
     own = [block, above, below, beyond]
-    other = [lax.ppermute(tile, "gx_1", [(0, 1), (1, 0)]) for tile in own]
+    swap = [(0, 1), (1, 0)]
+    other = [lax.ppermute(block, "gx_1", swap)]
+    other += [lax.ppermute(tile, "gx_1", swap) for tile in own[1:]]
 
     partial = pl.pallas_call(
         mix_kernel,
@@ -409,10 +413,9 @@
         out_specs=VMEM,
         scratch_shapes=[
             pltpu.VMEM((blocks, 1440, LANES), F32),
-            pltpu.VMEM((blocks, 1440, LANES), F32),
-            pltpu.VMEM((blocks, PAIRS * 256, LANES), F32),
+            pltpu.VMEM((blocks, 720, LANES), F32),
             pltpu.VMEM((1024, PAIRS * LANES), BF16),
-            pltpu.VMEM((1024, chans), BF16),
+            pltpu.VMEM((1024, chans), F32),
             pltpu.VMEM((PAIRS * 256, chans), BF16),
             pltpu.VMEM((32, each, LANES), BF16),
             pltpu.VMEM((32 * each, LANES), F32),
@@ -428,15 +431,14 @@
     rows, mass = pl.pallas_call(
         step_kernel,
         out_shape=(shape((32, chans), BF16), shape((64, LANES), F32)),
-        in_specs=[VMEM] * 3,
+        in_specs=[VMEM] * 2,
         out_specs=(VMEM,) * 2,
-        scratch_shapes=[pltpu.VMEM((blocks, 32, LANES), F32)],
         compiler_params=params,
         name="step",
-    )(partial, state, conv_bias[None])
-    mass = lax.all_to_all(mass.reshape(64, 1, LANES), ("gx_0",) + PROBE, 0, 0, tiled=True)
+    )(partial, start)
     tall = lax.axis_size("probe_0")
     facing_rows = lax.ppermute(rows, "probe_0", [(y, y ^ 1) for y in range(tall)])
+    mass = lax.all_to_all(mass.reshape(64, 1, LANES), ("gx_0",) + PROBE, 0, 0, tiled=True)
     scale = -0.25 / (probe_signs.shape[0] * lax.axis_size(PROBE))
     return pl.pallas_call(
         lambda *refs: final_kernel(scale, *refs),

time: 119 us -> 118 us (level)
  the two profiles are of different devices: /device:TPU:2 before, /device:TPU:1 now
where the time goes in v4:
time: 118 us; the launch traced here: 117 us
  starting transfers between devices  54.4 us (46%)
  waiting for transfers between devices  35.4 us (30%)
  Pallas kernels  13.8 us (12%)
  blocking collectives  11.3 us (10%)
    ppermute x1, waiting for transfers between devices, body(): facing = lax.ppermute(rim, GX, across)  20.1 us
    all_to_all x1, starting transfers between devices, body(): weights = lax.all_to_all(wsend, PROBE, 0, 0, tiled=True)  13.6 us
    all_to_all x1, blocking collectives, body(): partial = lax.all_to_all(partial, ('gy', 'gx_1'), 0, 0, tiled=True)  11.3 us
    all_to_all x1, starting transfers between devices, body(): lax.all_to_all(mass.reshape(64, 1, LANES), ('gx_0',) + PROBE, 0, 0, tiled...  9.41 us
    ppermute x1, starting transfers between devices, body(): facing = lax.ppermute(rim, GX, across)  8.78 us
    pallas_call x1, Pallas kernels, body(): pl.pallas_call(mix_kernel, out_shape=shape((8, 72, LANES), F32), in_specs...  8.38 us
    ppermute x3, starting transfers between devices, body(): other += [lax.ppermute(tile, 'gx_1', swap) for tile in own[1:]]  6.73 us
    all_to_all x1, waiting for transfers between devices, body(): lax.all_to_all(mass.reshape(64, 1, LANES), ('gx_0',) + PROBE, 0, 0, tiled...  5.86 us
  transfers between devices with their start and end apart: 11, of which 5 were waited for; matrix products, arithmetic and copies ran while one was open for 0% of the time, Pallas kernels for 2%

profile of v4, /device:TPU:1, one launch (start us, length us, event | category | flops | bytes accessed | tf_op | source)
XLA Modules:
  0.0 116.9 jit_solution(2890572503865000754)
XLA Ops:
  0.6 0.0 copy-start
  0.6 0.9 copy-done
  1.6 0.0 copy-start.2
  1.6 0.0 copy-start.3
  1.6 0.0 copy-start.4
  1.6 0.0 copy-start.1
  1.6 1.1 deal.1
  2.7 13.6 %all-to-all-start = ((bf16[32,120,128]{2,1,0:T(8,128)(2,1)}), bf16[32,120,128]{2,1,0:T(8,128)(2,1)}, u32[]{:S(2)}, u32[]{:S(2)}) async-start(bf16[32,120,128]{2,1,0:T(8,128)(2,1)} %deal.1), calls=%async_computation | async-start | bytes 1966080 | tf_op jit(solution)/shard_map/all_to_all | solution.py:396
  16.3 1.5 %pack.1 = (bf16[192,640]{1,0:T(8,128)(2,1)S(1)}, bf16[56,640]{1,0:T(8,128)(2,1)S(1)}, f32[32,640]{1,0:T(8,128)S(1)}) custom-call(s32[2,4,4,4,640]{4,3,2,1,0:T(4,128)} %signs_hbm.1, bf16[4,4,4,640]{3,2,1,0:T(4,128)(2,1)} %state_hbm.1), custom_call_target="tpu_custom_call" | custom-call | tf_op jit(solution)/shard_map/pack/pallas_call | solution.py:358
  17.8 8.8 %collective-permute-start = (bf16[56,640]{1,0:T(8,128)(2,1)S(1)}, bf16[56,640]{1,0:T(8,128)(2,1)S(1)}, u32[]{:S(2)}, u32[]{:S(2)}) collective-permute-start(bf16[56,640]{1,0:T(8,128)(2,1)S(1)} %get-tuple-element.10), channel_id=1, source_target_pairs={{0,96},{32,64},{64,32},{96,0},{1,97},{33,65},{65,33},{97,1},{2,98}... | collective-permute-start | bytes 215048 | tf_op jit(solution)/shard_map/ppermute | solution.py:395
  26.6 20.1 %collective-permute-done = bf16[56,640]{1,0:T(8,128)(2,1)S(1)} collective-permute-done((bf16[56,640]{1,0:T(8,128)(2,1)S(1)}, bf16[56,640]{1,0:T(8,128)(2,1)S(1)}, u32[]{:S(2)}, u32[]{:S(2)}) %collective-permute-start) | collective-permute-done | bytes 71712 | tf_op jit(solution)/shard_map/ppermute | solution.py:395
  46.7 3.1 %collective-permute-start.1 = (bf16[256,640]{1,0:T(8,128)(2,1)S(1)}, bf16[256,640]{1,0:T(8,128)(2,1)S(1)}, u32[]{:S(2)}, u32[]{:S(2)}) collective-permute-start(bf16[256,640]{1,0:T(8,128)(2,1)S(1)} %pad_maximum_fusion.own0), channel_id=1, source_target_pairs={{0,128},{128,256},{256,384},{384,0},{1,129},{129,257},{257,385},{3... | collective-permute-start | bytes 983048 | tf_op jit(solution)/shard_map/ppermute | solution.py:400
  49.9 3.4 %collective-permute-start.2 = (bf16[256,640]{1,0:T(8,128)(2,1)S(1)}, bf16[256,640]{1,0:T(8,128)(2,1)S(1)}, u32[]{:S(2)}, u32[]{:S(2)}) collective-permute-start(bf16[256,640]{1,0:T(8,128)(2,1)S(1)} %pad_maximum_fusion.own0), channel_id=1, source_target_pairs={{0,384},{128,0},{256,128},{384,256},{1,385},{129,1},{257,129},{385... | collective-permute-start | bytes 983048 | tf_op jit(solution)/shard_map/ppermute | solution.py:401
  53.2 5.7 %collective-permute-done.1.own1 = bf16[256,640]{1,0:T(8,128)(2,1)S(1)} collective-permute-done((bf16[256,640]{1,0:T(8,128)(2,1)S(1)}, bf16[256,640]{1,0:T(8,128)(2,1)S(1)}, u32[]{:S(2)}, u32[]{:S(2)}) %collective-permute-start.1) | collective-permute-done | bytes 327712 | tf_op jit(solution)/shard_map/ppermute | solution.py:400
  59.0 1.6 %collective-permute-done.2.own3 = bf16[256,640]{1,0:T(8,128)(2,1)S(1)} collective-permute-done((bf16[256,640]{1,0:T(8,128)(2,1)S(1)}, bf16[256,640]{1,0:T(8,128)(2,1)S(1)}, u32[]{:S(2)}, u32[]{:S(2)}) %collective-permute-start.2) | collective-permute-done | bytes 327712 | tf_op jit(solution)/shard_map/ppermute | solution.py:401
  60.7 4.6 %collective-permute-start.3 = (bf16[256,640]{1,0:T(8,128)(2,1)S(1)}, bf16[256,640]{1,0:T(8,128)(2,1)S(1)}, u32[]{:S(2)}, u32[]{:S(2)}) collective-permute-start(bf16[256,640]{1,0:T(8,128)(2,1)S(1)} %broadcast_select_fusion), channel_id=1, source_target_pairs={{0,128},{32,416},{128,256},{160,32},{256,384},{288,160},{384,0},{4... | collective-permute-start | bytes 983048 | tf_op jit(solution)/shard_map/ppermute | solution.py:403
  65.3 2.0 %collective-permute-start.4 = (bf16[256,640]{1,0:T(8,128)(2,1)S(1)}, bf16[256,640]{1,0:T(8,128)(2,1)S(1)}, u32[]{:S(2)}, u32[]{:S(2)}) collective-permute-start(bf16[256,640]{1,0:T(8,128)(2,1)S(1)} %pad_maximum_fusion.own0), channel_id=1, source_target_pairs={{0,32},{32,0},{1,33},{33,1},{2,34},{34,2},{3,35},{35,3},{4,36},{36... | collective-permute-start | bytes 983048 | tf_op jit(solution)/shard_map/ppermute | solution.py:406
  67.2 2.4 %collective-permute-start.5 = (bf16[256,640]{1,0:T(8,128)(2,1)S(1)}, bf16[256,640]{1,0:T(8,128)(2,1)S(1)}, u32[]{:S(2)}, u32[]{:S(2)}) collective-permute-start(bf16[256,640]{1,0:T(8,128)(2,1)S(1)} %collective-permute-done.1.own1), channel_id=1, source_target_pairs={{0,32},{32,0},{1,33},{33,1},{2,34},{34,2},{3,35},{35,3},{4,36},{36... | collective-permute-start | bytes 983048 | tf_op jit(solution)/shard_map/ppermute | solution.py:407
  69.6 2.0 %collective-permute-start.6 = (bf16[256,640]{1,0:T(8,128)(2,1)S(1)}, bf16[256,640]{1,0:T(8,128)(2,1)S(1)}, u32[]{:S(2)}, u32[]{:S(2)}) collective-permute-start(bf16[256,640]{1,0:T(8,128)(2,1)S(1)} %collective-permute-done.2.own3), channel_id=1, source_target_pairs={{0,32},{32,0},{1,33},{33,1},{2,34},{34,2},{3,35},{35,3},{4,36},{36... | collective-permute-start | bytes 983048 | tf_op jit(solution)/shard_map/ppermute | solution.py:407
  71.6 0.0 collective-permute-done.3.own2
  71.6 2.4 %collective-permute-start.7 = (bf16[256,640]{1,0:T(8,128)(2,1)S(1)}, bf16[256,640]{1,0:T(8,128)(2,1)S(1)}, u32[]{:S(2)}, u32[]{:S(2)}) collective-permute-start(bf16[256,640]{1,0:T(8,128)(2,1)S(1)} %collective-permute-done.3.own2), channel_id=1, source_target_pairs={{0,32},{32,0},{1,33},{33,1},{2,34},{34,2},{3,35},{35,3},{4,36},{36... | collective-permute-start | bytes 983048 | tf_op jit(solution)/shard_map/ppermute | solution.py:407
  74.0 0.0 copy-done.2
  74.0 0.0 copy-done.3
  74.0 0.0 copy-done.4
  74.1 0.0 copy-done.1
  74.1 1.4 %lookup.1 = (f32[8,640]{1,0:T(8,128)S(1)}, f32[32,640]{1,0:T(8,128)S(1)}) custom-call(s32[4]{0:T(128)S(1)} %copy-done.1, f32[1000,640]{1,0:T(8,128)} %table_hbm.1, f32[1,640]{1,0:T(1,128)S(1)} %broadcast_in_dim.10.shift_ref, f32[1,640]{1,0:T(1,128)S(1)} %broadcast_in_dim.11.bias_ref, f32[32,640]{1,0:T(8,128)S(1)} %get-tuple-element.11.base_ref), custom_call_target="tpu_custom_call" | custom-call | tf_op jit(solution)/shard_map/lookup/pallas_call | solution.py:384
  75.5 0.0 collective-permute-done.4.other0
  75.5 0.0 collective-permute-done.5.other1
  75.5 0.0 collective-permute-done.6.other3
  75.5 0.0 collective-permute-done.7.other2
  75.5 0.0 all-to-all-done.weight_hbm
  75.5 8.4 %mix.1 = f32[8,72,128]{2,1,0:T(8,128)S(1)} custom-call(bf16[256,640]{1,0:T(8,128)(2,1)S(1)} %pad_maximum_fusion.own0, bf16[256,640]{1,0:T(8,128)(2,1)S(1)} %collective-permute-done.1.own1, bf16[256,640]{1,0:T(8,128)(2,1)S(1)} %collective-permute-done.2.own3, bf16[256,640]{1,0:T(8,128)(2,1)S(1)} %collective-permute-done.3.own2, ...), custom_call_target="tpu_custom_call" | custom-call | tf_op jit(solution)/shard_map/mix/pallas_call | solution.py:409
  83.9 11.3 %all_to_all.15.parts_ref = f32[8,72,128]{2,1,0:T(8,128)S(1)} all-to-all(f32[8,72,128]{2,1,0:T(8,128)S(1)} %mix.1), channel_id=1, replica_groups=mesh['gy'=4,'gx_0'=2,'gx_1'=2,'probe_0'=8,'probe_1'=4] {'gy','gx_1'}, dimensions={0} | all-to-all | bytes 589824 | tf_op jit(solution)/shard_map/all_to_all | solution.py:430
  95.2 0.7 step.1
  95.9 9.4 %all-to-all-start.2 = ((f32[64,1,128]{2,1,0:T(1,128)}), f32[64,1,128]{2,1,0:T(1,128)S(1)}, u32[]{:S(2)}, u32[]{:S(2)}) async-start(f32[64,1,128]{2,1,0:T(1,128)} %bitcast.1), calls=%async_computation.2 | async-start | bytes 65536 | tf_op jit(solution)/shard_map/all_to_all | solution.py:441
  105.3 2.9 %collective-permute-start.8 = (bf16[32,640]{1,0:T(8,128)(2,1)S(1)}, bf16[32,640]{1,0:T(8,128)(2,1)S(1)}, u32[]{:S(2)}, u32[]{:S(2)}) collective-permute-start(bf16[32,640]{1,0:T(8,128)(2,1)S(1)} %get-tuple-element.15.refs_1_), channel_id=1, source_target_pairs={{0,4},{4,0},{8,12},{12,8},{16,20},{20,16},{24,28},{28,24},{1,5},{5... | collective-permute-start | bytes 122888 | tf_op jit(solution)/shard_map/ppermute | solution.py:440
  108.3 2.1 %collective-permute-done.8.refs_2_ = bf16[32,640]{1,0:T(8,128)(2,1)S(1)} collective-permute-done((bf16[32,640]{1,0:T(8,128)(2,1)S(1)}, bf16[32,640]{1,0:T(8,128)(2,1)S(1)}, u32[]{:S(2)}, u32[]{:S(2)}) %collective-permute-start.8) | collective-permute-done | bytes 40992 | tf_op jit(solution)/shard_map/ppermute | solution.py:440
  110.4 5.9 %all-to-all-done.2 = f32[64,1,128]{2,1,0:T(1,128)S(1)} async-done(((f32[64,1,128]{2,1,0:T(1,128)}), f32[64,1,128]{2,1,0:T(1,128)S(1)}, u32[]{:S(2)}, u32[]{:S(2)}) %all-to-all-start.2) | async-done | bytes 32800 | tf_op jit(solution)/shard_map/all_to_all | solution.py:441
  116.2 0.7 final.1
  (6 shorter events, 0.1 us)
Async XLA Ops:
  0.6 1.0 copy-start
  1.6 72.4 %copy-start.2 = (f32[640]{0:T(1024)S(1)}, f32[640]{0:T(1024)}, u32[]{:S(2)}) copy-start(f32[640]{0:T(1024)} %param.12) | copy-start | bytes 7684
  1.6 72.4 %copy-start.3 = (f32[640]{0:T(1024)S(1)}, f32[640]{0:T(1024)}, u32[]{:S(2)}) copy-start(f32[640]{0:T(1024)} %param.13) | copy-start | bytes 7684
  1.6 72.5 %copy-start.4 = (f32[640]{0:T(1024)S(1)}, f32[640]{0:T(1024)}, u32[]{:S(2)}) copy-start(f32[640]{0:T(1024)} %param.15) | copy-start | bytes 7684
  1.6 72.5 %copy-start.1 = (s32[4]{0:T(128)S(1)}, s32[4]{0:T(128)}, u32[]{:S(2)}) copy-start(s32[4]{0:T(128)} %step_ref.1) | copy-start | bytes 52
  2.7 72.8 %all-to-all-start = ((bf16[32,120,128]{2,1,0:T(8,128)(2,1)}), bf16[32,120,128]{2,1,0:T(8,128)(2,1)}, u32[]{:S(2)}, u32[]{:S(2)}) async-start(bf16[32,120,128]{2,1,0:T(8,128)(2,1)} %deal.1), calls=%async_computation | async-start | bytes 1966080 | tf_op jit(solution)/shard_map/all_to_all | solution.py:396
  17.8 28.9 %collective-permute-start = (bf16[56,640]{1,0:T(8,128)(2,1)S(1)}, bf16[56,640]{1,0:T(8,128)(2,1)S(1)}, u32[]{:S(2)}, u32[]{:S(2)}) collective-permute-start(bf16[56,640]{1,0:T(8,128)(2,1)S(1)} %get-tuple-element.10), channel_id=1, source_target_pairs={{0,96},{32,64},{64,32},{96,0},{1,97},{33,65},{65,33},{97,1},{2,98}... | collective-permute-start | bytes 215048 | tf_op jit(solution)/shard_map/ppermute | solution.py:395
  46.7 12.3 %collective-permute-start.1 = (bf16[256,640]{1,0:T(8,128)(2,1)S(1)}, bf16[256,640]{1,0:T(8,128)(2,1)S(1)}, u32[]{:S(2)}, u32[]{:S(2)}) collective-permute-start(bf16[256,640]{1,0:T(8,128)(2,1)S(1)} %pad_maximum_fusion.own0), channel_id=1, source_target_pairs={{0,128},{128,256},{256,384},{384,0},{1,129},{129,257},{257,385},{3... | collective-permute-start | bytes 983048 | tf_op jit(solution)/shard_map/ppermute | solution.py:400
  49.9 10.8 %collective-permute-start.2 = (bf16[256,640]{1,0:T(8,128)(2,1)S(1)}, bf16[256,640]{1,0:T(8,128)(2,1)S(1)}, u32[]{:S(2)}, u32[]{:S(2)}) collective-permute-start(bf16[256,640]{1,0:T(8,128)(2,1)S(1)} %pad_maximum_fusion.own0), channel_id=1, source_target_pairs={{0,384},{128,0},{256,128},{384,256},{1,385},{129,1},{257,129},{385... | collective-permute-start | bytes 983048 | tf_op jit(solution)/shard_map/ppermute | solution.py:401
  60.7 10.9 %collective-permute-start.3 = (bf16[256,640]{1,0:T(8,128)(2,1)S(1)}, bf16[256,640]{1,0:T(8,128)(2,1)S(1)}, u32[]{:S(2)}, u32[]{:S(2)}) collective-permute-start(bf16[256,640]{1,0:T(8,128)(2,1)S(1)} %broadcast_select_fusion), channel_id=1, source_target_pairs={{0,128},{32,416},{128,256},{160,32},{256,384},{288,160},{384,0},{4... | collective-permute-start | bytes 983048 | tf_op jit(solution)/shard_map/ppermute | solution.py:403
  65.3 10.2 %collective-permute-start.4 = (bf16[256,640]{1,0:T(8,128)(2,1)S(1)}, bf16[256,640]{1,0:T(8,128)(2,1)S(1)}, u32[]{:S(2)}, u32[]{:S(2)}) collective-permute-start(bf16[256,640]{1,0:T(8,128)(2,1)S(1)} %pad_maximum_fusion.own0), channel_id=1, source_target_pairs={{0,32},{32,0},{1,33},{33,1},{2,34},{34,2},{3,35},{35,3},{4,36},{36... | collective-permute-start | bytes 983048 | tf_op jit(solution)/shard_map/ppermute | solution.py:406
  67.2 8.2 %collective-permute-start.5 = (bf16[256,640]{1,0:T(8,128)(2,1)S(1)}, bf16[256,640]{1,0:T(8,128)(2,1)S(1)}, u32[]{:S(2)}, u32[]{:S(2)}) collective-permute-start(bf16[256,640]{1,0:T(8,128)(2,1)S(1)} %collective-permute-done.1.own1), channel_id=1, source_target_pairs={{0,32},{32,0},{1,33},{33,1},{2,34},{34,2},{3,35},{35,3},{4,36},{36... | collective-permute-start | bytes 983048 | tf_op jit(solution)/shard_map/ppermute | solution.py:407
  69.6 5.9 %collective-permute-start.6 = (bf16[256,640]{1,0:T(8,128)(2,1)S(1)}, bf16[256,640]{1,0:T(8,128)(2,1)S(1)}, u32[]{:S(2)}, u32[]{:S(2)}) collective-permute-start(bf16[256,640]{1,0:T(8,128)(2,1)S(1)} %collective-permute-done.2.own3), channel_id=1, source_target_pairs={{0,32},{32,0},{1,33},{33,1},{2,34},{34,2},{3,35},{35,3},{4,36},{36... | collective-permute-start | bytes 983048 | tf_op jit(solution)/shard_map/ppermute | solution.py:407
  71.6 3.9 %collective-permute-start.7 = (bf16[256,640]{1,0:T(8,128)(2,1)S(1)}, bf16[256,640]{1,0:T(8,128)(2,1)S(1)}, u32[]{:S(2)}, u32[]{:S(2)}) collective-permute-start(bf16[256,640]{1,0:T(8,128)(2,1)S(1)} %collective-permute-done.3.own2), channel_id=1, source_target_pairs={{0,32},{32,0},{1,33},{33,1},{2,34},{34,2},{3,35},{35,3},{4,36},{36... | collective-permute-start | bytes 983048 | tf_op jit(solution)/shard_map/ppermute | solution.py:407
  95.9 20.3 %all-to-all-start.2 = ((f32[64,1,128]{2,1,0:T(1,128)}), f32[64,1,128]{2,1,0:T(1,128)S(1)}, u32[]{:S(2)}, u32[]{:S(2)}) async-start(f32[64,1,128]{2,1,0:T(1,128)} %bitcast.1), calls=%async_computation.2 | async-start | bytes 65536 | tf_op jit(solution)/shard_map/all_to_all | solution.py:441
  105.3 5.0 %collective-permute-start.8 = (bf16[32,640]{1,0:T(8,128)(2,1)S(1)}, bf16[32,640]{1,0:T(8,128)(2,1)S(1)}, u32[]{:S(2)}, u32[]{:S(2)}) collective-permute-start(bf16[32,640]{1,0:T(8,128)(2,1)S(1)} %get-tuple-element.15.refs_1_), channel_id=1, source_target_pairs={{0,4},{4,0},{8,12},{12,8},{16,20},{20,16},{24,28},{28,24},{1,5},{5... | collective-permute-start | bytes 122888 | tf_op jit(solution)/shard_map/ppermute | solution.py:440

commit v5 on v4

--- a/solution.py
+++ b/solution.py
@@ -248,7 +248,7 @@
                     cell = two * 2 + half_cell
                     u = ug[o, pl.ds(pl.multiple_of(at + cell * 8, 8), 8), :]
                     out = first * (u - mean_u[:, ln]) - second * bend[:, ln]
-                    slope_ref[pl.ds(pl.multiple_of(gr * 64 + cell * 8, 8), 8), ln] = out
+                    slope_ref[pl.ds(pl.multiple_of(gr * 64 + cell * 8, 8), 8), ln] = out.astype(BF16).astype(F32)
             _, pre, sig = fields(xg[o, pl.ds(edge, 4), :], o, 4)
             xg[o, pl.ds(edge, 4), :] = pre * sig
         return carry
@@ -329,12 +329,15 @@
         rows_ref[:, lane_block(o)] = (start_ref[:, lane_block(o)] + 0.25 * velocity[o]).astype(BF16)
 
 
-def final_kernel(scale, mass_ref, rows0, rows1, next_ref, out_ref, lines):
-    blocks = lines.shape[0]
+def tally_kernel(scale, mass_ref, out_ref):
     total = jnp.sum(mass_ref[...], axis=0, keepdims=True)
     lane = lax.broadcasted_iota(jnp.int32, (1, LANES), 1)
     for b in range(4):
         out_ref[b] = scale * jnp.sum(jnp.where(lane == b, total, 0.0))
+
+
+def final_kernel(rows0, rows1, next_ref, lines):
+    blocks = lines.shape[0]
     for start, rows in ((half_rows(), rows0), (2 - half_rows(), rows1)):
         for o in range(blocks):
             lines[o] = rows[:, lane_block(o)].astype(F32)
@@ -391,10 +394,10 @@
         name="lookup",
     )(timesteps, far(time_table), gn_shift[None], conv_bias[None], base)
 
-    across = [(a * 2 + b, (1 - a) * 2 + 1 - b) for a in range(2) for b in range(2)]
-    facing = lax.ppermute(rim, GX, across)
+    facing = lax.ppermute(rim, GX, [(1, 2), (2, 1)])
+    outer = lax.ppermute(rim[48:56], GX, [(0, 3), (3, 0)])
     weights = lax.all_to_all(wsend, PROBE, 0, 0, tiled=True)
-    block = jnp.concatenate([main, facing, rim[48:56]], axis=0)
+    block = jnp.concatenate([main, facing[:48], facing[48:] + outer, rim[48:56]], axis=0)
     down = [(i, (i + 1) % 4) for i in range(4)]
     up = [(i, (i + 3) % 4) for i in range(4)]
     above = lax.ppermute(block, "gy", down)
@@ -440,15 +443,24 @@
     facing_rows = lax.ppermute(rows, "probe_0", [(y, y ^ 1) for y in range(tall)])
     mass = lax.all_to_all(mass.reshape(64, 1, LANES), ("gx_0",) + PROBE, 0, 0, tiled=True)
     scale = -0.25 / (probe_signs.shape[0] * lax.axis_size(PROBE))
-    return pl.pallas_call(
-        lambda *refs: final_kernel(scale, *refs),
-        out_shape=(shape(state.shape, BF16), shape((4,), F32)),
-        in_specs=[VMEM] * 3,
-        out_specs=(VMEM, SMEM),
+    total = pl.pallas_call(
+        lambda *refs: tally_kernel(scale, *refs),
+        out_shape=shape((4,), F32),
+        in_specs=[VMEM],
+        out_specs=SMEM,
+        compiler_params=params,
+        name="tally",
+    )(mass.reshape(64, LANES))
+    following = pl.pallas_call(
+        final_kernel,
+        out_shape=shape(state.shape, BF16),
+        in_specs=[VMEM] * 2,
+        out_specs=VMEM,
         scratch_shapes=[pltpu.VMEM((blocks, 32, LANES), F32)],
         compiler_params=params,
         name="final",
-    )(mass.reshape(64, LANES), rows, facing_rows)
+    )(rows, facing_rows)
+    return following, total
 
 
 def solution(mesh):

time: 118 us -> 114 us (0.966)
  waiting for transfers between devices: 35.4 us -> 28.9 us
  starting transfers between devices: 54.4 us -> 58.3 us
  blocking collectives: 11.3 us -> 9.77 us
    all_to_all x1, starting transfers between devices: 9.41 us -> 13.8 us  [body(): lax.all_to_all(mass.reshape(64, 1, LANES), ('gx_0',) + PROBE, 0, 0, tiled...]
    ppermute x1 -> x2, waiting for transfers between devices: 20.1 us -> 15.9 us  [the longest x1 15.9 us: body(): facing = lax.ppermute(rim, GX, [(1, 2), (2, 1)])]
    ppermute x1, waiting for transfers between devices: 1.64 us -> 0.01 us  [body(): below = lax.ppermute(block, 'gy', up)]
    all_to_all x1, blocking collectives: 11.3 us -> 9.77 us  [body(): partial = lax.all_to_all(partial, ('gy', 'gx_1'), 0, 0, tiled=True)]
    ppermute x1 -> x2, starting transfers between devices: 8.78 us -> 9.44 us  [the longest x1 8.78 us: body(): facing = lax.ppermute(rim, GX, [(1, 2), (2, 1)])]
  transfers between devices with their start and end apart: 11 -> 12, of which waited for: 5 -> 4; matrix products, arithmetic and copies ran while one was open for 0% -> 0% of each run, Pallas kernels for 2% -> 3%
where the time goes in v5:
time: 114 us; the launch traced here: 113 us
  starting transfers between devices  58.3 us (51%)
  waiting for transfers between devices  28.9 us (25%)
  Pallas kernels  14.5 us (13%)
  blocking collectives  9.77 us (9%)
    ppermute x1, waiting for transfers between devices, body(): facing = lax.ppermute(rim, GX, [(1, 2), (2, 1)])  15.9 us
    all_to_all x1, starting transfers between devices, body(): lax.all_to_all(mass.reshape(64, 1, LANES), ('gx_0',) + PROBE, 0, 0, tiled...  13.8 us
    all_to_all x1, starting transfers between devices, body(): weights = lax.all_to_all(wsend, PROBE, 0, 0, tiled=True)  13.6 us
    all_to_all x1, blocking collectives, body(): partial = lax.all_to_all(partial, ('gy', 'gx_1'), 0, 0, tiled=True)  9.77 us
    ppermute x1, starting transfers between devices, body(): facing = lax.ppermute(rim, GX, [(1, 2), (2, 1)])  8.78 us
    pallas_call x1, Pallas kernels, body(): pl.pallas_call(mix_kernel, out_shape=shape((8, 72, LANES), F32), in_specs...  8.45 us
    ppermute x3, starting transfers between devices, body(): other += [lax.ppermute(tile, 'gx_1', swap) for tile in own[1:]]  6.73 us
    ppermute x1, waiting for transfers between devices, body(): above = lax.ppermute(block, 'gy', down)  5.6 us
  transfers between devices with their start and end apart: 12, of which 4 were waited for; matrix products, arithmetic and copies ran while one was open for 0% of the time, Pallas kernels for 3%

profile of v5, /device:TPU:1, one launch (start us, length us, event | category | flops | bytes accessed | tf_op | source)
XLA Modules:
  0.0 113.4 jit_solution(5598164698370069192)
XLA Ops:
  0.6 0.0 copy-start
  0.6 0.9 copy-done
  1.6 0.0 copy-start.2
  1.6 0.0 copy-start.3
  1.6 0.0 copy-start.4
  1.6 0.0 copy-start.1
  1.6 1.1 deal.1
  2.7 13.6 %all-to-all-start = ((bf16[32,120,128]{2,1,0:T(8,128)(2,1)}), bf16[32,120,128]{2,1,0:T(8,128)(2,1)}, u32[]{:S(2)}, u32[]{:S(2)}) async-start(bf16[32,120,128]{2,1,0:T(8,128)(2,1)} %deal.1), calls=%async_computation | async-start | bytes 1966080 | tf_op jit(solution)/shard_map/all_to_all | solution.py:399
  16.3 1.5 %pack.1 = (bf16[192,640]{1,0:T(8,128)(2,1)S(1)}, bf16[56,640]{1,0:T(8,128)(2,1)S(1)}, f32[32,640]{1,0:T(8,128)S(1)}) custom-call(s32[2,4,4,4,640]{4,3,2,1,0:T(4,128)} %signs_hbm.1, bf16[4,4,4,640]{3,2,1,0:T(4,128)(2,1)} %state_hbm.1), custom_call_target="tpu_custom_call" | custom-call | tf_op jit(solution)/shard_map/pack/pallas_call | solution.py:361
  17.8 8.8 %collective-permute-start = (bf16[56,640]{1,0:T(8,128)(2,1)S(1)}, bf16[56,640]{1,0:T(8,128)(2,1)S(1)}, u32[]{:S(2)}, u32[]{:S(2)}) collective-permute-start(bf16[56,640]{1,0:T(8,128)(2,1)S(1)} %get-tuple-element.10), channel_id=1, source_target_pairs={{32,64},{64,32},{33,65},{65,33},{34,66},{66,34},{35,67},{67,35},{3... | collective-permute-start | bytes 215048 | tf_op jit(solution)/shard_map/ppermute | solution.py:397
  26.6 0.7 collective-permute-start.1
  27.3 15.9 %collective-permute-done = bf16[56,640]{1,0:T(8,128)(2,1)S(1)} collective-permute-done((bf16[56,640]{1,0:T(8,128)(2,1)S(1)}, bf16[56,640]{1,0:T(8,128)(2,1)S(1)}, u32[]{:S(2)}, u32[]{:S(2)}) %collective-permute-start) | collective-permute-done | bytes 71712 | tf_op jit(solution)/shard_map/ppermute | solution.py:397
  43.2 0.0 collective-permute-done.1
  43.3 3.1 %collective-permute-start.2 = (bf16[256,640]{1,0:T(8,128)(2,1)S(1)}, bf16[256,640]{1,0:T(8,128)(2,1)S(1)}, u32[]{:S(2)}, u32[]{:S(2)}) collective-permute-start(bf16[256,640]{1,0:T(8,128)(2,1)S(1)} %pad_maximum_fusion.own0), channel_id=1, source_target_pairs={{0,128},{128,256},{256,384},{384,0},{1,129},{129,257},{257,385},{3... | collective-permute-start | bytes 983048 | tf_op jit(solution)/shard_map/ppermute | solution.py:403
  46.4 3.4 %collective-permute-start.3 = (bf16[256,640]{1,0:T(8,128)(2,1)S(1)}, bf16[256,640]{1,0:T(8,128)(2,1)S(1)}, u32[]{:S(2)}, u32[]{:S(2)}) collective-permute-start(bf16[256,640]{1,0:T(8,128)(2,1)S(1)} %pad_maximum_fusion.own0), channel_id=1, source_target_pairs={{0,384},{128,0},{256,128},{384,256},{1,385},{129,1},{257,129},{385... | collective-permute-start | bytes 983048 | tf_op jit(solution)/shard_map/ppermute | solution.py:404
  49.8 5.6 %collective-permute-done.2.own1 = bf16[256,640]{1,0:T(8,128)(2,1)S(1)} collective-permute-done((bf16[256,640]{1,0:T(8,128)(2,1)S(1)}, bf16[256,640]{1,0:T(8,128)(2,1)S(1)}, u32[]{:S(2)}, u32[]{:S(2)}) %collective-permute-start.2) | collective-permute-done | bytes 327712 | tf_op jit(solution)/shard_map/ppermute | solution.py:403
  55.4 0.0 collective-permute-done.3.own3
  55.5 3.4 %collective-permute-start.4 = (bf16[256,640]{1,0:T(8,128)(2,1)S(1)}, bf16[256,640]{1,0:T(8,128)(2,1)S(1)}, u32[]{:S(2)}, u32[]{:S(2)}) collective-permute-start(bf16[256,640]{1,0:T(8,128)(2,1)S(1)} %broadcast_select_fusion), channel_id=1, source_target_pairs={{0,128},{32,416},{128,256},{160,32},{256,384},{288,160},{384,0},{4... | collective-permute-start | bytes 983048 | tf_op jit(solution)/shard_map/ppermute | solution.py:406
  58.9 1.9 %collective-permute-start.5 = (bf16[256,640]{1,0:T(8,128)(2,1)S(1)}, bf16[256,640]{1,0:T(8,128)(2,1)S(1)}, u32[]{:S(2)}, u32[]{:S(2)}) collective-permute-start(bf16[256,640]{1,0:T(8,128)(2,1)S(1)} %pad_maximum_fusion.own0), channel_id=1, source_target_pairs={{0,32},{32,0},{1,33},{33,1},{2,34},{34,2},{3,35},{35,3},{4,36},{36... | collective-permute-start | bytes 983048 | tf_op jit(solution)/shard_map/ppermute | solution.py:409
  60.8 2.4 %collective-permute-start.6 = (bf16[256,640]{1,0:T(8,128)(2,1)S(1)}, bf16[256,640]{1,0:T(8,128)(2,1)S(1)}, u32[]{:S(2)}, u32[]{:S(2)}) collective-permute-start(bf16[256,640]{1,0:T(8,128)(2,1)S(1)} %collective-permute-done.2.own1), channel_id=1, source_target_pairs={{0,32},{32,0},{1,33},{33,1},{2,34},{34,2},{3,35},{35,3},{4,36},{36... | collective-permute-start | bytes 983048 | tf_op jit(solution)/shard_map/ppermute | solution.py:410
  63.2 1.9 %collective-permute-start.7 = (bf16[256,640]{1,0:T(8,128)(2,1)S(1)}, bf16[256,640]{1,0:T(8,128)(2,1)S(1)}, u32[]{:S(2)}, u32[]{:S(2)}) collective-permute-start(bf16[256,640]{1,0:T(8,128)(2,1)S(1)} %collective-permute-done.3.own3), channel_id=1, source_target_pairs={{0,32},{32,0},{1,33},{33,1},{2,34},{34,2},{3,35},{35,3},{4,36},{36... | collective-permute-start | bytes 983048 | tf_op jit(solution)/shard_map/ppermute | solution.py:410
  65.2 0.0 collective-permute-done.4.own2
  65.2 2.4 %collective-permute-start.8 = (bf16[256,640]{1,0:T(8,128)(2,1)S(1)}, bf16[256,640]{1,0:T(8,128)(2,1)S(1)}, u32[]{:S(2)}, u32[]{:S(2)}) collective-permute-start(bf16[256,640]{1,0:T(8,128)(2,1)S(1)} %collective-permute-done.4.own2), channel_id=1, source_target_pairs={{0,32},{32,0},{1,33},{33,1},{2,34},{34,2},{3,35},{35,3},{4,36},{36... | collective-permute-start | bytes 983048 | tf_op jit(solution)/shard_map/ppermute | solution.py:410
  67.6 0.0 copy-done.2
  67.6 0.0 copy-done.3
  67.6 0.0 copy-done.4
  67.7 0.0 copy-done.1
  67.7 1.4 %lookup.1 = (f32[8,640]{1,0:T(8,128)S(1)}, f32[32,640]{1,0:T(8,128)S(1)}) custom-call(s32[4]{0:T(128)S(1)} %copy-done.1, f32[1000,640]{1,0:T(8,128)} %table_hbm.1, f32[1,640]{1,0:T(1,128)S(1)} %broadcast_in_dim.10.shift_ref, f32[1,640]{1,0:T(1,128)S(1)} %broadcast_in_dim.11.bias_ref, f32[32,640]{1,0:T(8,128)S(1)} %get-tuple-element.11.base_ref), custom_call_target="tpu_custom_call" | custom-call | tf_op jit(solution)/shard_map/lookup/pallas_call | solution.py:387
  69.0 0.0 collective-permute-done.5.other0
  69.1 0.0 collective-permute-done.6.other1
  69.1 0.0 collective-permute-done.7.other3
  69.1 0.0 collective-permute-done.8.other2
  69.1 0.0 all-to-all-done.weight_hbm
  69.1 8.4 %mix.1 = f32[8,72,128]{2,1,0:T(8,128)S(1)} custom-call(bf16[256,640]{1,0:T(8,128)(2,1)S(1)} %pad_maximum_fusion.own0, bf16[256,640]{1,0:T(8,128)(2,1)S(1)} %collective-permute-done.2.own1, bf16[256,640]{1,0:T(8,128)(2,1)S(1)} %collective-permute-done.3.own3, bf16[256,640]{1,0:T(8,128)(2,1)S(1)} %collective-permute-done.4.own2, ...), custom_call_target="tpu_custom_call" | custom-call | tf_op jit(solution)/shard_map/mix/pallas_call | solution.py:412
  77.6 9.8 %all_to_all.15.parts_ref = f32[8,72,128]{2,1,0:T(8,128)S(1)} all-to-all(f32[8,72,128]{2,1,0:T(8,128)S(1)} %mix.1), channel_id=1, replica_groups=mesh['gy'=4,'gx_0'=2,'gx_1'=2,'probe_0'=8,'probe_1'=4] {'gy','gx_1'}, dimensions={0} | all-to-all | bytes 589824 | tf_op jit(solution)/shard_map/all_to_all | solution.py:433
  87.3 0.7 step.1
  88.0 13.8 %all-to-all-start.2 = ((f32[64,1,128]{2,1,0:T(1,128)}), f32[64,1,128]{2,1,0:T(1,128)S(1)}, u32[]{:S(2)}, u32[]{:S(2)}) async-start(f32[64,1,128]{2,1,0:T(1,128)} %bitcast.1), calls=%async_computation.2 | async-start | bytes 65536 | tf_op jit(solution)/shard_map/all_to_all | solution.py:444
  101.8 2.9 %collective-permute-start.9 = (bf16[32,640]{1,0:T(8,128)(2,1)S(1)}, bf16[32,640]{1,0:T(8,128)(2,1)S(1)}, u32[]{:S(2)}, u32[]{:S(2)}) collective-permute-start(bf16[32,640]{1,0:T(8,128)(2,1)S(1)} %get-tuple-element.14.rows0), channel_id=1, source_target_pairs={{0,4},{4,0},{8,12},{12,8},{16,20},{20,16},{24,28},{28,24},{1,5},{5... | collective-permute-start | bytes 122888 | tf_op jit(solution)/shard_map/ppermute | solution.py:443
  104.7 2.1 %collective-permute-done.9.rows1 = bf16[32,640]{1,0:T(8,128)(2,1)S(1)} collective-permute-done((bf16[32,640]{1,0:T(8,128)(2,1)S(1)}, bf16[32,640]{1,0:T(8,128)(2,1)S(1)}, u32[]{:S(2)}, u32[]{:S(2)}) %collective-permute-start.9) | collective-permute-done | bytes 40992 | tf_op jit(solution)/shard_map/ppermute | solution.py:443
  106.9 0.7 final.1
  107.6 5.2 %all-to-all-done.2 = f32[64,1,128]{2,1,0:T(1,128)S(1)} async-done(((f32[64,1,128]{2,1,0:T(1,128)}), f32[64,1,128]{2,1,0:T(1,128)S(1)}, u32[]{:S(2)}, u32[]{:S(2)}) %all-to-all-start.2) | async-done | bytes 32800 | tf_op jit(solution)/shard_map/all_to_all | solution.py:444
  112.8 0.7 tally.1
  (8 shorter events, 0.1 us)
Async XLA Ops:
  0.6 1.0 copy-start
  1.6 66.0 %copy-start.2 = (f32[640]{0:T(1024)S(1)}, f32[640]{0:T(1024)}, u32[]{:S(2)}) copy-start(f32[640]{0:T(1024)} %param.12) | copy-start | bytes 7684
  1.6 66.0 %copy-start.3 = (f32[640]{0:T(1024)S(1)}, f32[640]{0:T(1024)}, u32[]{:S(2)}) copy-start(f32[640]{0:T(1024)} %param.13) | copy-start | bytes 7684
  1.6 66.1 %copy-start.4 = (f32[640]{0:T(1024)S(1)}, f32[640]{0:T(1024)}, u32[]{:S(2)}) copy-start(f32[640]{0:T(1024)} %param.15) | copy-start | bytes 7684
  1.6 66.1 %copy-start.1 = (s32[4]{0:T(128)S(1)}, s32[4]{0:T(128)}, u32[]{:S(2)}) copy-start(s32[4]{0:T(128)} %step_ref.1) | copy-start | bytes 52
  2.7 66.4 %all-to-all-start = ((bf16[32,120,128]{2,1,0:T(8,128)(2,1)}), bf16[32,120,128]{2,1,0:T(8,128)(2,1)}, u32[]{:S(2)}, u32[]{:S(2)}) async-start(bf16[32,120,128]{2,1,0:T(8,128)(2,1)} %deal.1), calls=%async_computation | async-start | bytes 1966080 | tf_op jit(solution)/shard_map/all_to_all | solution.py:399
  17.8 25.4 %collective-permute-start = (bf16[56,640]{1,0:T(8,128)(2,1)S(1)}, bf16[56,640]{1,0:T(8,128)(2,1)S(1)}, u32[]{:S(2)}, u32[]{:S(2)}) collective-permute-start(bf16[56,640]{1,0:T(8,128)(2,1)S(1)} %get-tuple-element.10), channel_id=1, source_target_pairs={{32,64},{64,32},{33,65},{65,33},{34,66},{66,34},{35,67},{67,35},{3... | collective-permute-start | bytes 215048 | tf_op jit(solution)/shard_map/ppermute | solution.py:397
  26.6 16.6 %collective-permute-start.1 = (bf16[8,640]{1,0:T(8,128)(2,1)S(1)}, bf16[8,640]{1,0:T(8,128)(2,1)S(1)}, u32[]{:S(2)}, u32[]{:S(2)}) collective-permute-start(bf16[8,640]{1,0:T(8,128)(2,1)S(1)} %slice.12), channel_id=1, source_target_pairs={{0,96},{96,0},{1,97},{97,1},{2,98},{98,2},{3,99},{99,3},{4,100},{1... | collective-permute-start | bytes 30728 | tf_op jit(solution)/shard_map/ppermute | solution.py:398
  43.3 12.1 %collective-permute-start.2 = (bf16[256,640]{1,0:T(8,128)(2,1)S(1)}, bf16[256,640]{1,0:T(8,128)(2,1)S(1)}, u32[]{:S(2)}, u32[]{:S(2)}) collective-permute-start(bf16[256,640]{1,0:T(8,128)(2,1)S(1)} %pad_maximum_fusion.own0), channel_id=1, source_target_pairs={{0,128},{128,256},{256,384},{384,0},{1,129},{129,257},{257,385},{3... | collective-permute-start | bytes 983048 | tf_op jit(solution)/shard_map/ppermute | solution.py:403
  46.4 9.0 %collective-permute-start.3 = (bf16[256,640]{1,0:T(8,128)(2,1)S(1)}, bf16[256,640]{1,0:T(8,128)(2,1)S(1)}, u32[]{:S(2)}, u32[]{:S(2)}) collective-permute-start(bf16[256,640]{1,0:T(8,128)(2,1)S(1)} %pad_maximum_fusion.own0), channel_id=1, source_target_pairs={{0,384},{128,0},{256,128},{384,256},{1,385},{129,1},{257,129},{385... | collective-permute-start | bytes 983048 | tf_op jit(solution)/shard_map/ppermute | solution.py:404
  55.5 9.7 %collective-permute-start.4 = (bf16[256,640]{1,0:T(8,128)(2,1)S(1)}, bf16[256,640]{1,0:T(8,128)(2,1)S(1)}, u32[]{:S(2)}, u32[]{:S(2)}) collective-permute-start(bf16[256,640]{1,0:T(8,128)(2,1)S(1)} %broadcast_select_fusion), channel_id=1, source_target_pairs={{0,128},{32,416},{128,256},{160,32},{256,384},{288,160},{384,0},{4... | collective-permute-start | bytes 983048 | tf_op jit(solution)/shard_map/ppermute | solution.py:406
  58.9 10.1 %collective-permute-start.5 = (bf16[256,640]{1,0:T(8,128)(2,1)S(1)}, bf16[256,640]{1,0:T(8,128)(2,1)S(1)}, u32[]{:S(2)}, u32[]{:S(2)}) collective-permute-start(bf16[256,640]{1,0:T(8,128)(2,1)S(1)} %pad_maximum_fusion.own0), channel_id=1, source_target_pairs={{0,32},{32,0},{1,33},{33,1},{2,34},{34,2},{3,35},{35,3},{4,36},{36... | collective-permute-start | bytes 983048 | tf_op jit(solution)/shard_map/ppermute | solution.py:409
  60.8 8.2 %collective-permute-start.6 = (bf16[256,640]{1,0:T(8,128)(2,1)S(1)}, bf16[256,640]{1,0:T(8,128)(2,1)S(1)}, u32[]{:S(2)}, u32[]{:S(2)}) collective-permute-start(bf16[256,640]{1,0:T(8,128)(2,1)S(1)} %collective-permute-done.2.own1), channel_id=1, source_target_pairs={{0,32},{32,0},{1,33},{33,1},{2,34},{34,2},{3,35},{35,3},{4,36},{36... | collective-permute-start | bytes 983048 | tf_op jit(solution)/shard_map/ppermute | solution.py:410
  63.2 5.8 %collective-permute-start.7 = (bf16[256,640]{1,0:T(8,128)(2,1)S(1)}, bf16[256,640]{1,0:T(8,128)(2,1)S(1)}, u32[]{:S(2)}, u32[]{:S(2)}) collective-permute-start(bf16[256,640]{1,0:T(8,128)(2,1)S(1)} %collective-permute-done.3.own3), channel_id=1, source_target_pairs={{0,32},{32,0},{1,33},{33,1},{2,34},{34,2},{3,35},{35,3},{4,36},{36... | collective-permute-start | bytes 983048 | tf_op jit(solution)/shard_map/ppermute | solution.py:410
  65.2 3.9 %collective-permute-start.8 = (bf16[256,640]{1,0:T(8,128)(2,1)S(1)}, bf16[256,640]{1,0:T(8,128)(2,1)S(1)}, u32[]{:S(2)}, u32[]{:S(2)}) collective-permute-start(bf16[256,640]{1,0:T(8,128)(2,1)S(1)} %collective-permute-done.4.own2), channel_id=1, source_target_pairs={{0,32},{32,0},{1,33},{33,1},{2,34},{34,2},{3,35},{35,3},{4,36},{36... | collective-permute-start | bytes 983048 | tf_op jit(solution)/shard_map/ppermute | solution.py:410
  88.0 24.8 %all-to-all-start.2 = ((f32[64,1,128]{2,1,0:T(1,128)}), f32[64,1,128]{2,1,0:T(1,128)S(1)}, u32[]{:S(2)}, u32[]{:S(2)}) async-start(f32[64,1,128]{2,1,0:T(1,128)} %bitcast.1), calls=%async_computation.2 | async-start | bytes 65536 | tf_op jit(solution)/shard_map/all_to_all | solution.py:444
  101.8 5.1 %collective-permute-start.9 = (bf16[32,640]{1,0:T(8,128)(2,1)S(1)}, bf16[32,640]{1,0:T(8,128)(2,1)S(1)}, u32[]{:S(2)}, u32[]{:S(2)}) collective-permute-start(bf16[32,640]{1,0:T(8,128)(2,1)S(1)} %get-tuple-element.14.rows0), channel_id=1, source_target_pairs={{0,4},{4,0},{8,12},{12,8},{16,20},{20,16},{24,28},{28,24},{1,5},{5... | collective-permute-start | bytes 122888 | tf_op jit(solution)/shard_map/ppermute | solution.py:443

commit v6 on v4

--- a/solution.py
+++ b/solution.py
@@ -49,19 +49,6 @@
     member = lax.axis_index("gy") * 2 + lax.axis_index("gx_1")
     number = member * PAIRS + index
     return lax.rem(number, 9), lax.div(number, 9)
-
-
-def spread_kernel(weight_ref, wsend_ref, wf):
-    for index in range(PAIRS):
-        tap, ob = pair_of(index)
-        rows = weight_ref[tap].astype(F32)
-        picked = jnp.zeros((rows.shape[0], LANES), F32)
-        for o in range(rows.shape[1] // LANES):
-            picked = picked + jnp.where(ob == o, rows[:, lane_block(o)], 0.0)
-        wf[pl.ds(index, rows.shape[0], stride=PAIRS), :] = picked
-    packed = wf[...].astype(BF16)
-    for target in range(wsend_ref.shape[0]):
-        wsend_ref[target] = packed
 
 
 def lookup_kernel(step_ref, table_hbm, shift_ref, bias_ref, base_ref, offset_ref, start_ref, table, found):
@@ -82,16 +69,34 @@
         offset_ref[b + 4 : b + 5, :] = line
 
 
-def pack_kernel(signs_hbm, state_hbm, main_ref, rim_ref, base_ref, signs_ref, state_ref, uf, xf, rim, sums, arrived):
+def pack_kernel(
+    weight_hbm, state_hbm, signs_hbm, main_ref, rim_ref, base_ref, wsend_hbm,
+    weight_ref, state_ref, signs_ref, uf, xf, wf, wsend_ref, rim, sums, arrived, left,
+):
     blocks = uf.shape[0]
     loads = [
         pltpu.make_async_copy(src, dst, arrived.at[index])
-        for index, (src, dst) in enumerate(((signs_hbm, signs_ref), (state_hbm, state_ref)))
+        for index, (src, dst) in enumerate(
+            ((weight_hbm, weight_ref), (state_hbm, state_ref), (signs_hbm, signs_ref))
+        )
     ]
     for load in loads:
         load.start()
-    for load in loads:
-        load.wait()
+    loads[0].wait()
+    for index in range(PAIRS):
+        tap, ob = pair_of(index)
+        rows = weight_ref[tap].astype(F32)
+        picked = jnp.zeros((rows.shape[0], LANES), F32)
+        for o in range(blocks):
+            picked = picked + jnp.where(ob == o, rows[:, lane_block(o)], 0.0)
+        wf[pl.ds(index, rows.shape[0], stride=PAIRS), :] = picked
+    packed = wf[...].astype(BF16)
+    for target in range(wsend_ref.shape[0]):
+        wsend_ref[target] = packed
+    leave = pltpu.make_async_copy(wsend_ref, wsend_hbm, left)
+    leave.start()
+    loads[1].wait()
+    loads[2].wait()
     for p in range(2):
         for b in range(4):
             for r in range(4):
@@ -144,6 +149,7 @@
         main_ref[0:128, lane_block(o)] = uf[o].astype(BF16)
         main_ref[128:192, lane_block(o)] = xf[o].astype(BF16)
     rim_ref[...] = rim[...].astype(BF16)
+    leave.wait()
 
 
 def mix_kernel(
@@ -248,7 +254,7 @@
                     cell = two * 2 + half_cell
                     u = ug[o, pl.ds(pl.multiple_of(at + cell * 8, 8), 8), :]
                     out = first * (u - mean_u[:, ln]) - second * bend[:, ln]
-                    slope_ref[pl.ds(pl.multiple_of(gr * 64 + cell * 8, 8), 8), ln] = out
+                    slope_ref[pl.ds(pl.multiple_of(gr * 64 + cell * 8, 8), 8), ln] = out.astype(BF16).astype(F32)
             _, pre, sig = fields(xg[o, pl.ds(edge, 4), :], o, 4)
             xg[o, pl.ds(edge, 4), :] = pre * sig
         return carry
@@ -355,32 +361,32 @@
     each = conv_weight.shape[1] * PAIRS
     params = pltpu.CompilerParams(vmem_limit_bytes=40 * 1024 * 1024)
     far = lambda array: pltpu.with_memory_space_constraint(array, pltpu.HBM)
-    main, rim, base = pl.pallas_call(
+    main, rim, base, wsend = pl.pallas_call(
         pack_kernel,
-        out_shape=(shape((192, chans), BF16), shape((56, chans), BF16), shape((32, chans), F32)),
-        in_specs=[HBM] * 2,
-        out_specs=(VMEM,) * 3,
+        out_shape=(
+            shape((192, chans), BF16),
+            shape((56, chans), BF16),
+            shape((32, chans), F32),
+            pltpu.HBM((32, each, LANES), BF16),
+        ),
+        in_specs=[HBM] * 3,
+        out_specs=(VMEM,) * 3 + (HBM,),
         scratch_shapes=[
+            pltpu.VMEM(conv_weight.shape, BF16),
+            pltpu.VMEM(state.shape, BF16),
             pltpu.VMEM(probe_signs.shape, jnp.int32),
-            pltpu.VMEM(state.shape, BF16),
             pltpu.VMEM((blocks, 128, LANES), F32),
             pltpu.VMEM((blocks, 64, LANES), F32),
+            pltpu.VMEM((each, LANES), F32),
+            pltpu.VMEM((32, each, LANES), BF16),
             pltpu.VMEM((56, chans), F32),
             pltpu.VMEM((32, chans), F32),
-            pltpu.SemaphoreType.DMA((2,)),
+            pltpu.SemaphoreType.DMA((3,)),
+            pltpu.SemaphoreType.DMA,
         ],
         compiler_params=params,
         name="pack",
-    )(far(probe_signs), far(state))
-    wsend = pl.pallas_call(
-        spread_kernel,
-        out_shape=shape((32, each, LANES), BF16),
-        in_specs=[VMEM],
-        out_specs=VMEM,
-        scratch_shapes=[pltpu.VMEM((each, LANES), F32)],
-        compiler_params=params,
-        name="deal",
-    )(conv_weight)
+    )(far(conv_weight), far(state), far(probe_signs))
     offset, start = pl.pallas_call(
         lookup_kernel,
         out_shape=(shape((8, chans), F32), shape((32, chans), F32)),
@@ -391,10 +397,10 @@
         name="lookup",
     )(timesteps, far(time_table), gn_shift[None], conv_bias[None], base)
 
-    across = [(a * 2 + b, (1 - a) * 2 + 1 - b) for a in range(2) for b in range(2)]
-    facing = lax.ppermute(rim, GX, across)
+    facing = lax.ppermute(rim, GX, [(1, 2), (2, 1)])
+    outer = lax.ppermute(rim[48:56], GX, [(0, 3), (3, 0)])
     weights = lax.all_to_all(wsend, PROBE, 0, 0, tiled=True)
-    block = jnp.concatenate([main, facing, rim[48:56]], axis=0)
+    block = jnp.concatenate([main, facing[:48], facing[48:] + outer, rim[48:56]], axis=0)
     down = [(i, (i + 1) % 4) for i in range(4)]
     up = [(i, (i + 3) % 4) for i in range(4)]
     above = lax.ppermute(block, "gy", down)
@@ -436,9 +442,9 @@
         compiler_params=params,
         name="step",
     )(partial, start)
+    mass = lax.all_to_all(mass.reshape(64, 1, LANES), ("gx_0",) + PROBE, 0, 0, tiled=True)
     tall = lax.axis_size("probe_0")
     facing_rows = lax.ppermute(rows, "probe_0", [(y, y ^ 1) for y in range(tall)])
-    mass = lax.all_to_all(mass.reshape(64, 1, LANES), ("gx_0",) + PROBE, 0, 0, tiled=True)
     scale = -0.25 / (probe_signs.shape[0] * lax.axis_size(PROBE))
     return pl.pallas_call(
         lambda *refs: final_kernel(scale, *refs),

time: 118 us -> 115 us (0.975)
  starting transfers between devices: 54.4 us -> 57.7 us
  waiting for transfers between devices: 35.4 us -> 32.3 us
    all_to_all x1, starting transfers between devices: 9.41 us -> 14.9 us  [body(): lax.all_to_all(mass.reshape(64, 1, LANES), ('gx_0',) + PROBE, 0, 0, tiled...]
    ppermute x1 -> x2, waiting for transfers between devices: 20.1 us -> 17.3 us  [the longest x1 17.2 us: body(): facing = lax.ppermute(rim, GX, [(1, 2), (2, 1)])]
    ppermute x1, starting transfers between devices: 4.58 us -> 1.92 us  [body(): lax.ppermute(jnp.where(lax.axis_index('gx_1') == 0, above, below), ('gy',...]
    ppermute x1, starting transfers between devices: 3.12 us -> 1.92 us  [body(): above = lax.ppermute(block, 'gy', down)]
    ppermute x1 -> x2, starting transfers between devices: 8.78 us -> 9.44 us  [the longest x1 8.78 us: body(): facing = lax.ppermute(rim, GX, [(1, 2), (2, 1)])]
  transfers between devices with their start and end apart: 11 -> 12, of which waited for: 5 -> 5; matrix products, arithmetic and copies ran while one was open for 0% -> 0% of each run, Pallas kernels for 2% -> 1%
where the time goes in v6:
time: 115 us
  starting transfers between devices  57.7 us (50%)
  waiting for transfers between devices  32.3 us (28%)
  Pallas kernels  13.3 us (12%)
  blocking collectives  10.2 us (9%)
    ppermute x1, waiting for transfers between devices, body(): facing = lax.ppermute(rim, GX, [(1, 2), (2, 1)])  17.2 us
    all_to_all x1, starting transfers between devices, body(): lax.all_to_all(mass.reshape(64, 1, LANES), ('gx_0',) + PROBE, 0, 0, tiled...  14.9 us
    all_to_all x1, starting transfers between devices, body(): weights = lax.all_to_all(wsend, PROBE, 0, 0, tiled=True)  13.6 us
    all_to_all x1, blocking collectives, body(): partial = lax.all_to_all(partial, ('gy', 'gx_1'), 0, 0, tiled=True)  10.2 us
    ppermute x1, starting transfers between devices, body(): facing = lax.ppermute(rim, GX, [(1, 2), (2, 1)])  8.78 us
    pallas_call x1, Pallas kernels, body(): pl.pallas_call(mix_kernel, out_shape=shape((8, 72, LANES), F32), in_specs...  8.46 us
    ppermute x3, starting transfers between devices, body(): other += [lax.ppermute(tile, 'gx_1', swap) for tile in own[1:]]  6.73 us
    all_to_all x1, waiting for transfers between devices, body(): lax.all_to_all(mass.reshape(64, 1, LANES), ('gx_0',) + PROBE, 0, 0, tiled...  5.86 us
  transfers between devices with their start and end apart: 12, of which 5 were waited for; matrix products, arithmetic and copies ran while one was open for 0% of the time, Pallas kernels for 1%

profile of v6, /device:TPU:1, one launch (start us, length us, event | category | flops | bytes accessed | tf_op | source)
XLA Modules:
  0.0 114.6 jit_solution(16533815815852194645)
XLA Ops:
  0.6 0.0 copy-start.1
  0.6 0.0 copy-start.2
  0.7 0.0 copy-start.3
  0.7 0.0 copy-start
  0.7 2.1 %pack.1 = (bf16[192,640]{1,0:T(8,128)(2,1)S(1)}, bf16[56,640]{1,0:T(8,128)(2,1)S(1)}, f32[32,640]{1,0:T(8,128)S(1)}, bf16[32,120,128]{2,1,0:T(8,128)(2,1)}) custom-call(bf16[9,20,640]{2,1,0:T(8,128)(2,1)} %weight_hbm.1, bf16[4,4,4,640]{3,2,1,0:T(4,128)(2,1)} %state_hbm.1, s32[2,4,4,4,640]{4,3,2,1,0:T(4,128)} %signs_hbm.1), custom_call_target="tpu_custom_call" | custom-call | tf_op jit(solution)/shard_map/pack/pallas_call | solution.py:364
  2.8 13.6 %all-to-all-start = ((bf16[32,120,128]{2,1,0:T(8,128)(2,1)}), bf16[32,120,128]{2,1,0:T(8,128)(2,1)}, u32[]{:S(2)}, u32[]{:S(2)}) async-start(bf16[32,120,128]{2,1,0:T(8,128)(2,1)} %get-tuple-element.12), calls=%async_computation | async-start | bytes 1966080 | tf_op jit(solution)/shard_map/all_to_all | solution.py:402
  16.4 8.8 %collective-permute-start = (bf16[56,640]{1,0:T(8,128)(2,1)S(1)}, bf16[56,640]{1,0:T(8,128)(2,1)S(1)}, u32[]{:S(2)}, u32[]{:S(2)}) collective-permute-start(bf16[56,640]{1,0:T(8,128)(2,1)S(1)} %get-tuple-element.11), channel_id=1, source_target_pairs={{32,64},{64,32},{33,65},{65,33},{34,66},{66,34},{35,67},{67,35},{3... | collective-permute-start | bytes 215048 | tf_op jit(solution)/shard_map/ppermute | solution.py:400
  25.2 0.7 collective-permute-start.1
  25.8 17.2 %collective-permute-done = bf16[56,640]{1,0:T(8,128)(2,1)S(1)} collective-permute-done((bf16[56,640]{1,0:T(8,128)(2,1)S(1)}, bf16[56,640]{1,0:T(8,128)(2,1)S(1)}, u32[]{:S(2)}, u32[]{:S(2)}) %collective-permute-start) | collective-permute-done | bytes 71712 | tf_op jit(solution)/shard_map/ppermute | solution.py:400
  43.1 0.0 collective-permute-done.1
  43.1 4.4 %collective-permute-start.3 = (bf16[256,640]{1,0:T(8,128)(2,1)S(1)}, bf16[256,640]{1,0:T(8,128)(2,1)S(1)}, u32[]{:S(2)}, u32[]{:S(2)}) collective-permute-start(bf16[256,640]{1,0:T(8,128)(2,1)S(1)} %pad_maximum_fusion.own0), channel_id=1, source_target_pairs={{0,384},{128,0},{256,128},{384,256},{1,385},{129,1},{257,129},{385... | collective-permute-start | bytes 983048 | tf_op jit(solution)/shard_map/ppermute | solution.py:407
  47.5 1.9 %collective-permute-start.2 = (bf16[256,640]{1,0:T(8,128)(2,1)S(1)}, bf16[256,640]{1,0:T(8,128)(2,1)S(1)}, u32[]{:S(2)}, u32[]{:S(2)}) collective-permute-start(bf16[256,640]{1,0:T(8,128)(2,1)S(1)} %pad_maximum_fusion.own0), channel_id=1, source_target_pairs={{0,128},{128,256},{256,384},{384,0},{1,129},{129,257},{257,385},{3... | collective-permute-start | bytes 983048 | tf_op jit(solution)/shard_map/ppermute | solution.py:406
  49.5 2.1 %collective-permute-done.3.own3 = bf16[256,640]{1,0:T(8,128)(2,1)S(1)} collective-permute-done((bf16[256,640]{1,0:T(8,128)(2,1)S(1)}, bf16[256,640]{1,0:T(8,128)(2,1)S(1)}, u32[]{:S(2)}, u32[]{:S(2)}) %collective-permute-start.3) | collective-permute-done | bytes 327712 | tf_op jit(solution)/shard_map/ppermute | solution.py:407
  51.5 5.0 %collective-permute-done.2.own1 = bf16[256,640]{1,0:T(8,128)(2,1)S(1)} collective-permute-done((bf16[256,640]{1,0:T(8,128)(2,1)S(1)}, bf16[256,640]{1,0:T(8,128)(2,1)S(1)}, u32[]{:S(2)}, u32[]{:S(2)}) %collective-permute-start.2) | collective-permute-done | bytes 327712 | tf_op jit(solution)/shard_map/ppermute | solution.py:406
  56.6 1.9 %collective-permute-start.4 = (bf16[256,640]{1,0:T(8,128)(2,1)S(1)}, bf16[256,640]{1,0:T(8,128)(2,1)S(1)}, u32[]{:S(2)}, u32[]{:S(2)}) collective-permute-start(bf16[256,640]{1,0:T(8,128)(2,1)S(1)} %broadcast_select_fusion), channel_id=1, source_target_pairs={{0,128},{32,416},{128,256},{160,32},{256,384},{288,160},{384,0},{4... | collective-permute-start | bytes 983048 | tf_op jit(solution)/shard_map/ppermute | solution.py:409
  58.5 1.9 %collective-permute-start.5 = (bf16[256,640]{1,0:T(8,128)(2,1)S(1)}, bf16[256,640]{1,0:T(8,128)(2,1)S(1)}, u32[]{:S(2)}, u32[]{:S(2)}) collective-permute-start(bf16[256,640]{1,0:T(8,128)(2,1)S(1)} %pad_maximum_fusion.own0), channel_id=1, source_target_pairs={{0,32},{32,0},{1,33},{33,1},{2,34},{34,2},{3,35},{35,3},{4,36},{36... | collective-permute-start | bytes 983048 | tf_op jit(solution)/shard_map/ppermute | solution.py:412
  60.5 2.4 %collective-permute-start.7 = (bf16[256,640]{1,0:T(8,128)(2,1)S(1)}, bf16[256,640]{1,0:T(8,128)(2,1)S(1)}, u32[]{:S(2)}, u32[]{:S(2)}) collective-permute-start(bf16[256,640]{1,0:T(8,128)(2,1)S(1)} %collective-permute-done.3.own3), channel_id=1, source_target_pairs={{0,32},{32,0},{1,33},{33,1},{2,34},{34,2},{3,35},{35,3},{4,36},{36... | collective-permute-start | bytes 983048 | tf_op jit(solution)/shard_map/ppermute | solution.py:413
  62.9 1.9 %collective-permute-start.6 = (bf16[256,640]{1,0:T(8,128)(2,1)S(1)}, bf16[256,640]{1,0:T(8,128)(2,1)S(1)}, u32[]{:S(2)}, u32[]{:S(2)}) collective-permute-start(bf16[256,640]{1,0:T(8,128)(2,1)S(1)} %collective-permute-done.2.own1), channel_id=1, source_target_pairs={{0,32},{32,0},{1,33},{33,1},{2,34},{34,2},{3,35},{35,3},{4,36},{36... | collective-permute-start | bytes 983048 | tf_op jit(solution)/shard_map/ppermute | solution.py:413
  64.8 0.0 collective-permute-done.4.own2
  64.8 2.4 %collective-permute-start.8 = (bf16[256,640]{1,0:T(8,128)(2,1)S(1)}, bf16[256,640]{1,0:T(8,128)(2,1)S(1)}, u32[]{:S(2)}, u32[]{:S(2)}) collective-permute-start(bf16[256,640]{1,0:T(8,128)(2,1)S(1)} %collective-permute-done.4.own2), channel_id=1, source_target_pairs={{0,32},{32,0},{1,33},{33,1},{2,34},{34,2},{3,35},{35,3},{4,36},{36... | collective-permute-start | bytes 983048 | tf_op jit(solution)/shard_map/ppermute | solution.py:413
  67.2 0.0 copy-done.1
  67.3 0.0 copy-done.2
  67.3 0.0 copy-done.3
  67.3 0.0 copy-done
  67.3 1.4 %lookup.1 = (f32[8,640]{1,0:T(8,128)S(1)}, f32[32,640]{1,0:T(8,128)S(1)}) custom-call(s32[4]{0:T(128)S(1)} %copy-done, f32[1000,640]{1,0:T(8,128)} %table_hbm.1, f32[1,640]{1,0:T(1,128)S(1)} %broadcast_in_dim.10.shift_ref, f32[1,640]{1,0:T(1,128)S(1)} %broadcast_in_dim.11.bias_ref, f32[32,640]{1,0:T(8,128)S(1)} %get-tuple-element.13.base_ref), custom_call_target="tpu_custom_call" | custom-call | tf_op jit(solution)/shard_map/lookup/pallas_call | solution.py:390
  68.7 0.0 collective-permute-done.5.other0
  68.7 0.0 collective-permute-done.7.other3
  68.7 0.0 collective-permute-done.6.other1
  68.7 0.0 collective-permute-done.8.other2
  68.7 0.0 all-to-all-done.weight_hbm
  68.7 8.5 %mix.1 = f32[8,72,128]{2,1,0:T(8,128)S(1)} custom-call(bf16[256,640]{1,0:T(8,128)(2,1)S(1)} %pad_maximum_fusion.own0, bf16[256,640]{1,0:T(8,128)(2,1)S(1)} %collective-permute-done.2.own1, bf16[256,640]{1,0:T(8,128)(2,1)S(1)} %collective-permute-done.3.own3, bf16[256,640]{1,0:T(8,128)(2,1)S(1)} %collective-permute-done.4.own2, ...), custom_call_target="tpu_custom_call" | custom-call | tf_op jit(solution)/shard_map/mix/pallas_call | solution.py:415
  77.2 10.2 %all_to_all.15.parts_ref = f32[8,72,128]{2,1,0:T(8,128)S(1)} all-to-all(f32[8,72,128]{2,1,0:T(8,128)S(1)} %mix.1), channel_id=1, replica_groups=mesh['gy'=4,'gx_0'=2,'gx_1'=2,'probe_0'=8,'probe_1'=4] {'gy','gx_1'}, dimensions={0} | all-to-all | bytes 589824 | tf_op jit(solution)/shard_map/all_to_all | solution.py:436
  87.4 0.7 step.1
  88.1 14.9 %all-to-all-start.2 = ((f32[64,1,128]{2,1,0:T(1,128)}), f32[64,1,128]{2,1,0:T(1,128)S(1)}, u32[]{:S(2)}, u32[]{:S(2)}) async-start(f32[64,1,128]{2,1,0:T(1,128)} %bitcast.1), calls=%async_computation.2 | async-start | bytes 65536 | tf_op jit(solution)/shard_map/all_to_all | solution.py:445
  103.0 2.9 %collective-permute-start.9 = (bf16[32,640]{1,0:T(8,128)(2,1)S(1)}, bf16[32,640]{1,0:T(8,128)(2,1)S(1)}, u32[]{:S(2)}, u32[]{:S(2)}) collective-permute-start(bf16[32,640]{1,0:T(8,128)(2,1)S(1)} %get-tuple-element.17.refs_1_), channel_id=1, source_target_pairs={{0,4},{4,0},{8,12},{12,8},{16,20},{20,16},{24,28},{28,24},{1,5},{5... | collective-permute-start | bytes 122888 | tf_op jit(solution)/shard_map/ppermute | solution.py:447
  105.9 2.1 %collective-permute-done.9.refs_2_ = bf16[32,640]{1,0:T(8,128)(2,1)S(1)} collective-permute-done((bf16[32,640]{1,0:T(8,128)(2,1)S(1)}, bf16[32,640]{1,0:T(8,128)(2,1)S(1)}, u32[]{:S(2)}, u32[]{:S(2)}) %collective-permute-start.9) | collective-permute-done | bytes 40992 | tf_op jit(solution)/shard_map/ppermute | solution.py:447
  108.0 5.9 %all-to-all-done.2 = f32[64,1,128]{2,1,0:T(1,128)S(1)} async-done(((f32[64,1,128]{2,1,0:T(1,128)}), f32[64,1,128]{2,1,0:T(1,128)S(1)}, u32[]{:S(2)}, u32[]{:S(2)}) %all-to-all-start.2) | async-done | bytes 32800 | tf_op jit(solution)/shard_map/all_to_all | solution.py:445
  113.9 0.7 final.1
  (8 shorter events, 0.1 us)
Async XLA Ops:
  0.6 66.6 %copy-start.1 = (f32[640]{0:T(1024)S(1)}, f32[640]{0:T(1024)}, u32[]{:S(2)}) copy-start(f32[640]{0:T(1024)} %param.12) | copy-start | bytes 7684
  0.6 66.6 %copy-start.2 = (f32[640]{0:T(1024)S(1)}, f32[640]{0:T(1024)}, u32[]{:S(2)}) copy-start(f32[640]{0:T(1024)} %param.13) | copy-start | bytes 7684
  0.7 66.6 %copy-start.3 = (f32[640]{0:T(1024)S(1)}, f32[640]{0:T(1024)}, u32[]{:S(2)}) copy-start(f32[640]{0:T(1024)} %param.15) | copy-start | bytes 7684
  0.7 66.6 %copy-start = (s32[4]{0:T(128)S(1)}, s32[4]{0:T(128)}, u32[]{:S(2)}) copy-start(s32[4]{0:T(128)} %step_ref.1) | copy-start | bytes 52
  2.8 66.0 %all-to-all-start = ((bf16[32,120,128]{2,1,0:T(8,128)(2,1)}), bf16[32,120,128]{2,1,0:T(8,128)(2,1)}, u32[]{:S(2)}, u32[]{:S(2)}) async-start(bf16[32,120,128]{2,1,0:T(8,128)(2,1)} %get-tuple-element.12), calls=%async_computation | async-start | bytes 1966080 | tf_op jit(solution)/shard_map/all_to_all | solution.py:402
  16.4 26.7 %collective-permute-start = (bf16[56,640]{1,0:T(8,128)(2,1)S(1)}, bf16[56,640]{1,0:T(8,128)(2,1)S(1)}, u32[]{:S(2)}, u32[]{:S(2)}) collective-permute-start(bf16[56,640]{1,0:T(8,128)(2,1)S(1)} %get-tuple-element.11), channel_id=1, source_target_pairs={{32,64},{64,32},{33,65},{65,33},{34,66},{66,34},{35,67},{67,35},{3... | collective-permute-start | bytes 215048 | tf_op jit(solution)/shard_map/ppermute | solution.py:400
  25.2 17.9 %collective-permute-start.1 = (bf16[8,640]{1,0:T(8,128)(2,1)S(1)}, bf16[8,640]{1,0:T(8,128)(2,1)S(1)}, u32[]{:S(2)}, u32[]{:S(2)}) collective-permute-start(bf16[8,640]{1,0:T(8,128)(2,1)S(1)} %slice.12), channel_id=1, source_target_pairs={{0,96},{96,0},{1,97},{97,1},{2,98},{98,2},{3,99},{99,3},{4,100},{1... | collective-permute-start | bytes 30728 | tf_op jit(solution)/shard_map/ppermute | solution.py:401
  43.1 8.4 %collective-permute-start.3 = (bf16[256,640]{1,0:T(8,128)(2,1)S(1)}, bf16[256,640]{1,0:T(8,128)(2,1)S(1)}, u32[]{:S(2)}, u32[]{:S(2)}) collective-permute-start(bf16[256,640]{1,0:T(8,128)(2,1)S(1)} %pad_maximum_fusion.own0), channel_id=1, source_target_pairs={{0,384},{128,0},{256,128},{384,256},{1,385},{129,1},{257,129},{385... | collective-permute-start | bytes 983048 | tf_op jit(solution)/shard_map/ppermute | solution.py:407
  47.5 9.0 %collective-permute-start.2 = (bf16[256,640]{1,0:T(8,128)(2,1)S(1)}, bf16[256,640]{1,0:T(8,128)(2,1)S(1)}, u32[]{:S(2)}, u32[]{:S(2)}) collective-permute-start(bf16[256,640]{1,0:T(8,128)(2,1)S(1)} %pad_maximum_fusion.own0), channel_id=1, source_target_pairs={{0,128},{128,256},{256,384},{384,0},{1,129},{129,257},{257,385},{3... | collective-permute-start | bytes 983048 | tf_op jit(solution)/shard_map/ppermute | solution.py:406
  56.6 8.2 %collective-permute-start.4 = (bf16[256,640]{1,0:T(8,128)(2,1)S(1)}, bf16[256,640]{1,0:T(8,128)(2,1)S(1)}, u32[]{:S(2)}, u32[]{:S(2)}) collective-permute-start(bf16[256,640]{1,0:T(8,128)(2,1)S(1)} %broadcast_select_fusion), channel_id=1, source_target_pairs={{0,128},{32,416},{128,256},{160,32},{256,384},{288,160},{384,0},{4... | collective-permute-start | bytes 983048 | tf_op jit(solution)/shard_map/ppermute | solution.py:409
  58.5 10.1 %collective-permute-start.5 = (bf16[256,640]{1,0:T(8,128)(2,1)S(1)}, bf16[256,640]{1,0:T(8,128)(2,1)S(1)}, u32[]{:S(2)}, u32[]{:S(2)}) collective-permute-start(bf16[256,640]{1,0:T(8,128)(2,1)S(1)} %pad_maximum_fusion.own0), channel_id=1, source_target_pairs={{0,32},{32,0},{1,33},{33,1},{2,34},{34,2},{3,35},{35,3},{4,36},{36... | collective-permute-start | bytes 983048 | tf_op jit(solution)/shard_map/ppermute | solution.py:412
  60.5 8.2 %collective-permute-start.7 = (bf16[256,640]{1,0:T(8,128)(2,1)S(1)}, bf16[256,640]{1,0:T(8,128)(2,1)S(1)}, u32[]{:S(2)}, u32[]{:S(2)}) collective-permute-start(bf16[256,640]{1,0:T(8,128)(2,1)S(1)} %collective-permute-done.3.own3), channel_id=1, source_target_pairs={{0,32},{32,0},{1,33},{33,1},{2,34},{34,2},{3,35},{35,3},{4,36},{36... | collective-permute-start | bytes 983048 | tf_op jit(solution)/shard_map/ppermute | solution.py:413
  62.9 5.8 %collective-permute-start.6 = (bf16[256,640]{1,0:T(8,128)(2,1)S(1)}, bf16[256,640]{1,0:T(8,128)(2,1)S(1)}, u32[]{:S(2)}, u32[]{:S(2)}) collective-permute-start(bf16[256,640]{1,0:T(8,128)(2,1)S(1)} %collective-permute-done.2.own1), channel_id=1, source_target_pairs={{0,32},{32,0},{1,33},{33,1},{2,34},{34,2},{3,35},{35,3},{4,36},{36... | collective-permute-start | bytes 983048 | tf_op jit(solution)/shard_map/ppermute | solution.py:413
  64.8 3.9 %collective-permute-start.8 = (bf16[256,640]{1,0:T(8,128)(2,1)S(1)}, bf16[256,640]{1,0:T(8,128)(2,1)S(1)}, u32[]{:S(2)}, u32[]{:S(2)}) collective-permute-start(bf16[256,640]{1,0:T(8,128)(2,1)S(1)} %collective-permute-done.4.own2), channel_id=1, source_target_pairs={{0,32},{32,0},{1,33},{33,1},{2,34},{34,2},{3,35},{35,3},{4,36},{36... | collective-permute-start | bytes 983048 | tf_op jit(solution)/shard_map/ppermute | solution.py:413
  88.1 25.8 %all-to-all-start.2 = ((f32[64,1,128]{2,1,0:T(1,128)}), f32[64,1,128]{2,1,0:T(1,128)S(1)}, u32[]{:S(2)}, u32[]{:S(2)}) async-start(f32[64,1,128]{2,1,0:T(1,128)} %bitcast.1), calls=%async_computation.2 | async-start | bytes 65536 | tf_op jit(solution)/shard_map/all_to_all | solution.py:445
  103.0 5.0 %collective-permute-start.9 = (bf16[32,640]{1,0:T(8,128)(2,1)S(1)}, bf16[32,640]{1,0:T(8,128)(2,1)S(1)}, u32[]{:S(2)}, u32[]{:S(2)}) collective-permute-start(bf16[32,640]{1,0:T(8,128)(2,1)S(1)} %get-tuple-element.17.refs_1_), channel_id=1, source_target_pairs={{0,4},{4,0},{8,12},{12,8},{16,20},{20,16},{24,28},{28,24},{1,5},{5... | collective-permute-start | bytes 122888 | tf_op jit(solution)/shard_map/ppermute | solution.py:447

commit v7 on v6

--- a/solution.py
+++ b/solution.py
@@ -154,7 +154,7 @@
 
 def mix_kernel(
     own0, own1, own3, own2, other0, other1, other3, other2, weight_hbm, gain_ref, offset_ref,
-    out_ref, ug, xg, lhs_ref, slope_ref, rows_ref, weight_ref, wf, wc, velocity, arrived,
+    out_ref, ug, xg, edges, lhs_ref, slope_ref, rows_ref, weight_ref, wf, wc, velocity, arrived,
 ):
     load = pltpu.make_async_copy(weight_hbm, weight_ref, arrived)
     load.start()
@@ -200,7 +200,8 @@
             at = spot(4 * tile + r + 1, rim_col)
             for o in range(blocks):
                 ug[o, pl.ds(at, 8), :] = rim[r * 8 : r * 8 + 8, lane_block(o)]
-                xg[o, pl.ds(small(4 * tile + r + 1, rim_col), 4), :] = rim[32 + r * 4 : 36 + r * 4, lane_block(o)]
+        for o in range(blocks):
+            edges[o, pl.ds(pl.multiple_of(tile * 16, 16), 16), :] = rim[32:48, lane_block(o)]
 
     stats = total[:, lane_block(0)] + total[:, lane_block(1)] + total[:, lane_block(2)]
     width = chans // GROUPS
@@ -233,13 +234,12 @@
         at = lane_block(o)
         centered = x - mean[:rows, at]
         pre = centered * scale[:rows, at] + offset[:rows, at]
-        sig = 1.0 / (1.0 + jnp.exp(-pre))
+        sig = 0.5 + 0.5 * jnp.tanh(0.5 * pre)
         return centered, pre, sig
 
     def grid_row(gr, carry):
         at = spot(gr + 1, 1)
         near = small(gr + 1, 1)
-        edge = small(gr + 1, rim_col)
         for o in range(blocks):
             ln = lane_block(o)
             x = xg[o, pl.ds(near, 32), :].reshape(4, 8, LANES)
@@ -250,16 +250,21 @@
             across = slope * gain[:, ln] * centered
             for two in range(4):
                 spans = zip(doubled_rows(along[two]), doubled_rows(across[two]))
+                cells = []
                 for half_cell, (first, second) in enumerate(spans):
-                    cell = two * 2 + half_cell
-                    u = ug[o, pl.ds(pl.multiple_of(at + cell * 8, 8), 8), :]
-                    out = first * (u - mean_u[:, ln]) - second * bend[:, ln]
-                    slope_ref[pl.ds(pl.multiple_of(gr * 64 + cell * 8, 8), 8), ln] = out.astype(BF16).astype(F32)
-            _, pre, sig = fields(xg[o, pl.ds(edge, 4), :], o, 4)
-            xg[o, pl.ds(edge, 4), :] = pre * sig
+                    u = ug[o, pl.ds(pl.multiple_of(at + (two * 2 + half_cell) * 8, 8), 8), :]
+                    cells.append(first * (u - mean_u[:, ln]) - second * bend[:, ln])
+                out = jnp.concatenate(cells, axis=0).astype(BF16)
+                slope_ref[pl.ds(pl.multiple_of(gr * 64 + two * 16, 16), 16), ln] = out
         return carry
 
     lax.fori_loop(0, 16, grid_row, 0)
+
+    for o in range(blocks):
+        _, pre, sig = fields(edges[o].reshape(8, 8, LANES), o, 8)
+        edges[o] = (pre * sig).reshape(64, LANES)
+        for row in range(16):
+            xg[o, pl.ds(small(row + 1, rim_col), 4), :] = edges[o, row * 4 : row * 4 + 4, :]
 
     taps = [pair_of(index) for index in range(PAIRS)]
 
@@ -289,13 +294,13 @@
     for index in range(PAIRS):
         wc[:, lane_block(index)] = wf[pl.ds(index, chans, stride=PAIRS), :].astype(BF16)
 
-    chunk = 256
+    chunk = 512
     total = jnp.zeros((8, chans), F32)
     for start in range(0, lhs_ref.shape[0], chunk):
         value = lax.dot_general(
             lhs_ref[start : start + chunk, :], wc[...], (((1,), (1,)), ((), ())), preferred_element_type=F32
         )
-        value = value * slope_ref[start : start + chunk, :]
+        value = value * slope_ref[start : start + chunk, :].astype(F32)
         total = total + jnp.sum(value.reshape(chunk // 8, 8, chans), axis=0)
     lanes = total[:, lane_block(0)]
     for o in range(1, blocks):
@@ -420,8 +425,9 @@
         scratch_shapes=[
             pltpu.VMEM((blocks, 1440, LANES), F32),
             pltpu.VMEM((blocks, 720, LANES), F32),
+            pltpu.VMEM((blocks, 64, LANES), F32),
             pltpu.VMEM((1024, PAIRS * LANES), BF16),
-            pltpu.VMEM((1024, chans), F32),
+            pltpu.VMEM((1024, chans), BF16),
             pltpu.VMEM((PAIRS * 256, chans), BF16),
             pltpu.VMEM((32, each, LANES), BF16),
             pltpu.VMEM((32 * each, LANES), F32),

time: 115 us -> 113 us (0.983)
  Pallas kernels: 13.3 us -> 11.1 us
    pallas_call x1, Pallas kernels: 8.46 us -> 6.24 us  [body(): pl.pallas_call(mix_kernel, out_shape=shape((8, 72, LANES), F32), in_specs...]
where the time goes in v7:
time: 113 us; the launch traced here: 112 us
  starting transfers between devices  57.7 us (51%)
  waiting for transfers between devices  32.3 us (29%)
  Pallas kernels  11.1 us (10%)
  blocking collectives  10.2 us (9%)
    ppermute x1, waiting for transfers between devices, body(): facing = lax.ppermute(rim, GX, [(1, 2), (2, 1)])  17.2 us
    all_to_all x1, starting transfers between devices, body(): lax.all_to_all(mass.reshape(64, 1, LANES), ('gx_0',) + PROBE, 0, 0, tiled...  14.9 us
    all_to_all x1, starting transfers between devices, body(): weights = lax.all_to_all(wsend, PROBE, 0, 0, tiled=True)  13.6 us
    all_to_all x1, blocking collectives, body(): partial = lax.all_to_all(partial, ('gy', 'gx_1'), 0, 0, tiled=True)  10.2 us
    ppermute x1, starting transfers between devices, body(): facing = lax.ppermute(rim, GX, [(1, 2), (2, 1)])  8.78 us
    ppermute x3, starting transfers between devices, body(): other += [lax.ppermute(tile, 'gx_1', swap) for tile in own[1:]]  6.73 us
    pallas_call x1, Pallas kernels, body(): pl.pallas_call(mix_kernel, out_shape=shape((8, 72, LANES), F32), in_specs...  6.24 us
    all_to_all x1, waiting for transfers between devices, body(): lax.all_to_all(mass.reshape(64, 1, LANES), ('gx_0',) + PROBE, 0, 0, tiled...  5.86 us
  transfers between devices with their start and end apart: 12, of which 5 were waited for; matrix products, arithmetic and copies ran while one was open for 0% of the time, Pallas kernels for 1%

profile of v7, /device:TPU:1, one launch (start us, length us, event | category | flops | bytes accessed | tf_op | source)
XLA Modules:
  0.0 112.4 jit_solution(1613517941382503188)
XLA Ops:
  0.6 0.0 copy-start.1
  0.6 0.0 copy-start.2
  0.7 0.0 copy-start.3
  0.7 0.0 copy-start
  0.7 2.1 %pack.1 = (bf16[192,640]{1,0:T(8,128)(2,1)S(1)}, bf16[56,640]{1,0:T(8,128)(2,1)S(1)}, f32[32,640]{1,0:T(8,128)S(1)}, bf16[32,120,128]{2,1,0:T(8,128)(2,1)}) custom-call(bf16[9,20,640]{2,1,0:T(8,128)(2,1)} %weight_hbm.1, bf16[4,4,4,640]{3,2,1,0:T(4,128)(2,1)} %state_hbm.1, s32[2,4,4,4,640]{4,3,2,1,0:T(4,128)} %signs_hbm.1), custom_call_target="tpu_custom_call" | custom-call | tf_op jit(solution)/shard_map/pack/pallas_call | solution.py:369
  2.8 13.6 %all-to-all-start = ((bf16[32,120,128]{2,1,0:T(8,128)(2,1)}), bf16[32,120,128]{2,1,0:T(8,128)(2,1)}, u32[]{:S(2)}, u32[]{:S(2)}) async-start(bf16[32,120,128]{2,1,0:T(8,128)(2,1)} %get-tuple-element.12), calls=%async_computation | async-start | bytes 1966080 | tf_op jit(solution)/shard_map/all_to_all | solution.py:407
  16.4 8.8 %collective-permute-start = (bf16[56,640]{1,0:T(8,128)(2,1)S(1)}, bf16[56,640]{1,0:T(8,128)(2,1)S(1)}, u32[]{:S(2)}, u32[]{:S(2)}) collective-permute-start(bf16[56,640]{1,0:T(8,128)(2,1)S(1)} %get-tuple-element.11), channel_id=1, source_target_pairs={{32,64},{64,32},{33,65},{65,33},{34,66},{66,34},{35,67},{67,35},{3... | collective-permute-start | bytes 215048 | tf_op jit(solution)/shard_map/ppermute | solution.py:405
  25.2 0.7 collective-permute-start.1
  25.8 17.2 %collective-permute-done = bf16[56,640]{1,0:T(8,128)(2,1)S(1)} collective-permute-done((bf16[56,640]{1,0:T(8,128)(2,1)S(1)}, bf16[56,640]{1,0:T(8,128)(2,1)S(1)}, u32[]{:S(2)}, u32[]{:S(2)}) %collective-permute-start) | collective-permute-done | bytes 71712 | tf_op jit(solution)/shard_map/ppermute | solution.py:405
  43.1 0.0 collective-permute-done.1
  43.1 4.4 %collective-permute-start.3 = (bf16[256,640]{1,0:T(8,128)(2,1)S(1)}, bf16[256,640]{1,0:T(8,128)(2,1)S(1)}, u32[]{:S(2)}, u32[]{:S(2)}) collective-permute-start(bf16[256,640]{1,0:T(8,128)(2,1)S(1)} %pad_maximum_fusion.own0), channel_id=1, source_target_pairs={{0,384},{128,0},{256,128},{384,256},{1,385},{129,1},{257,129},{385... | collective-permute-start | bytes 983048 | tf_op jit(solution)/shard_map/ppermute | solution.py:412
  47.5 1.9 %collective-permute-start.2 = (bf16[256,640]{1,0:T(8,128)(2,1)S(1)}, bf16[256,640]{1,0:T(8,128)(2,1)S(1)}, u32[]{:S(2)}, u32[]{:S(2)}) collective-permute-start(bf16[256,640]{1,0:T(8,128)(2,1)S(1)} %pad_maximum_fusion.own0), channel_id=1, source_target_pairs={{0,128},{128,256},{256,384},{384,0},{1,129},{129,257},{257,385},{3... | collective-permute-start | bytes 983048 | tf_op jit(solution)/shard_map/ppermute | solution.py:411
  49.5 2.1 %collective-permute-done.3.own3 = bf16[256,640]{1,0:T(8,128)(2,1)S(1)} collective-permute-done((bf16[256,640]{1,0:T(8,128)(2,1)S(1)}, bf16[256,640]{1,0:T(8,128)(2,1)S(1)}, u32[]{:S(2)}, u32[]{:S(2)}) %collective-permute-start.3) | collective-permute-done | bytes 327712 | tf_op jit(solution)/shard_map/ppermute | solution.py:412
  51.5 5.0 %collective-permute-done.2.own1 = bf16[256,640]{1,0:T(8,128)(2,1)S(1)} collective-permute-done((bf16[256,640]{1,0:T(8,128)(2,1)S(1)}, bf16[256,640]{1,0:T(8,128)(2,1)S(1)}, u32[]{:S(2)}, u32[]{:S(2)}) %collective-permute-start.2) | collective-permute-done | bytes 327712 | tf_op jit(solution)/shard_map/ppermute | solution.py:411
  56.6 1.9 %collective-permute-start.4 = (bf16[256,640]{1,0:T(8,128)(2,1)S(1)}, bf16[256,640]{1,0:T(8,128)(2,1)S(1)}, u32[]{:S(2)}, u32[]{:S(2)}) collective-permute-start(bf16[256,640]{1,0:T(8,128)(2,1)S(1)} %broadcast_select_fusion), channel_id=1, source_target_pairs={{0,128},{32,416},{128,256},{160,32},{256,384},{288,160},{384,0},{4... | collective-permute-start | bytes 983048 | tf_op jit(solution)/shard_map/ppermute | solution.py:414
  58.5 1.9 %collective-permute-start.5 = (bf16[256,640]{1,0:T(8,128)(2,1)S(1)}, bf16[256,640]{1,0:T(8,128)(2,1)S(1)}, u32[]{:S(2)}, u32[]{:S(2)}) collective-permute-start(bf16[256,640]{1,0:T(8,128)(2,1)S(1)} %pad_maximum_fusion.own0), channel_id=1, source_target_pairs={{0,32},{32,0},{1,33},{33,1},{2,34},{34,2},{3,35},{35,3},{4,36},{36... | collective-permute-start | bytes 983048 | tf_op jit(solution)/shard_map/ppermute | solution.py:417
  60.5 2.4 %collective-permute-start.7 = (bf16[256,640]{1,0:T(8,128)(2,1)S(1)}, bf16[256,640]{1,0:T(8,128)(2,1)S(1)}, u32[]{:S(2)}, u32[]{:S(2)}) collective-permute-start(bf16[256,640]{1,0:T(8,128)(2,1)S(1)} %collective-permute-done.3.own3), channel_id=1, source_target_pairs={{0,32},{32,0},{1,33},{33,1},{2,34},{34,2},{3,35},{35,3},{4,36},{36... | collective-permute-start | bytes 983048 | tf_op jit(solution)/shard_map/ppermute | solution.py:418
  62.9 1.9 %collective-permute-start.6 = (bf16[256,640]{1,0:T(8,128)(2,1)S(1)}, bf16[256,640]{1,0:T(8,128)(2,1)S(1)}, u32[]{:S(2)}, u32[]{:S(2)}) collective-permute-start(bf16[256,640]{1,0:T(8,128)(2,1)S(1)} %collective-permute-done.2.own1), channel_id=1, source_target_pairs={{0,32},{32,0},{1,33},{33,1},{2,34},{34,2},{3,35},{35,3},{4,36},{36... | collective-permute-start | bytes 983048 | tf_op jit(solution)/shard_map/ppermute | solution.py:418
  64.8 0.0 collective-permute-done.4.own2
  64.8 2.4 %collective-permute-start.8 = (bf16[256,640]{1,0:T(8,128)(2,1)S(1)}, bf16[256,640]{1,0:T(8,128)(2,1)S(1)}, u32[]{:S(2)}, u32[]{:S(2)}) collective-permute-start(bf16[256,640]{1,0:T(8,128)(2,1)S(1)} %collective-permute-done.4.own2), channel_id=1, source_target_pairs={{0,32},{32,0},{1,33},{33,1},{2,34},{34,2},{3,35},{35,3},{4,36},{36... | collective-permute-start | bytes 983048 | tf_op jit(solution)/shard_map/ppermute | solution.py:418
  67.2 0.0 copy-done.1
  67.3 0.0 copy-done.2
  67.3 0.0 copy-done.3
  67.3 0.0 copy-done
  67.3 1.4 %lookup.1 = (f32[8,640]{1,0:T(8,128)S(1)}, f32[32,640]{1,0:T(8,128)S(1)}) custom-call(s32[4]{0:T(128)S(1)} %copy-done, f32[1000,640]{1,0:T(8,128)} %table_hbm.1, f32[1,640]{1,0:T(1,128)S(1)} %broadcast_in_dim.10.shift_ref, f32[1,640]{1,0:T(1,128)S(1)} %broadcast_in_dim.11.bias_ref, f32[32,640]{1,0:T(8,128)S(1)} %get-tuple-element.13.base_ref), custom_call_target="tpu_custom_call" | custom-call | tf_op jit(solution)/shard_map/lookup/pallas_call | solution.py:395
  68.7 0.0 collective-permute-done.5.other0
  68.7 0.0 collective-permute-done.7.other3
  68.7 0.0 collective-permute-done.6.other1
  68.7 0.0 collective-permute-done.8.other2
  68.7 0.0 all-to-all-done.weight_hbm
  68.7 6.2 %mix.1 = f32[8,72,128]{2,1,0:T(8,128)S(1)} custom-call(bf16[256,640]{1,0:T(8,128)(2,1)S(1)} %pad_maximum_fusion.own0, bf16[256,640]{1,0:T(8,128)(2,1)S(1)} %collective-permute-done.2.own1, bf16[256,640]{1,0:T(8,128)(2,1)S(1)} %collective-permute-done.3.own3, bf16[256,640]{1,0:T(8,128)(2,1)S(1)} %collective-permute-done.4.own2, ...), custom_call_target="tpu_custom_call" | custom-call | tf_op jit(solution)/shard_map/mix/pallas_call | solution.py:420
  75.0 10.2 %all_to_all.15.parts_ref = f32[8,72,128]{2,1,0:T(8,128)S(1)} all-to-all(f32[8,72,128]{2,1,0:T(8,128)S(1)} %mix.1), channel_id=1, replica_groups=mesh['gy'=4,'gx_0'=2,'gx_1'=2,'probe_0'=8,'probe_1'=4] {'gy','gx_1'}, dimensions={0} | all-to-all | bytes 589824 | tf_op jit(solution)/shard_map/all_to_all | solution.py:442
  85.2 0.7 step.1
  85.9 14.9 %all-to-all-start.2 = ((f32[64,1,128]{2,1,0:T(1,128)}), f32[64,1,128]{2,1,0:T(1,128)S(1)}, u32[]{:S(2)}, u32[]{:S(2)}) async-start(f32[64,1,128]{2,1,0:T(1,128)} %bitcast.1), calls=%async_computation.2 | async-start | bytes 65536 | tf_op jit(solution)/shard_map/all_to_all | solution.py:451
  100.8 2.9 %collective-permute-start.9 = (bf16[32,640]{1,0:T(8,128)(2,1)S(1)}, bf16[32,640]{1,0:T(8,128)(2,1)S(1)}, u32[]{:S(2)}, u32[]{:S(2)}) collective-permute-start(bf16[32,640]{1,0:T(8,128)(2,1)S(1)} %get-tuple-element.17.refs_1_), channel_id=1, source_target_pairs={{0,4},{4,0},{8,12},{12,8},{16,20},{20,16},{24,28},{28,24},{1,5},{5... | collective-permute-start | bytes 122888 | tf_op jit(solution)/shard_map/ppermute | solution.py:453
  103.7 2.1 %collective-permute-done.9.refs_2_ = bf16[32,640]{1,0:T(8,128)(2,1)S(1)} collective-permute-done((bf16[32,640]{1,0:T(8,128)(2,1)S(1)}, bf16[32,640]{1,0:T(8,128)(2,1)S(1)}, u32[]{:S(2)}, u32[]{:S(2)}) %collective-permute-start.9) | collective-permute-done | bytes 40992 | tf_op jit(solution)/shard_map/ppermute | solution.py:453
  105.8 5.9 %all-to-all-done.2 = f32[64,1,128]{2,1,0:T(1,128)S(1)} async-done(((f32[64,1,128]{2,1,0:T(1,128)}), f32[64,1,128]{2,1,0:T(1,128)S(1)}, u32[]{:S(2)}, u32[]{:S(2)}) %all-to-all-start.2) | async-done | bytes 32800 | tf_op jit(solution)/shard_map/all_to_all | solution.py:451
  111.7 0.7 final.1
  (8 shorter events, 0.1 us)
Async XLA Ops:
  0.6 66.6 %copy-start.1 = (f32[640]{0:T(1024)S(1)}, f32[640]{0:T(1024)}, u32[]{:S(2)}) copy-start(f32[640]{0:T(1024)} %param.12) | copy-start | bytes 7684
  0.6 66.6 %copy-start.2 = (f32[640]{0:T(1024)S(1)}, f32[640]{0:T(1024)}, u32[]{:S(2)}) copy-start(f32[640]{0:T(1024)} %param.13) | copy-start | bytes 7684
  0.7 66.6 %copy-start.3 = (f32[640]{0:T(1024)S(1)}, f32[640]{0:T(1024)}, u32[]{:S(2)}) copy-start(f32[640]{0:T(1024)} %param.15) | copy-start | bytes 7684
  0.7 66.6 %copy-start = (s32[4]{0:T(128)S(1)}, s32[4]{0:T(128)}, u32[]{:S(2)}) copy-start(s32[4]{0:T(128)} %step_ref.1) | copy-start | bytes 52
  2.8 66.0 %all-to-all-start = ((bf16[32,120,128]{2,1,0:T(8,128)(2,1)}), bf16[32,120,128]{2,1,0:T(8,128)(2,1)}, u32[]{:S(2)}, u32[]{:S(2)}) async-start(bf16[32,120,128]{2,1,0:T(8,128)(2,1)} %get-tuple-element.12), calls=%async_computation | async-start | bytes 1966080 | tf_op jit(solution)/shard_map/all_to_all | solution.py:407
  16.4 26.7 %collective-permute-start = (bf16[56,640]{1,0:T(8,128)(2,1)S(1)}, bf16[56,640]{1,0:T(8,128)(2,1)S(1)}, u32[]{:S(2)}, u32[]{:S(2)}) collective-permute-start(bf16[56,640]{1,0:T(8,128)(2,1)S(1)} %get-tuple-element.11), channel_id=1, source_target_pairs={{32,64},{64,32},{33,65},{65,33},{34,66},{66,34},{35,67},{67,35},{3... | collective-permute-start | bytes 215048 | tf_op jit(solution)/shard_map/ppermute | solution.py:405
  25.2 17.9 %collective-permute-start.1 = (bf16[8,640]{1,0:T(8,128)(2,1)S(1)}, bf16[8,640]{1,0:T(8,128)(2,1)S(1)}, u32[]{:S(2)}, u32[]{:S(2)}) collective-permute-start(bf16[8,640]{1,0:T(8,128)(2,1)S(1)} %slice.12), channel_id=1, source_target_pairs={{0,96},{96,0},{1,97},{97,1},{2,98},{98,2},{3,99},{99,3},{4,100},{1... | collective-permute-start | bytes 30728 | tf_op jit(solution)/shard_map/ppermute | solution.py:406
  43.1 8.4 %collective-permute-start.3 = (bf16[256,640]{1,0:T(8,128)(2,1)S(1)}, bf16[256,640]{1,0:T(8,128)(2,1)S(1)}, u32[]{:S(2)}, u32[]{:S(2)}) collective-permute-start(bf16[256,640]{1,0:T(8,128)(2,1)S(1)} %pad_maximum_fusion.own0), channel_id=1, source_target_pairs={{0,384},{128,0},{256,128},{384,256},{1,385},{129,1},{257,129},{385... | collective-permute-start | bytes 983048 | tf_op jit(solution)/shard_map/ppermute | solution.py:412
  47.5 9.0 %collective-permute-start.2 = (bf16[256,640]{1,0:T(8,128)(2,1)S(1)}, bf16[256,640]{1,0:T(8,128)(2,1)S(1)}, u32[]{:S(2)}, u32[]{:S(2)}) collective-permute-start(bf16[256,640]{1,0:T(8,128)(2,1)S(1)} %pad_maximum_fusion.own0), channel_id=1, source_target_pairs={{0,128},{128,256},{256,384},{384,0},{1,129},{129,257},{257,385},{3... | collective-permute-start | bytes 983048 | tf_op jit(solution)/shard_map/ppermute | solution.py:411
  56.6 8.2 %collective-permute-start.4 = (bf16[256,640]{1,0:T(8,128)(2,1)S(1)}, bf16[256,640]{1,0:T(8,128)(2,1)S(1)}, u32[]{:S(2)}, u32[]{:S(2)}) collective-permute-start(bf16[256,640]{1,0:T(8,128)(2,1)S(1)} %broadcast_select_fusion), channel_id=1, source_target_pairs={{0,128},{32,416},{128,256},{160,32},{256,384},{288,160},{384,0},{4... | collective-permute-start | bytes 983048 | tf_op jit(solution)/shard_map/ppermute | solution.py:414
  58.5 10.1 %collective-permute-start.5 = (bf16[256,640]{1,0:T(8,128)(2,1)S(1)}, bf16[256,640]{1,0:T(8,128)(2,1)S(1)}, u32[]{:S(2)}, u32[]{:S(2)}) collective-permute-start(bf16[256,640]{1,0:T(8,128)(2,1)S(1)} %pad_maximum_fusion.own0), channel_id=1, source_target_pairs={{0,32},{32,0},{1,33},{33,1},{2,34},{34,2},{3,35},{35,3},{4,36},{36... | collective-permute-start | bytes 983048 | tf_op jit(solution)/shard_map/ppermute | solution.py:417
  60.5 8.2 %collective-permute-start.7 = (bf16[256,640]{1,0:T(8,128)(2,1)S(1)}, bf16[256,640]{1,0:T(8,128)(2,1)S(1)}, u32[]{:S(2)}, u32[]{:S(2)}) collective-permute-start(bf16[256,640]{1,0:T(8,128)(2,1)S(1)} %collective-permute-done.3.own3), channel_id=1, source_target_pairs={{0,32},{32,0},{1,33},{33,1},{2,34},{34,2},{3,35},{35,3},{4,36},{36... | collective-permute-start | bytes 983048 | tf_op jit(solution)/shard_map/ppermute | solution.py:418
  62.9 5.8 %collective-permute-start.6 = (bf16[256,640]{1,0:T(8,128)(2,1)S(1)}, bf16[256,640]{1,0:T(8,128)(2,1)S(1)}, u32[]{:S(2)}, u32[]{:S(2)}) collective-permute-start(bf16[256,640]{1,0:T(8,128)(2,1)S(1)} %collective-permute-done.2.own1), channel_id=1, source_target_pairs={{0,32},{32,0},{1,33},{33,1},{2,34},{34,2},{3,35},{35,3},{4,36},{36... | collective-permute-start | bytes 983048 | tf_op jit(solution)/shard_map/ppermute | solution.py:418
  64.8 3.9 %collective-permute-start.8 = (bf16[256,640]{1,0:T(8,128)(2,1)S(1)}, bf16[256,640]{1,0:T(8,128)(2,1)S(1)}, u32[]{:S(2)}, u32[]{:S(2)}) collective-permute-start(bf16[256,640]{1,0:T(8,128)(2,1)S(1)} %collective-permute-done.4.own2), channel_id=1, source_target_pairs={{0,32},{32,0},{1,33},{33,1},{2,34},{34,2},{3,35},{35,3},{4,36},{36... | collective-permute-start | bytes 983048 | tf_op jit(solution)/shard_map/ppermute | solution.py:418
  85.9 25.8 %all-to-all-start.2 = ((f32[64,1,128]{2,1,0:T(1,128)}), f32[64,1,128]{2,1,0:T(1,128)S(1)}, u32[]{:S(2)}, u32[]{:S(2)}) async-start(f32[64,1,128]{2,1,0:T(1,128)} %bitcast.1), calls=%async_computation.2 | async-start | bytes 65536 | tf_op jit(solution)/shard_map/all_to_all | solution.py:451
  100.8 5.0 %collective-permute-start.9 = (bf16[32,640]{1,0:T(8,128)(2,1)S(1)}, bf16[32,640]{1,0:T(8,128)(2,1)S(1)}, u32[]{:S(2)}, u32[]{:S(2)}) collective-permute-start(bf16[32,640]{1,0:T(8,128)(2,1)S(1)} %get-tuple-element.17.refs_1_), channel_id=1, source_target_pairs={{0,4},{4,0},{8,12},{12,8},{16,20},{20,16},{24,28},{28,24},{1,5},{5... | collective-permute-start | bytes 122888 | tf_op jit(solution)/shard_map/ppermute | solution.py:453

commit v8 on v7

--- a/solution.py
+++ b/solution.py
@@ -402,20 +402,24 @@
         name="lookup",
     )(timesteps, far(time_table), gn_shift[None], conv_bias[None], base)
 
-    facing = lax.ppermute(rim, GX, [(1, 2), (2, 1)])
-    outer = lax.ppermute(rim[48:56], GX, [(0, 3), (3, 0)])
+    across = [(a * 2 + b, (1 - a) * 2 + 1 - b) for a in range(2) for b in range(2)]
+    facing = lax.ppermute(rim, GX, across)
     weights = lax.all_to_all(wsend, PROBE, 0, 0, tiled=True)
-    block = jnp.concatenate([main, facing[:48], facing[48:] + outer, rim[48:56]], axis=0)
+    block = jnp.concatenate([main, facing, rim[48:56]], axis=0)
     down = [(i, (i + 1) % 4) for i in range(4)]
     up = [(i, (i + 3) % 4) for i in range(4)]
     above = lax.ppermute(block, "gy", down)
     below = lax.ppermute(block, "gy", up)
+    lower = lax.axis_index("gx_1") == 0
     onward = [(x * 2 + c, (x + 1 - 2 * c) % 4 * 2 + c) for x in range(4) for c in range(2)]
-    beyond = lax.ppermute(jnp.where(lax.axis_index("gx_1") == 0, above, below), ("gy", "gx_1"), onward)
+    crossing = [(x * 2 + c, (x - 1 + 2 * c) % 4 * 2 + 1 - c) for x in range(4) for c in range(2)]
+    beyond = lax.ppermute(jnp.where(lower, above, below), ("gy", "gx_1"), onward)
+    crossed = lax.ppermute(jnp.where(lower, below, above), ("gy", "gx_1"), crossing)
     own = [block, above, below, beyond]
     swap = [(0, 1), (1, 0)]
     other = [lax.ppermute(block, "gx_1", swap)]
-    other += [lax.ppermute(tile, "gx_1", swap) for tile in own[1:]]
+    other += [lax.ppermute(tile, "gx_1", swap) for tile in (above, below)]
+    other.append(crossed)
 
     partial = pl.pallas_call(
         mix_kernel,

time: 113 us -> 120 us (1.062)
  waiting for transfers between devices: 32.3 us -> 39.5 us
  starting transfers between devices: 57.7 us -> 55.5 us
  blocking collectives: 10.2 us -> 11.9 us
    ppermute x6 -> x5, waiting for transfers between devices: 17.3 us -> 23.8 us  [the longest x1 21.2 us: body(): facing = lax.ppermute(rim, GX, across)]
    all_to_all x1, starting transfers between devices: 14.9 us -> 9.71 us  [body(): lax.all_to_all(mass.reshape(64, 1, LANES), ('gx_0',) + PROBE, 0, 0, tiled...]
    ppermute x6 -> x5, starting transfers between devices: 18.1 us -> 20.7 us  [the longest x1 8.78 us: body(): facing = lax.ppermute(rim, GX, across)]
    all_to_all x1, blocking collectives: 10.2 us -> 11.9 us  [body(): partial = lax.all_to_all(partial, ('gy', 'gx_1'), 0, 0, tiled=True)]
  transfers between devices with their start and end apart: 12 -> 11, of which waited for: 5 -> 6; matrix products, arithmetic and copies ran while one was open for 0% -> 0% of each run, Pallas kernels for 1% -> 1%
where the time goes in v8:
time: 120 us; the launch traced here: 119 us
  starting transfers between devices  55.5 us (46%)
  waiting for transfers between devices  39.5 us (33%)
  blocking collectives  11.9 us (10%)
  Pallas kernels  11.1 us (9%)
    ppermute x1, waiting for transfers between devices, body(): facing = lax.ppermute(rim, GX, across)  21.2 us
    all_to_all x1, starting transfers between devices, body(): weights = lax.all_to_all(wsend, PROBE, 0, 0, tiled=True)  13.6 us
    all_to_all x1, blocking collectives, body(): partial = lax.all_to_all(partial, ('gy', 'gx_1'), 0, 0, tiled=True)  11.9 us
    all_to_all x1, starting transfers between devices, body(): lax.all_to_all(mass.reshape(64, 1, LANES), ('gx_0',) + PROBE, 0, 0, tiled...  9.71 us
    ppermute x1, starting transfers between devices, body(): facing = lax.ppermute(rim, GX, across)  8.78 us
    pallas_call x1, Pallas kernels, body(): pl.pallas_call(mix_kernel, out_shape=shape((8, 72, LANES), F32), in_specs...  6.21 us
    all_to_all x1, waiting for transfers between devices, body(): lax.all_to_all(mass.reshape(64, 1, LANES), ('gx_0',) + PROBE, 0, 0, tiled...  5.86 us
    ppermute x2, starting transfers between devices, body(): other += [lax.ppermute(tile, 'gx_1', swap) for tile in (above, below)]  5.06 us
  transfers between devices with their start and end apart: 11, of which 6 were waited for; matrix products, arithmetic and copies ran while one was open for 0% of the time, Pallas kernels for 1%

profile of v8, /device:TPU:1, one launch (start us, length us, event | category | flops | bytes accessed | tf_op | source)
XLA Modules:
  0.0 119.0 jit_solution(6840832714091495402)
XLA Ops:
  0.6 0.0 copy-start.1
  0.6 0.0 copy-start.2
  0.7 0.0 copy-start.3
  0.7 0.0 copy-start
  0.7 2.1 %pack.1 = (bf16[192,640]{1,0:T(8,128)(2,1)S(1)}, bf16[56,640]{1,0:T(8,128)(2,1)S(1)}, f32[32,640]{1,0:T(8,128)S(1)}, bf16[32,120,128]{2,1,0:T(8,128)(2,1)}) custom-call(bf16[9,20,640]{2,1,0:T(8,128)(2,1)} %weight_hbm.1, bf16[4,4,4,640]{3,2,1,0:T(4,128)(2,1)} %state_hbm.1, s32[2,4,4,4,640]{4,3,2,1,0:T(4,128)} %signs_hbm.1), custom_call_target="tpu_custom_call" | custom-call | tf_op jit(solution)/shard_map/pack/pallas_call | solution.py:369
  2.8 13.6 %all-to-all-start = ((bf16[32,120,128]{2,1,0:T(8,128)(2,1)}), bf16[32,120,128]{2,1,0:T(8,128)(2,1)}, u32[]{:S(2)}, u32[]{:S(2)}) async-start(bf16[32,120,128]{2,1,0:T(8,128)(2,1)} %get-tuple-element.12), calls=%async_computation | async-start | bytes 1966080 | tf_op jit(solution)/shard_map/all_to_all | solution.py:407
  16.4 8.8 %collective-permute-start = (bf16[56,640]{1,0:T(8,128)(2,1)S(1)}, bf16[56,640]{1,0:T(8,128)(2,1)S(1)}, u32[]{:S(2)}, u32[]{:S(2)}) collective-permute-start(bf16[56,640]{1,0:T(8,128)(2,1)S(1)} %get-tuple-element.11), channel_id=1, source_target_pairs={{0,96},{32,64},{64,32},{96,0},{1,97},{33,65},{65,33},{97,1},{2,98}... | collective-permute-start | bytes 215048 | tf_op jit(solution)/shard_map/ppermute | solution.py:406
  25.2 21.2 %collective-permute-done = bf16[56,640]{1,0:T(8,128)(2,1)S(1)} collective-permute-done((bf16[56,640]{1,0:T(8,128)(2,1)S(1)}, bf16[56,640]{1,0:T(8,128)(2,1)S(1)}, u32[]{:S(2)}, u32[]{:S(2)}) %collective-permute-start) | collective-permute-done | bytes 71712 | tf_op jit(solution)/shard_map/ppermute | solution.py:406
  46.4 4.4 %collective-permute-start.2 = (bf16[256,640]{1,0:T(8,128)(2,1)S(1)}, bf16[256,640]{1,0:T(8,128)(2,1)S(1)}, u32[]{:S(2)}, u32[]{:S(2)}) collective-permute-start(bf16[256,640]{1,0:T(8,128)(2,1)S(1)} %pad_maximum_fusion.own0), channel_id=1, source_target_pairs={{0,384},{128,0},{256,128},{384,256},{1,385},{129,1},{257,129},{385... | collective-permute-start | bytes 983048 | tf_op jit(solution)/shard_map/ppermute | solution.py:412
  50.8 1.9 %collective-permute-start.1 = (bf16[256,640]{1,0:T(8,128)(2,1)S(1)}, bf16[256,640]{1,0:T(8,128)(2,1)S(1)}, u32[]{:S(2)}, u32[]{:S(2)}) collective-permute-start(bf16[256,640]{1,0:T(8,128)(2,1)S(1)} %pad_maximum_fusion.own0), channel_id=1, source_target_pairs={{0,128},{128,256},{256,384},{384,0},{1,129},{129,257},{257,385},{3... | collective-permute-start | bytes 983048 | tf_op jit(solution)/shard_map/ppermute | solution.py:411
  52.8 2.3 %collective-permute-start.4 = (bf16[256,640]{1,0:T(8,128)(2,1)S(1)}, bf16[256,640]{1,0:T(8,128)(2,1)S(1)}, u32[]{:S(2)}, u32[]{:S(2)}) collective-permute-start(bf16[256,640]{1,0:T(8,128)(2,1)S(1)} %pad_maximum_fusion.own0), channel_id=1, source_target_pairs={{0,32},{32,0},{1,33},{33,1},{2,34},{34,2},{3,35},{35,3},{4,36},{36... | collective-permute-start | bytes 983048 | tf_op jit(solution)/shard_map/ppermute | solution.py:420
  55.1 2.7 %collective-permute-done.2.own3 = bf16[256,640]{1,0:T(8,128)(2,1)S(1)} collective-permute-done((bf16[256,640]{1,0:T(8,128)(2,1)S(1)}, bf16[256,640]{1,0:T(8,128)(2,1)S(1)}, u32[]{:S(2)}, u32[]{:S(2)}) %collective-permute-start.2) | collective-permute-done | bytes 327712 | tf_op jit(solution)/shard_map/ppermute | solution.py:412
  57.8 5.0 %collective-permute-done.1.own1 = bf16[256,640]{1,0:T(8,128)(2,1)S(1)} collective-permute-done((bf16[256,640]{1,0:T(8,128)(2,1)S(1)}, bf16[256,640]{1,0:T(8,128)(2,1)S(1)}, u32[]{:S(2)}, u32[]{:S(2)}) %collective-permute-start.1) | collective-permute-done | bytes 327712 | tf_op jit(solution)/shard_map/ppermute | solution.py:411
  62.8 0.1 broadcast_select_fusion
  62.9 1.9 %collective-permute-start.7 = (bf16[256,640]{1,0:T(8,128)(2,1)S(1)}, bf16[256,640]{1,0:T(8,128)(2,1)S(1)}, u32[]{:S(2)}, u32[]{:S(2)}) collective-permute-start(bf16[256,640]{1,0:T(8,128)(2,1)S(1)} %get-tuple-element.18), channel_id=1, source_target_pairs={{0,416},{32,128},{128,32},{160,256},{256,160},{288,384},{384,288},... | collective-permute-start | bytes 983048 | tf_op jit(solution)/shard_map/ppermute | solution.py:417
  64.8 3.1 %collective-permute-start.6 = (bf16[256,640]{1,0:T(8,128)(2,1)S(1)}, bf16[256,640]{1,0:T(8,128)(2,1)S(1)}, u32[]{:S(2)}, u32[]{:S(2)}) collective-permute-start(bf16[256,640]{1,0:T(8,128)(2,1)S(1)} %collective-permute-done.2.own3), channel_id=1, source_target_pairs={{0,32},{32,0},{1,33},{33,1},{2,34},{34,2},{3,35},{35,3},{4,36},{36... | collective-permute-start | bytes 983048 | tf_op jit(solution)/shard_map/ppermute | solution.py:421
  68.0 1.9 %collective-permute-start.5 = (bf16[256,640]{1,0:T(8,128)(2,1)S(1)}, bf16[256,640]{1,0:T(8,128)(2,1)S(1)}, u32[]{:S(2)}, u32[]{:S(2)}) collective-permute-start(bf16[256,640]{1,0:T(8,128)(2,1)S(1)} %collective-permute-done.1.own1), channel_id=1, source_target_pairs={{0,32},{32,0},{1,33},{33,1},{2,34},{34,2},{3,35},{35,3},{4,36},{36... | collective-permute-start | bytes 983048 | tf_op jit(solution)/shard_map/ppermute | solution.py:421
  69.9 5.0 %collective-permute-start.3 = (bf16[256,640]{1,0:T(8,128)(2,1)S(1)}, bf16[256,640]{1,0:T(8,128)(2,1)S(1)}, u32[]{:S(2)}, u32[]{:S(2)}) collective-permute-start(bf16[256,640]{1,0:T(8,128)(2,1)S(1)} %get-tuple-element.19), channel_id=1, source_target_pairs={{0,128},{32,416},{128,256},{160,32},{256,384},{288,160},{384,0},{4... | collective-permute-start | bytes 983048 | tf_op jit(solution)/shard_map/ppermute | solution.py:416
  74.9 0.0 copy-done.1
  74.9 0.0 copy-done.2
  74.9 0.0 copy-done.3
  74.9 0.0 copy-done
  75.0 1.4 %lookup.1 = (f32[8,640]{1,0:T(8,128)S(1)}, f32[32,640]{1,0:T(8,128)S(1)}) custom-call(s32[4]{0:T(128)S(1)} %copy-done, f32[1000,640]{1,0:T(8,128)} %table_hbm.1, f32[1,640]{1,0:T(1,128)S(1)} %broadcast_in_dim.10.shift_ref, f32[1,640]{1,0:T(1,128)S(1)} %broadcast_in_dim.11.bias_ref, f32[32,640]{1,0:T(8,128)S(1)} %get-tuple-element.13.base_ref), custom_call_target="tpu_custom_call" | custom-call | tf_op jit(solution)/shard_map/lookup/pallas_call | solution.py:395
  76.3 0.0 collective-permute-done.4.other0
  76.3 0.0 collective-permute-done.6.other3
  76.3 0.0 collective-permute-done.5.other1
  76.4 0.0 collective-permute-done.7.other2
  76.4 2.5 %collective-permute-done.3.own2 = bf16[256,640]{1,0:T(8,128)(2,1)S(1)} collective-permute-done((bf16[256,640]{1,0:T(8,128)(2,1)S(1)}, bf16[256,640]{1,0:T(8,128)(2,1)S(1)}, u32[]{:S(2)}, u32[]{:S(2)}) %collective-permute-start.3) | collective-permute-done | bytes 327712 | tf_op jit(solution)/shard_map/ppermute | solution.py:416
  78.9 0.0 all-to-all-done.weight_hbm
  78.9 6.2 %mix.1 = f32[8,72,128]{2,1,0:T(8,128)S(1)} custom-call(bf16[256,640]{1,0:T(8,128)(2,1)S(1)} %pad_maximum_fusion.own0, bf16[256,640]{1,0:T(8,128)(2,1)S(1)} %collective-permute-done.1.own1, bf16[256,640]{1,0:T(8,128)(2,1)S(1)} %collective-permute-done.2.own3, bf16[256,640]{1,0:T(8,128)(2,1)S(1)} %collective-permute-done.3.own2, ...), custom_call_target="tpu_custom_call" | custom-call | tf_op jit(solution)/shard_map/mix/pallas_call | solution.py:424
  85.1 11.9 %all_to_all.15.parts_ref = f32[8,72,128]{2,1,0:T(8,128)S(1)} all-to-all(f32[8,72,128]{2,1,0:T(8,128)S(1)} %mix.1), channel_id=1, replica_groups=mesh['gy'=4,'gx_0'=2,'gx_1'=2,'probe_0'=8,'probe_1'=4] {'gy','gx_1'}, dimensions={0} | all-to-all | bytes 589824 | tf_op jit(solution)/shard_map/all_to_all | solution.py:446
  97.0 0.7 step.1
  97.7 9.7 %all-to-all-start.2 = ((f32[64,1,128]{2,1,0:T(1,128)}), f32[64,1,128]{2,1,0:T(1,128)S(1)}, u32[]{:S(2)}, u32[]{:S(2)}) async-start(f32[64,1,128]{2,1,0:T(1,128)} %bitcast.1), calls=%async_computation.2 | async-start | bytes 65536 | tf_op jit(solution)/shard_map/all_to_all | solution.py:455
  107.4 2.9 %collective-permute-start.8 = (bf16[32,640]{1,0:T(8,128)(2,1)S(1)}, bf16[32,640]{1,0:T(8,128)(2,1)S(1)}, u32[]{:S(2)}, u32[]{:S(2)}) collective-permute-start(bf16[32,640]{1,0:T(8,128)(2,1)S(1)} %get-tuple-element.17.refs_1_), channel_id=1, source_target_pairs={{0,4},{4,0},{8,12},{12,8},{16,20},{20,16},{24,28},{28,24},{1,5},{5... | collective-permute-start | bytes 122888 | tf_op jit(solution)/shard_map/ppermute | solution.py:457
  110.3 2.1 %collective-permute-done.8.refs_2_ = bf16[32,640]{1,0:T(8,128)(2,1)S(1)} collective-permute-done((bf16[32,640]{1,0:T(8,128)(2,1)S(1)}, bf16[32,640]{1,0:T(8,128)(2,1)S(1)}, u32[]{:S(2)}, u32[]{:S(2)}) %collective-permute-start.8) | collective-permute-done | bytes 40992 | tf_op jit(solution)/shard_map/ppermute | solution.py:457
  112.4 5.9 %all-to-all-done.2 = f32[64,1,128]{2,1,0:T(1,128)S(1)} async-done(((f32[64,1,128]{2,1,0:T(1,128)}), f32[64,1,128]{2,1,0:T(1,128)S(1)}, u32[]{:S(2)}, u32[]{:S(2)}) %all-to-all-start.2) | async-done | bytes 32800 | tf_op jit(solution)/shard_map/all_to_all | solution.py:455
  118.3 0.7 final.1
  (5 shorter events, 0.0 us)
Async XLA Ops:
  0.6 74.2 %copy-start.1 = (f32[640]{0:T(1024)S(1)}, f32[640]{0:T(1024)}, u32[]{:S(2)}) copy-start(f32[640]{0:T(1024)} %param.12) | copy-start | bytes 7684
  0.6 74.3 %copy-start.2 = (f32[640]{0:T(1024)S(1)}, f32[640]{0:T(1024)}, u32[]{:S(2)}) copy-start(f32[640]{0:T(1024)} %param.13) | copy-start | bytes 7684
  0.7 74.3 %copy-start.3 = (f32[640]{0:T(1024)S(1)}, f32[640]{0:T(1024)}, u32[]{:S(2)}) copy-start(f32[640]{0:T(1024)} %param.15) | copy-start | bytes 7684
  0.7 74.3 %copy-start = (s32[4]{0:T(128)S(1)}, s32[4]{0:T(128)}, u32[]{:S(2)}) copy-start(s32[4]{0:T(128)} %step_ref.1) | copy-start | bytes 52
  2.8 76.1 %all-to-all-start = ((bf16[32,120,128]{2,1,0:T(8,128)(2,1)}), bf16[32,120,128]{2,1,0:T(8,128)(2,1)}, u32[]{:S(2)}, u32[]{:S(2)}) async-start(bf16[32,120,128]{2,1,0:T(8,128)(2,1)} %get-tuple-element.12), calls=%async_computation | async-start | bytes 1966080 | tf_op jit(solution)/shard_map/all_to_all | solution.py:407
  16.4 30.0 %collective-permute-start = (bf16[56,640]{1,0:T(8,128)(2,1)S(1)}, bf16[56,640]{1,0:T(8,128)(2,1)S(1)}, u32[]{:S(2)}, u32[]{:S(2)}) collective-permute-start(bf16[56,640]{1,0:T(8,128)(2,1)S(1)} %get-tuple-element.11), channel_id=1, source_target_pairs={{0,96},{32,64},{64,32},{96,0},{1,97},{33,65},{65,33},{97,1},{2,98}... | collective-permute-start | bytes 215048 | tf_op jit(solution)/shard_map/ppermute | solution.py:406
  46.4 11.3 %collective-permute-start.2 = (bf16[256,640]{1,0:T(8,128)(2,1)S(1)}, bf16[256,640]{1,0:T(8,128)(2,1)S(1)}, u32[]{:S(2)}, u32[]{:S(2)}) collective-permute-start(bf16[256,640]{1,0:T(8,128)(2,1)S(1)} %pad_maximum_fusion.own0), channel_id=1, source_target_pairs={{0,384},{128,0},{256,128},{384,256},{1,385},{129,1},{257,129},{385... | collective-permute-start | bytes 983048 | tf_op jit(solution)/shard_map/ppermute | solution.py:412
  50.8 12.0 %collective-permute-start.1 = (bf16[256,640]{1,0:T(8,128)(2,1)S(1)}, bf16[256,640]{1,0:T(8,128)(2,1)S(1)}, u32[]{:S(2)}, u32[]{:S(2)}) collective-permute-start(bf16[256,640]{1,0:T(8,128)(2,1)S(1)} %pad_maximum_fusion.own0), channel_id=1, source_target_pairs={{0,128},{128,256},{256,384},{384,0},{1,129},{129,257},{257,385},{3... | collective-permute-start | bytes 983048 | tf_op jit(solution)/shard_map/ppermute | solution.py:411
  52.8 23.6 %collective-permute-start.4 = (bf16[256,640]{1,0:T(8,128)(2,1)S(1)}, bf16[256,640]{1,0:T(8,128)(2,1)S(1)}, u32[]{:S(2)}, u32[]{:S(2)}) collective-permute-start(bf16[256,640]{1,0:T(8,128)(2,1)S(1)} %pad_maximum_fusion.own0), channel_id=1, source_target_pairs={{0,32},{32,0},{1,33},{33,1},{2,34},{34,2},{3,35},{35,3},{4,36},{36... | collective-permute-start | bytes 983048 | tf_op jit(solution)/shard_map/ppermute | solution.py:420
  62.9 13.5 %collective-permute-start.7 = (bf16[256,640]{1,0:T(8,128)(2,1)S(1)}, bf16[256,640]{1,0:T(8,128)(2,1)S(1)}, u32[]{:S(2)}, u32[]{:S(2)}) collective-permute-start(bf16[256,640]{1,0:T(8,128)(2,1)S(1)} %get-tuple-element.18), channel_id=1, source_target_pairs={{0,416},{32,128},{128,32},{160,256},{256,160},{288,384},{384,288},... | collective-permute-start | bytes 983048 | tf_op jit(solution)/shard_map/ppermute | solution.py:417
  64.8 11.5 %collective-permute-start.6 = (bf16[256,640]{1,0:T(8,128)(2,1)S(1)}, bf16[256,640]{1,0:T(8,128)(2,1)S(1)}, u32[]{:S(2)}, u32[]{:S(2)}) collective-permute-start(bf16[256,640]{1,0:T(8,128)(2,1)S(1)} %collective-permute-done.2.own3), channel_id=1, source_target_pairs={{0,32},{32,0},{1,33},{33,1},{2,34},{34,2},{3,35},{35,3},{4,36},{36... | collective-permute-start | bytes 983048 | tf_op jit(solution)/shard_map/ppermute | solution.py:421
  68.0 8.4 %collective-permute-start.5 = (bf16[256,640]{1,0:T(8,128)(2,1)S(1)}, bf16[256,640]{1,0:T(8,128)(2,1)S(1)}, u32[]{:S(2)}, u32[]{:S(2)}) collective-permute-start(bf16[256,640]{1,0:T(8,128)(2,1)S(1)} %collective-permute-done.1.own1), channel_id=1, source_target_pairs={{0,32},{32,0},{1,33},{33,1},{2,34},{34,2},{3,35},{35,3},{4,36},{36... | collective-permute-start | bytes 983048 | tf_op jit(solution)/shard_map/ppermute | solution.py:421
  69.9 9.0 %collective-permute-start.3 = (bf16[256,640]{1,0:T(8,128)(2,1)S(1)}, bf16[256,640]{1,0:T(8,128)(2,1)S(1)}, u32[]{:S(2)}, u32[]{:S(2)}) collective-permute-start(bf16[256,640]{1,0:T(8,128)(2,1)S(1)} %get-tuple-element.19), channel_id=1, source_target_pairs={{0,128},{32,416},{128,256},{160,32},{256,384},{288,160},{384,0},{4... | collective-permute-start | bytes 983048 | tf_op jit(solution)/shard_map/ppermute | solution.py:416
  97.7 20.6 %all-to-all-start.2 = ((f32[64,1,128]{2,1,0:T(1,128)}), f32[64,1,128]{2,1,0:T(1,128)S(1)}, u32[]{:S(2)}, u32[]{:S(2)}) async-start(f32[64,1,128]{2,1,0:T(1,128)} %bitcast.1), calls=%async_computation.2 | async-start | bytes 65536 | tf_op jit(solution)/shard_map/all_to_all | solution.py:455
  107.4 5.0 %collective-permute-start.8 = (bf16[32,640]{1,0:T(8,128)(2,1)S(1)}, bf16[32,640]{1,0:T(8,128)(2,1)S(1)}, u32[]{:S(2)}, u32[]{:S(2)}) collective-permute-start(bf16[32,640]{1,0:T(8,128)(2,1)S(1)} %get-tuple-element.17.refs_1_), channel_id=1, source_target_pairs={{0,4},{4,0},{8,12},{12,8},{16,20},{20,16},{24,28},{28,24},{1,5},{5... | collective-permute-start | bytes 122888 | tf_op jit(solution)/shard_map/ppermute | solution.py:457

commit v9 on v8

--- a/solution.py
+++ b/solution.py
@@ -258,8 +258,6 @@
                 slope_ref[pl.ds(pl.multiple_of(gr * 64 + two * 16, 16), 16), ln] = out
         return carry
 
-    lax.fori_loop(0, 16, grid_row, 0)
-
     for o in range(blocks):
         _, pre, sig = fields(edges[o].reshape(8, 8, LANES), o, 8)
         edges[o] = (pre * sig).reshape(64, LANES)
@@ -268,15 +266,31 @@
 
     taps = [pair_of(index) for index in range(PAIRS)]
 
-    def lhs_row(gr, carry):
+    def lhs_row(gr):
         for index, (tap, ob) in enumerate(taps):
             dy, dx = lax.div(tap, 3), lax.rem(tap, 3)
             at = spot(gr + 2 - dy, 2 - dx)
             value = ug[jnp.minimum(ob, blocks - 1), pl.ds(at, 64), :]
             lhs_ref[pl.ds(pl.multiple_of(gr * 64, 64), 64), lane_block(index)] = value.astype(BF16)
-        return carry
-
-    lax.fori_loop(0, 16, lhs_row, 0)
+
+    load.wait()
+    each = weight_ref.shape[1]
+    for source in range(weight_ref.shape[0]):
+        wf[source * each : (source + 1) * each, :] = weight_ref[source].astype(F32)
+    for index in range(PAIRS):
+        wc[:, lane_block(index)] = wf[pl.ds(index, chans, stride=PAIRS), :].astype(BF16)
+
+    def grid_rows(quad, total):
+        for sub in range(4):
+            lhs_row(quad * 4 + sub)
+        span = pl.ds(pl.multiple_of(quad * 256, 256), 256)
+        value = lax.dot_general(lhs_ref[span, :], wc[...], (((1,), (1,)), ((), ())), preferred_element_type=F32)
+        for sub in range(4):
+            grid_row(quad * 4 + sub, 0)
+        value = value * slope_ref[span, :].astype(F32)
+        return total + jnp.sum(value.reshape(32, 8, chans), axis=0)
+
+    total = lax.fori_loop(0, 4, grid_rows, jnp.zeros((8, chans), F32))
 
     for index, (tap, ob) in enumerate(taps):
         dy, dx = lax.div(tap, 3), lax.rem(tap, 3)
@@ -287,21 +301,6 @@
                 for o in range(blocks):
                     rows_ref[to : to + 16, lane_block(o)] = xg[o, pl.ds(at, 16), :].astype(BF16)
 
-    load.wait()
-    each = weight_ref.shape[1]
-    for source in range(weight_ref.shape[0]):
-        wf[source * each : (source + 1) * each, :] = weight_ref[source].astype(F32)
-    for index in range(PAIRS):
-        wc[:, lane_block(index)] = wf[pl.ds(index, chans, stride=PAIRS), :].astype(BF16)
-
-    chunk = 512
-    total = jnp.zeros((8, chans), F32)
-    for start in range(0, lhs_ref.shape[0], chunk):
-        value = lax.dot_general(
-            lhs_ref[start : start + chunk, :], wc[...], (((1,), (1,)), ((), ())), preferred_element_type=F32
-        )
-        value = value * slope_ref[start : start + chunk, :].astype(F32)
-        total = total + jnp.sum(value.reshape(chunk // 8, 8, chans), axis=0)
     lanes = total[:, lane_block(0)]
     for o in range(1, blocks):
         lanes = lanes + total[:, lane_block(o)]

time: 120 us -> 120 us (level)
  no operation moved by 1% of the time
where the time goes in v9:
time: 120 us; the launch traced here: 119 us
  starting transfers between devices  55.5 us (46%)
  waiting for transfers between devices  39.5 us (33%)
  blocking collectives  11.9 us (10%)
  Pallas kernels  11.3 us (9%)
    ppermute x1, waiting for transfers between devices, body(): facing = lax.ppermute(rim, GX, across)  21.2 us
    all_to_all x1, starting transfers between devices, body(): weights = lax.all_to_all(wsend, PROBE, 0, 0, tiled=True)  13.6 us
    all_to_all x1, blocking collectives, body(): partial = lax.all_to_all(partial, ('gy', 'gx_1'), 0, 0, tiled=True)  11.9 us
    all_to_all x1, starting transfers between devices, body(): lax.all_to_all(mass.reshape(64, 1, LANES), ('gx_0',) + PROBE, 0, 0, tiled...  9.72 us
    ppermute x1, starting transfers between devices, body(): facing = lax.ppermute(rim, GX, across)  8.78 us
    pallas_call x1, Pallas kernels, body(): pl.pallas_call(mix_kernel, out_shape=shape((8, 72, LANES), F32), in_specs...  6.47 us
    all_to_all x1, waiting for transfers between devices, body(): lax.all_to_all(mass.reshape(64, 1, LANES), ('gx_0',) + PROBE, 0, 0, tiled...  5.86 us
    ppermute x2, starting transfers between devices, body(): other += [lax.ppermute(tile, 'gx_1', swap) for tile in (above, below)]  5.06 us
  transfers between devices with their start and end apart: 11, of which 6 were waited for; matrix products, arithmetic and copies ran while one was open for 0% of the time, Pallas kernels for 1%

profile of v9, /device:TPU:1, one launch (start us, length us, event | category | flops | bytes accessed | tf_op | source)
XLA Modules:
  0.0 119.3 jit_solution(14910787720961259996)
XLA Ops:
  0.6 0.0 copy-start.1
  0.6 0.0 copy-start.2
  0.7 0.0 copy-start.3
  0.7 0.0 copy-start
  0.7 2.1 %pack.1 = (bf16[192,640]{1,0:T(8,128)(2,1)S(1)}, bf16[56,640]{1,0:T(8,128)(2,1)S(1)}, f32[32,640]{1,0:T(8,128)S(1)}, bf16[32,120,128]{2,1,0:T(8,128)(2,1)}) custom-call(bf16[9,20,640]{2,1,0:T(8,128)(2,1)} %weight_hbm.1, bf16[4,4,4,640]{3,2,1,0:T(4,128)(2,1)} %state_hbm.1, s32[2,4,4,4,640]{4,3,2,1,0:T(4,128)} %signs_hbm.1), custom_call_target="tpu_custom_call" | custom-call | tf_op jit(solution)/shard_map/pack/pallas_call | solution.py:368
  2.8 13.6 %all-to-all-start = ((bf16[32,120,128]{2,1,0:T(8,128)(2,1)}), bf16[32,120,128]{2,1,0:T(8,128)(2,1)}, u32[]{:S(2)}, u32[]{:S(2)}) async-start(bf16[32,120,128]{2,1,0:T(8,128)(2,1)} %get-tuple-element.12), calls=%async_computation | async-start | bytes 1966080 | tf_op jit(solution)/shard_map/all_to_all | solution.py:406
  16.4 8.8 %collective-permute-start = (bf16[56,640]{1,0:T(8,128)(2,1)S(1)}, bf16[56,640]{1,0:T(8,128)(2,1)S(1)}, u32[]{:S(2)}, u32[]{:S(2)}) collective-permute-start(bf16[56,640]{1,0:T(8,128)(2,1)S(1)} %get-tuple-element.11), channel_id=1, source_target_pairs={{0,96},{32,64},{64,32},{96,0},{1,97},{33,65},{65,33},{97,1},{2,98}... | collective-permute-start | bytes 215048 | tf_op jit(solution)/shard_map/ppermute | solution.py:405
  25.2 21.2 %collective-permute-done = bf16[56,640]{1,0:T(8,128)(2,1)S(1)} collective-permute-done((bf16[56,640]{1,0:T(8,128)(2,1)S(1)}, bf16[56,640]{1,0:T(8,128)(2,1)S(1)}, u32[]{:S(2)}, u32[]{:S(2)}) %collective-permute-start) | collective-permute-done | bytes 71712 | tf_op jit(solution)/shard_map/ppermute | solution.py:405
  46.4 4.4 %collective-permute-start.2 = (bf16[256,640]{1,0:T(8,128)(2,1)S(1)}, bf16[256,640]{1,0:T(8,128)(2,1)S(1)}, u32[]{:S(2)}, u32[]{:S(2)}) collective-permute-start(bf16[256,640]{1,0:T(8,128)(2,1)S(1)} %pad_maximum_fusion.own0), channel_id=1, source_target_pairs={{0,384},{128,0},{256,128},{384,256},{1,385},{129,1},{257,129},{385... | collective-permute-start | bytes 983048 | tf_op jit(solution)/shard_map/ppermute | solution.py:411
  50.8 1.9 %collective-permute-start.1 = (bf16[256,640]{1,0:T(8,128)(2,1)S(1)}, bf16[256,640]{1,0:T(8,128)(2,1)S(1)}, u32[]{:S(2)}, u32[]{:S(2)}) collective-permute-start(bf16[256,640]{1,0:T(8,128)(2,1)S(1)} %pad_maximum_fusion.own0), channel_id=1, source_target_pairs={{0,128},{128,256},{256,384},{384,0},{1,129},{129,257},{257,385},{3... | collective-permute-start | bytes 983048 | tf_op jit(solution)/shard_map/ppermute | solution.py:410
  52.8 2.3 %collective-permute-start.4 = (bf16[256,640]{1,0:T(8,128)(2,1)S(1)}, bf16[256,640]{1,0:T(8,128)(2,1)S(1)}, u32[]{:S(2)}, u32[]{:S(2)}) collective-permute-start(bf16[256,640]{1,0:T(8,128)(2,1)S(1)} %pad_maximum_fusion.own0), channel_id=1, source_target_pairs={{0,32},{32,0},{1,33},{33,1},{2,34},{34,2},{3,35},{35,3},{4,36},{36... | collective-permute-start | bytes 983048 | tf_op jit(solution)/shard_map/ppermute | solution.py:419
  55.1 2.7 %collective-permute-done.2.own3 = bf16[256,640]{1,0:T(8,128)(2,1)S(1)} collective-permute-done((bf16[256,640]{1,0:T(8,128)(2,1)S(1)}, bf16[256,640]{1,0:T(8,128)(2,1)S(1)}, u32[]{:S(2)}, u32[]{:S(2)}) %collective-permute-start.2) | collective-permute-done | bytes 327712 | tf_op jit(solution)/shard_map/ppermute | solution.py:411
  57.8 5.0 %collective-permute-done.1.own1 = bf16[256,640]{1,0:T(8,128)(2,1)S(1)} collective-permute-done((bf16[256,640]{1,0:T(8,128)(2,1)S(1)}, bf16[256,640]{1,0:T(8,128)(2,1)S(1)}, u32[]{:S(2)}, u32[]{:S(2)}) %collective-permute-start.1) | collective-permute-done | bytes 327712 | tf_op jit(solution)/shard_map/ppermute | solution.py:410
  62.8 0.1 broadcast_select_fusion
  62.9 1.9 %collective-permute-start.7 = (bf16[256,640]{1,0:T(8,128)(2,1)S(1)}, bf16[256,640]{1,0:T(8,128)(2,1)S(1)}, u32[]{:S(2)}, u32[]{:S(2)}) collective-permute-start(bf16[256,640]{1,0:T(8,128)(2,1)S(1)} %get-tuple-element.18), channel_id=1, source_target_pairs={{0,416},{32,128},{128,32},{160,256},{256,160},{288,384},{384,288},... | collective-permute-start | bytes 983048 | tf_op jit(solution)/shard_map/ppermute | solution.py:416
  64.8 3.1 %collective-permute-start.6 = (bf16[256,640]{1,0:T(8,128)(2,1)S(1)}, bf16[256,640]{1,0:T(8,128)(2,1)S(1)}, u32[]{:S(2)}, u32[]{:S(2)}) collective-permute-start(bf16[256,640]{1,0:T(8,128)(2,1)S(1)} %collective-permute-done.2.own3), channel_id=1, source_target_pairs={{0,32},{32,0},{1,33},{33,1},{2,34},{34,2},{3,35},{35,3},{4,36},{36... | collective-permute-start | bytes 983048 | tf_op jit(solution)/shard_map/ppermute | solution.py:420
  68.0 1.9 %collective-permute-start.5 = (bf16[256,640]{1,0:T(8,128)(2,1)S(1)}, bf16[256,640]{1,0:T(8,128)(2,1)S(1)}, u32[]{:S(2)}, u32[]{:S(2)}) collective-permute-start(bf16[256,640]{1,0:T(8,128)(2,1)S(1)} %collective-permute-done.1.own1), channel_id=1, source_target_pairs={{0,32},{32,0},{1,33},{33,1},{2,34},{34,2},{3,35},{35,3},{4,36},{36... | collective-permute-start | bytes 983048 | tf_op jit(solution)/shard_map/ppermute | solution.py:420
  69.9 5.0 %collective-permute-start.3 = (bf16[256,640]{1,0:T(8,128)(2,1)S(1)}, bf16[256,640]{1,0:T(8,128)(2,1)S(1)}, u32[]{:S(2)}, u32[]{:S(2)}) collective-permute-start(bf16[256,640]{1,0:T(8,128)(2,1)S(1)} %get-tuple-element.19), channel_id=1, source_target_pairs={{0,128},{32,416},{128,256},{160,32},{256,384},{288,160},{384,0},{4... | collective-permute-start | bytes 983048 | tf_op jit(solution)/shard_map/ppermute | solution.py:415
  74.9 0.0 copy-done.1
  74.9 0.0 copy-done.2
  74.9 0.0 copy-done.3
  74.9 0.0 copy-done
  75.0 1.4 %lookup.1 = (f32[8,640]{1,0:T(8,128)S(1)}, f32[32,640]{1,0:T(8,128)S(1)}) custom-call(s32[4]{0:T(128)S(1)} %copy-done, f32[1000,640]{1,0:T(8,128)} %table_hbm.1, f32[1,640]{1,0:T(1,128)S(1)} %broadcast_in_dim.10.shift_ref, f32[1,640]{1,0:T(1,128)S(1)} %broadcast_in_dim.11.bias_ref, f32[32,640]{1,0:T(8,128)S(1)} %get-tuple-element.13.base_ref), custom_call_target="tpu_custom_call" | custom-call | tf_op jit(solution)/shard_map/lookup/pallas_call | solution.py:394
  76.3 0.0 collective-permute-done.4.other0
  76.3 0.0 collective-permute-done.6.other3
  76.3 0.0 collective-permute-done.5.other1
  76.4 0.0 collective-permute-done.7.other2
  76.4 2.5 %collective-permute-done.3.own2 = bf16[256,640]{1,0:T(8,128)(2,1)S(1)} collective-permute-done((bf16[256,640]{1,0:T(8,128)(2,1)S(1)}, bf16[256,640]{1,0:T(8,128)(2,1)S(1)}, u32[]{:S(2)}, u32[]{:S(2)}) %collective-permute-start.3) | collective-permute-done | bytes 327712 | tf_op jit(solution)/shard_map/ppermute | solution.py:415
  78.9 0.0 all-to-all-done.weight_hbm
  78.9 6.5 %mix.1 = f32[8,72,128]{2,1,0:T(8,128)S(1)} custom-call(bf16[256,640]{1,0:T(8,128)(2,1)S(1)} %pad_maximum_fusion.own0, bf16[256,640]{1,0:T(8,128)(2,1)S(1)} %collective-permute-done.1.own1, bf16[256,640]{1,0:T(8,128)(2,1)S(1)} %collective-permute-done.2.own3, bf16[256,640]{1,0:T(8,128)(2,1)S(1)} %collective-permute-done.3.own2, ...), custom_call_target="tpu_custom_call" | custom-call | tf_op jit(solution)/shard_map/mix/pallas_call | solution.py:423
  85.4 11.9 %all_to_all.15.parts_ref = f32[8,72,128]{2,1,0:T(8,128)S(1)} all-to-all(f32[8,72,128]{2,1,0:T(8,128)S(1)} %mix.1), channel_id=1, replica_groups=mesh['gy'=4,'gx_0'=2,'gx_1'=2,'probe_0'=8,'probe_1'=4] {'gy','gx_1'}, dimensions={0} | all-to-all | bytes 589824 | tf_op jit(solution)/shard_map/all_to_all | solution.py:445
  97.2 0.7 step.1
  97.9 9.7 %all-to-all-start.2 = ((f32[64,1,128]{2,1,0:T(1,128)}), f32[64,1,128]{2,1,0:T(1,128)S(1)}, u32[]{:S(2)}, u32[]{:S(2)}) async-start(f32[64,1,128]{2,1,0:T(1,128)} %bitcast.1), calls=%async_computation.2 | async-start | bytes 65536 | tf_op jit(solution)/shard_map/all_to_all | solution.py:454
  107.7 2.9 %collective-permute-start.8 = (bf16[32,640]{1,0:T(8,128)(2,1)S(1)}, bf16[32,640]{1,0:T(8,128)(2,1)S(1)}, u32[]{:S(2)}, u32[]{:S(2)}) collective-permute-start(bf16[32,640]{1,0:T(8,128)(2,1)S(1)} %get-tuple-element.17.refs_1_), channel_id=1, source_target_pairs={{0,4},{4,0},{8,12},{12,8},{16,20},{20,16},{24,28},{28,24},{1,5},{5... | collective-permute-start | bytes 122888 | tf_op jit(solution)/shard_map/ppermute | solution.py:456
  110.6 2.1 %collective-permute-done.8.refs_2_ = bf16[32,640]{1,0:T(8,128)(2,1)S(1)} collective-permute-done((bf16[32,640]{1,0:T(8,128)(2,1)S(1)}, bf16[32,640]{1,0:T(8,128)(2,1)S(1)}, u32[]{:S(2)}, u32[]{:S(2)}) %collective-permute-start.8) | collective-permute-done | bytes 40992 | tf_op jit(solution)/shard_map/ppermute | solution.py:456
  112.7 5.9 %all-to-all-done.2 = f32[64,1,128]{2,1,0:T(1,128)S(1)} async-done(((f32[64,1,128]{2,1,0:T(1,128)}), f32[64,1,128]{2,1,0:T(1,128)S(1)}, u32[]{:S(2)}, u32[]{:S(2)}) %all-to-all-start.2) | async-done | bytes 32800 | tf_op jit(solution)/shard_map/all_to_all | solution.py:454
  118.6 0.7 final.1
  (5 shorter events, 0.0 us)
Async XLA Ops:
  0.6 74.2 %copy-start.1 = (f32[640]{0:T(1024)S(1)}, f32[640]{0:T(1024)}, u32[]{:S(2)}) copy-start(f32[640]{0:T(1024)} %param.12) | copy-start | bytes 7684
  0.6 74.3 %copy-start.2 = (f32[640]{0:T(1024)S(1)}, f32[640]{0:T(1024)}, u32[]{:S(2)}) copy-start(f32[640]{0:T(1024)} %param.13) | copy-start | bytes 7684
  0.7 74.3 %copy-start.3 = (f32[640]{0:T(1024)S(1)}, f32[640]{0:T(1024)}, u32[]{:S(2)}) copy-start(f32[640]{0:T(1024)} %param.15) | copy-start | bytes 7684
  0.7 74.3 %copy-start = (s32[4]{0:T(128)S(1)}, s32[4]{0:T(128)}, u32[]{:S(2)}) copy-start(s32[4]{0:T(128)} %step_ref.1) | copy-start | bytes 52
  2.8 76.1 %all-to-all-start = ((bf16[32,120,128]{2,1,0:T(8,128)(2,1)}), bf16[32,120,128]{2,1,0:T(8,128)(2,1)}, u32[]{:S(2)}, u32[]{:S(2)}) async-start(bf16[32,120,128]{2,1,0:T(8,128)(2,1)} %get-tuple-element.12), calls=%async_computation | async-start | bytes 1966080 | tf_op jit(solution)/shard_map/all_to_all | solution.py:406
  16.4 30.0 %collective-permute-start = (bf16[56,640]{1,0:T(8,128)(2,1)S(1)}, bf16[56,640]{1,0:T(8,128)(2,1)S(1)}, u32[]{:S(2)}, u32[]{:S(2)}) collective-permute-start(bf16[56,640]{1,0:T(8,128)(2,1)S(1)} %get-tuple-element.11), channel_id=1, source_target_pairs={{0,96},{32,64},{64,32},{96,0},{1,97},{33,65},{65,33},{97,1},{2,98}... | collective-permute-start | bytes 215048 | tf_op jit(solution)/shard_map/ppermute | solution.py:405
  46.4 11.3 %collective-permute-start.2 = (bf16[256,640]{1,0:T(8,128)(2,1)S(1)}, bf16[256,640]{1,0:T(8,128)(2,1)S(1)}, u32[]{:S(2)}, u32[]{:S(2)}) collective-permute-start(bf16[256,640]{1,0:T(8,128)(2,1)S(1)} %pad_maximum_fusion.own0), channel_id=1, source_target_pairs={{0,384},{128,0},{256,128},{384,256},{1,385},{129,1},{257,129},{385... | collective-permute-start | bytes 983048 | tf_op jit(solution)/shard_map/ppermute | solution.py:411
  50.8 12.0 %collective-permute-start.1 = (bf16[256,640]{1,0:T(8,128)(2,1)S(1)}, bf16[256,640]{1,0:T(8,128)(2,1)S(1)}, u32[]{:S(2)}, u32[]{:S(2)}) collective-permute-start(bf16[256,640]{1,0:T(8,128)(2,1)S(1)} %pad_maximum_fusion.own0), channel_id=1, source_target_pairs={{0,128},{128,256},{256,384},{384,0},{1,129},{129,257},{257,385},{3... | collective-permute-start | bytes 983048 | tf_op jit(solution)/shard_map/ppermute | solution.py:410
  52.8 23.6 %collective-permute-start.4 = (bf16[256,640]{1,0:T(8,128)(2,1)S(1)}, bf16[256,640]{1,0:T(8,128)(2,1)S(1)}, u32[]{:S(2)}, u32[]{:S(2)}) collective-permute-start(bf16[256,640]{1,0:T(8,128)(2,1)S(1)} %pad_maximum_fusion.own0), channel_id=1, source_target_pairs={{0,32},{32,0},{1,33},{33,1},{2,34},{34,2},{3,35},{35,3},{4,36},{36... | collective-permute-start | bytes 983048 | tf_op jit(solution)/shard_map/ppermute | solution.py:419
  62.9 13.5 %collective-permute-start.7 = (bf16[256,640]{1,0:T(8,128)(2,1)S(1)}, bf16[256,640]{1,0:T(8,128)(2,1)S(1)}, u32[]{:S(2)}, u32[]{:S(2)}) collective-permute-start(bf16[256,640]{1,0:T(8,128)(2,1)S(1)} %get-tuple-element.18), channel_id=1, source_target_pairs={{0,416},{32,128},{128,32},{160,256},{256,160},{288,384},{384,288},... | collective-permute-start | bytes 983048 | tf_op jit(solution)/shard_map/ppermute | solution.py:416
  64.8 11.5 %collective-permute-start.6 = (bf16[256,640]{1,0:T(8,128)(2,1)S(1)}, bf16[256,640]{1,0:T(8,128)(2,1)S(1)}, u32[]{:S(2)}, u32[]{:S(2)}) collective-permute-start(bf16[256,640]{1,0:T(8,128)(2,1)S(1)} %collective-permute-done.2.own3), channel_id=1, source_target_pairs={{0,32},{32,0},{1,33},{33,1},{2,34},{34,2},{3,35},{35,3},{4,36},{36... | collective-permute-start | bytes 983048 | tf_op jit(solution)/shard_map/ppermute | solution.py:420
  68.0 8.4 %collective-permute-start.5 = (bf16[256,640]{1,0:T(8,128)(2,1)S(1)}, bf16[256,640]{1,0:T(8,128)(2,1)S(1)}, u32[]{:S(2)}, u32[]{:S(2)}) collective-permute-start(bf16[256,640]{1,0:T(8,128)(2,1)S(1)} %collective-permute-done.1.own1), channel_id=1, source_target_pairs={{0,32},{32,0},{1,33},{33,1},{2,34},{34,2},{3,35},{35,3},{4,36},{36... | collective-permute-start | bytes 983048 | tf_op jit(solution)/shard_map/ppermute | solution.py:420
  69.9 9.0 %collective-permute-start.3 = (bf16[256,640]{1,0:T(8,128)(2,1)S(1)}, bf16[256,640]{1,0:T(8,128)(2,1)S(1)}, u32[]{:S(2)}, u32[]{:S(2)}) collective-permute-start(bf16[256,640]{1,0:T(8,128)(2,1)S(1)} %get-tuple-element.19), channel_id=1, source_target_pairs={{0,128},{32,416},{128,256},{160,32},{256,384},{288,160},{384,0},{4... | collective-permute-start | bytes 983048 | tf_op jit(solution)/shard_map/ppermute | solution.py:415
  97.9 20.6 %all-to-all-start.2 = ((f32[64,1,128]{2,1,0:T(1,128)}), f32[64,1,128]{2,1,0:T(1,128)S(1)}, u32[]{:S(2)}, u32[]{:S(2)}) async-start(f32[64,1,128]{2,1,0:T(1,128)} %bitcast.1), calls=%async_computation.2 | async-start | bytes 65536 | tf_op jit(solution)/shard_map/all_to_all | solution.py:454
  107.7 5.0 %collective-permute-start.8 = (bf16[32,640]{1,0:T(8,128)(2,1)S(1)}, bf16[32,640]{1,0:T(8,128)(2,1)S(1)}, u32[]{:S(2)}, u32[]{:S(2)}) collective-permute-start(bf16[32,640]{1,0:T(8,128)(2,1)S(1)} %get-tuple-element.17.refs_1_), channel_id=1, source_target_pairs={{0,4},{4,0},{8,12},{12,8},{16,20},{20,16},{24,28},{28,24},{1,5},{5... | collective-permute-start | bytes 122888 | tf_op jit(solution)/shard_map/ppermute | solution.py:456

commit v10 on v8

--- a/solution.py
+++ b/solution.py
@@ -90,7 +90,7 @@
         for o in range(blocks):
             picked = picked + jnp.where(ob == o, rows[:, lane_block(o)], 0.0)
         wf[pl.ds(index, rows.shape[0], stride=PAIRS), :] = picked
-    packed = wf[...].astype(BF16)
+    packed = wf[0 : wsend_ref.shape[1], :].astype(BF16)
     for target in range(wsend_ref.shape[0]):
         wsend_ref[target] = packed
     leave = pltpu.make_async_copy(wsend_ref, wsend_hbm, left)
@@ -146,8 +146,8 @@
         rim[48:56, lane_block(index)] = part.astype(F32)
 
     for o in range(blocks):
-        main_ref[0:128, lane_block(o)] = uf[o].astype(BF16)
-        main_ref[128:192, lane_block(o)] = xf[o].astype(BF16)
+        main_ref[0:128, lane_block(o)] = uf[o, 0:128, :].astype(BF16)
+        main_ref[128:192, lane_block(o)] = xf[o, 0:64, :].astype(BF16)
     rim_ref[...] = rim[...].astype(BF16)
     leave.wait()
 
@@ -348,7 +348,7 @@
         out_ref[b] = scale * jnp.sum(jnp.where(lane == b, total, 0.0))
     for start, rows in ((half_rows(), rows0), (2 - half_rows(), rows1)):
         for o in range(blocks):
-            lines[o] = rows[:, lane_block(o)].astype(F32)
+            lines[o, 0:32, :] = rows[:, lane_block(o)].astype(F32)
         for o in range(blocks):
             for b in range(4):
                 for r in range(2):
@@ -380,9 +380,9 @@
             pltpu.VMEM(conv_weight.shape, BF16),
             pltpu.VMEM(state.shape, BF16),
             pltpu.VMEM(probe_signs.shape, jnp.int32),
-            pltpu.VMEM((blocks, 128, LANES), F32),
-            pltpu.VMEM((blocks, 64, LANES), F32),
-            pltpu.VMEM((each, LANES), F32),
+            pltpu.VMEM((blocks, 192, LANES), F32),
+            pltpu.VMEM((blocks, 96, LANES), F32),
+            pltpu.VMEM((each + 40, LANES), F32),
             pltpu.VMEM((32, each, LANES), BF16),
             pltpu.VMEM((56, chans), F32),
             pltpu.VMEM((32, chans), F32),
@@ -461,7 +461,7 @@
         out_shape=(shape(state.shape, BF16), shape((4,), F32)),
         in_specs=[VMEM] * 3,
         out_specs=(VMEM, SMEM),
-        scratch_shapes=[pltpu.VMEM((blocks, 32, LANES), F32)],
+        scratch_shapes=[pltpu.VMEM((blocks, 64, LANES), F32)],
         compiler_params=params,
         name="final",
     )(mass.reshape(64, LANES), rows, facing_rows)

time: 120 us -> 120 us (level)
  no operation moved by 1% of the time
where the time goes in v10:
time: 120 us; the launch traced here: 119 us
  starting transfers between devices  55.5 us (46%)
  waiting for transfers between devices  39.5 us (33%)
  blocking collectives  11.9 us (10%)
  Pallas kernels  11.1 us (9%)
    ppermute x1, waiting for transfers between devices, body(): facing = lax.ppermute(rim, GX, across)  21.2 us
    all_to_all x1, starting transfers between devices, body(): weights = lax.all_to_all(wsend, PROBE, 0, 0, tiled=True)  13.6 us
    all_to_all x1, blocking collectives, body(): partial = lax.all_to_all(partial, ('gy', 'gx_1'), 0, 0, tiled=True)  11.9 us
    all_to_all x1, starting transfers between devices, body(): lax.all_to_all(mass.reshape(64, 1, LANES), ('gx_0',) + PROBE, 0, 0, tiled...  9.71 us
    ppermute x1, starting transfers between devices, body(): facing = lax.ppermute(rim, GX, across)  8.78 us
    pallas_call x1, Pallas kernels, body(): pl.pallas_call(mix_kernel, out_shape=shape((8, 72, LANES), F32), in_specs...  6.21 us
    all_to_all x1, waiting for transfers between devices, body(): lax.all_to_all(mass.reshape(64, 1, LANES), ('gx_0',) + PROBE, 0, 0, tiled...  5.86 us
    ppermute x2, starting transfers between devices, body(): other += [lax.ppermute(tile, 'gx_1', swap) for tile in (above, below)]  5.06 us
  transfers between devices with their start and end apart: 11, of which 6 were waited for; matrix products, arithmetic and copies ran while one was open for 0% of the time, Pallas kernels for 1%

profile of v10, /device:TPU:1, one launch (start us, length us, event | category | flops | bytes accessed | tf_op | source)
XLA Modules:
  0.0 119.0 jit_solution(111583829190865869)
XLA Ops:
  0.6 0.0 copy-start.1
  0.6 0.0 copy-start.2
  0.7 0.0 copy-start.3
  0.7 0.0 copy-start
  0.7 2.1 %pack.1 = (bf16[192,640]{1,0:T(8,128)(2,1)S(1)}, bf16[56,640]{1,0:T(8,128)(2,1)S(1)}, f32[32,640]{1,0:T(8,128)S(1)}, bf16[32,120,128]{2,1,0:T(8,128)(2,1)}) custom-call(bf16[9,20,640]{2,1,0:T(8,128)(2,1)} %weight_hbm.1, bf16[4,4,4,640]{3,2,1,0:T(4,128)(2,1)} %state_hbm.1, s32[2,4,4,4,640]{4,3,2,1,0:T(4,128)} %signs_hbm.1), custom_call_target="tpu_custom_call" | custom-call | tf_op jit(solution)/shard_map/pack/pallas_call | solution.py:369
  2.8 13.6 %all-to-all-start = ((bf16[32,120,128]{2,1,0:T(8,128)(2,1)}), bf16[32,120,128]{2,1,0:T(8,128)(2,1)}, u32[]{:S(2)}, u32[]{:S(2)}) async-start(bf16[32,120,128]{2,1,0:T(8,128)(2,1)} %get-tuple-element.12), calls=%async_computation | async-start | bytes 1966080 | tf_op jit(solution)/shard_map/all_to_all | solution.py:407
  16.4 8.8 %collective-permute-start = (bf16[56,640]{1,0:T(8,128)(2,1)S(1)}, bf16[56,640]{1,0:T(8,128)(2,1)S(1)}, u32[]{:S(2)}, u32[]{:S(2)}) collective-permute-start(bf16[56,640]{1,0:T(8,128)(2,1)S(1)} %get-tuple-element.11), channel_id=1, source_target_pairs={{0,96},{32,64},{64,32},{96,0},{1,97},{33,65},{65,33},{97,1},{2,98}... | collective-permute-start | bytes 215048 | tf_op jit(solution)/shard_map/ppermute | solution.py:406
  25.2 21.2 %collective-permute-done = bf16[56,640]{1,0:T(8,128)(2,1)S(1)} collective-permute-done((bf16[56,640]{1,0:T(8,128)(2,1)S(1)}, bf16[56,640]{1,0:T(8,128)(2,1)S(1)}, u32[]{:S(2)}, u32[]{:S(2)}) %collective-permute-start) | collective-permute-done | bytes 71712 | tf_op jit(solution)/shard_map/ppermute | solution.py:406
  46.4 4.4 %collective-permute-start.2 = (bf16[256,640]{1,0:T(8,128)(2,1)S(1)}, bf16[256,640]{1,0:T(8,128)(2,1)S(1)}, u32[]{:S(2)}, u32[]{:S(2)}) collective-permute-start(bf16[256,640]{1,0:T(8,128)(2,1)S(1)} %pad_maximum_fusion.own0), channel_id=1, source_target_pairs={{0,384},{128,0},{256,128},{384,256},{1,385},{129,1},{257,129},{385... | collective-permute-start | bytes 983048 | tf_op jit(solution)/shard_map/ppermute | solution.py:412
  50.8 1.9 %collective-permute-start.1 = (bf16[256,640]{1,0:T(8,128)(2,1)S(1)}, bf16[256,640]{1,0:T(8,128)(2,1)S(1)}, u32[]{:S(2)}, u32[]{:S(2)}) collective-permute-start(bf16[256,640]{1,0:T(8,128)(2,1)S(1)} %pad_maximum_fusion.own0), channel_id=1, source_target_pairs={{0,128},{128,256},{256,384},{384,0},{1,129},{129,257},{257,385},{3... | collective-permute-start | bytes 983048 | tf_op jit(solution)/shard_map/ppermute | solution.py:411
  52.8 2.3 %collective-permute-start.4 = (bf16[256,640]{1,0:T(8,128)(2,1)S(1)}, bf16[256,640]{1,0:T(8,128)(2,1)S(1)}, u32[]{:S(2)}, u32[]{:S(2)}) collective-permute-start(bf16[256,640]{1,0:T(8,128)(2,1)S(1)} %pad_maximum_fusion.own0), channel_id=1, source_target_pairs={{0,32},{32,0},{1,33},{33,1},{2,34},{34,2},{3,35},{35,3},{4,36},{36... | collective-permute-start | bytes 983048 | tf_op jit(solution)/shard_map/ppermute | solution.py:420
  55.1 2.7 %collective-permute-done.2.own3 = bf16[256,640]{1,0:T(8,128)(2,1)S(1)} collective-permute-done((bf16[256,640]{1,0:T(8,128)(2,1)S(1)}, bf16[256,640]{1,0:T(8,128)(2,1)S(1)}, u32[]{:S(2)}, u32[]{:S(2)}) %collective-permute-start.2) | collective-permute-done | bytes 327712 | tf_op jit(solution)/shard_map/ppermute | solution.py:412
  57.8 5.0 %collective-permute-done.1.own1 = bf16[256,640]{1,0:T(8,128)(2,1)S(1)} collective-permute-done((bf16[256,640]{1,0:T(8,128)(2,1)S(1)}, bf16[256,640]{1,0:T(8,128)(2,1)S(1)}, u32[]{:S(2)}, u32[]{:S(2)}) %collective-permute-start.1) | collective-permute-done | bytes 327712 | tf_op jit(solution)/shard_map/ppermute | solution.py:411
  62.8 0.1 broadcast_select_fusion
  62.9 1.9 %collective-permute-start.7 = (bf16[256,640]{1,0:T(8,128)(2,1)S(1)}, bf16[256,640]{1,0:T(8,128)(2,1)S(1)}, u32[]{:S(2)}, u32[]{:S(2)}) collective-permute-start(bf16[256,640]{1,0:T(8,128)(2,1)S(1)} %get-tuple-element.18), channel_id=1, source_target_pairs={{0,416},{32,128},{128,32},{160,256},{256,160},{288,384},{384,288},... | collective-permute-start | bytes 983048 | tf_op jit(solution)/shard_map/ppermute | solution.py:417
  64.8 3.1 %collective-permute-start.6 = (bf16[256,640]{1,0:T(8,128)(2,1)S(1)}, bf16[256,640]{1,0:T(8,128)(2,1)S(1)}, u32[]{:S(2)}, u32[]{:S(2)}) collective-permute-start(bf16[256,640]{1,0:T(8,128)(2,1)S(1)} %collective-permute-done.2.own3), channel_id=1, source_target_pairs={{0,32},{32,0},{1,33},{33,1},{2,34},{34,2},{3,35},{35,3},{4,36},{36... | collective-permute-start | bytes 983048 | tf_op jit(solution)/shard_map/ppermute | solution.py:421
  68.0 1.9 %collective-permute-start.5 = (bf16[256,640]{1,0:T(8,128)(2,1)S(1)}, bf16[256,640]{1,0:T(8,128)(2,1)S(1)}, u32[]{:S(2)}, u32[]{:S(2)}) collective-permute-start(bf16[256,640]{1,0:T(8,128)(2,1)S(1)} %collective-permute-done.1.own1), channel_id=1, source_target_pairs={{0,32},{32,0},{1,33},{33,1},{2,34},{34,2},{3,35},{35,3},{4,36},{36... | collective-permute-start | bytes 983048 | tf_op jit(solution)/shard_map/ppermute | solution.py:421
  69.9 5.0 %collective-permute-start.3 = (bf16[256,640]{1,0:T(8,128)(2,1)S(1)}, bf16[256,640]{1,0:T(8,128)(2,1)S(1)}, u32[]{:S(2)}, u32[]{:S(2)}) collective-permute-start(bf16[256,640]{1,0:T(8,128)(2,1)S(1)} %get-tuple-element.19), channel_id=1, source_target_pairs={{0,128},{32,416},{128,256},{160,32},{256,384},{288,160},{384,0},{4... | collective-permute-start | bytes 983048 | tf_op jit(solution)/shard_map/ppermute | solution.py:416
  74.9 0.0 copy-done.1
  74.9 0.0 copy-done.2
  74.9 0.0 copy-done.3
  74.9 0.0 copy-done
  75.0 1.4 %lookup.1 = (f32[8,640]{1,0:T(8,128)S(1)}, f32[32,640]{1,0:T(8,128)S(1)}) custom-call(s32[4]{0:T(128)S(1)} %copy-done, f32[1000,640]{1,0:T(8,128)} %table_hbm.1, f32[1,640]{1,0:T(1,128)S(1)} %broadcast_in_dim.10.shift_ref, f32[1,640]{1,0:T(1,128)S(1)} %broadcast_in_dim.11.bias_ref, f32[32,640]{1,0:T(8,128)S(1)} %get-tuple-element.13.base_ref), custom_call_target="tpu_custom_call" | custom-call | tf_op jit(solution)/shard_map/lookup/pallas_call | solution.py:395
  76.3 0.0 collective-permute-done.4.other0
  76.3 0.0 collective-permute-done.6.other3
  76.3 0.0 collective-permute-done.5.other1
  76.4 0.0 collective-permute-done.7.other2
  76.4 2.5 %collective-permute-done.3.own2 = bf16[256,640]{1,0:T(8,128)(2,1)S(1)} collective-permute-done((bf16[256,640]{1,0:T(8,128)(2,1)S(1)}, bf16[256,640]{1,0:T(8,128)(2,1)S(1)}, u32[]{:S(2)}, u32[]{:S(2)}) %collective-permute-start.3) | collective-permute-done | bytes 327712 | tf_op jit(solution)/shard_map/ppermute | solution.py:416
  78.9 0.0 all-to-all-done.weight_hbm
  78.9 6.2 %mix.1 = f32[8,72,128]{2,1,0:T(8,128)S(1)} custom-call(bf16[256,640]{1,0:T(8,128)(2,1)S(1)} %pad_maximum_fusion.own0, bf16[256,640]{1,0:T(8,128)(2,1)S(1)} %collective-permute-done.1.own1, bf16[256,640]{1,0:T(8,128)(2,1)S(1)} %collective-permute-done.2.own3, bf16[256,640]{1,0:T(8,128)(2,1)S(1)} %collective-permute-done.3.own2, ...), custom_call_target="tpu_custom_call" | custom-call | tf_op jit(solution)/shard_map/mix/pallas_call | solution.py:424
  85.1 11.9 %all_to_all.15.parts_ref = f32[8,72,128]{2,1,0:T(8,128)S(1)} all-to-all(f32[8,72,128]{2,1,0:T(8,128)S(1)} %mix.1), channel_id=1, replica_groups=mesh['gy'=4,'gx_0'=2,'gx_1'=2,'probe_0'=8,'probe_1'=4] {'gy','gx_1'}, dimensions={0} | all-to-all | bytes 589824 | tf_op jit(solution)/shard_map/all_to_all | solution.py:446
  97.0 0.7 step.1
  97.7 9.7 %all-to-all-start.2 = ((f32[64,1,128]{2,1,0:T(1,128)}), f32[64,1,128]{2,1,0:T(1,128)S(1)}, u32[]{:S(2)}, u32[]{:S(2)}) async-start(f32[64,1,128]{2,1,0:T(1,128)} %bitcast.1), calls=%async_computation.2 | async-start | bytes 65536 | tf_op jit(solution)/shard_map/all_to_all | solution.py:455
  107.4 2.9 %collective-permute-start.8 = (bf16[32,640]{1,0:T(8,128)(2,1)S(1)}, bf16[32,640]{1,0:T(8,128)(2,1)S(1)}, u32[]{:S(2)}, u32[]{:S(2)}) collective-permute-start(bf16[32,640]{1,0:T(8,128)(2,1)S(1)} %get-tuple-element.17.refs_1_), channel_id=1, source_target_pairs={{0,4},{4,0},{8,12},{12,8},{16,20},{20,16},{24,28},{28,24},{1,5},{5... | collective-permute-start | bytes 122888 | tf_op jit(solution)/shard_map/ppermute | solution.py:457
  110.3 2.1 %collective-permute-done.8.refs_2_ = bf16[32,640]{1,0:T(8,128)(2,1)S(1)} collective-permute-done((bf16[32,640]{1,0:T(8,128)(2,1)S(1)}, bf16[32,640]{1,0:T(8,128)(2,1)S(1)}, u32[]{:S(2)}, u32[]{:S(2)}) %collective-permute-start.8) | collective-permute-done | bytes 40992 | tf_op jit(solution)/shard_map/ppermute | solution.py:457
  112.4 5.9 %all-to-all-done.2 = f32[64,1,128]{2,1,0:T(1,128)S(1)} async-done(((f32[64,1,128]{2,1,0:T(1,128)}), f32[64,1,128]{2,1,0:T(1,128)S(1)}, u32[]{:S(2)}, u32[]{:S(2)}) %all-to-all-start.2) | async-done | bytes 32800 | tf_op jit(solution)/shard_map/all_to_all | solution.py:455
  118.3 0.7 final.1
  (5 shorter events, 0.0 us)
Async XLA Ops:
  0.6 74.2 %copy-start.1 = (f32[640]{0:T(1024)S(1)}, f32[640]{0:T(1024)}, u32[]{:S(2)}) copy-start(f32[640]{0:T(1024)} %param.12) | copy-start | bytes 7684
  0.6 74.3 %copy-start.2 = (f32[640]{0:T(1024)S(1)}, f32[640]{0:T(1024)}, u32[]{:S(2)}) copy-start(f32[640]{0:T(1024)} %param.13) | copy-start | bytes 7684
  0.7 74.3 %copy-start.3 = (f32[640]{0:T(1024)S(1)}, f32[640]{0:T(1024)}, u32[]{:S(2)}) copy-start(f32[640]{0:T(1024)} %param.15) | copy-start | bytes 7684
  0.7 74.3 %copy-start = (s32[4]{0:T(128)S(1)}, s32[4]{0:T(128)}, u32[]{:S(2)}) copy-start(s32[4]{0:T(128)} %step_ref.1) | copy-start | bytes 52
  2.8 76.1 %all-to-all-start = ((bf16[32,120,128]{2,1,0:T(8,128)(2,1)}), bf16[32,120,128]{2,1,0:T(8,128)(2,1)}, u32[]{:S(2)}, u32[]{:S(2)}) async-start(bf16[32,120,128]{2,1,0:T(8,128)(2,1)} %get-tuple-element.12), calls=%async_computation | async-start | bytes 1966080 | tf_op jit(solution)/shard_map/all_to_all | solution.py:407
  16.4 30.0 %collective-permute-start = (bf16[56,640]{1,0:T(8,128)(2,1)S(1)}, bf16[56,640]{1,0:T(8,128)(2,1)S(1)}, u32[]{:S(2)}, u32[]{:S(2)}) collective-permute-start(bf16[56,640]{1,0:T(8,128)(2,1)S(1)} %get-tuple-element.11), channel_id=1, source_target_pairs={{0,96},{32,64},{64,32},{96,0},{1,97},{33,65},{65,33},{97,1},{2,98}... | collective-permute-start | bytes 215048 | tf_op jit(solution)/shard_map/ppermute | solution.py:406
  46.4 11.3 %collective-permute-start.2 = (bf16[256,640]{1,0:T(8,128)(2,1)S(1)}, bf16[256,640]{1,0:T(8,128)(2,1)S(1)}, u32[]{:S(2)}, u32[]{:S(2)}) collective-permute-start(bf16[256,640]{1,0:T(8,128)(2,1)S(1)} %pad_maximum_fusion.own0), channel_id=1, source_target_pairs={{0,384},{128,0},{256,128},{384,256},{1,385},{129,1},{257,129},{385... | collective-permute-start | bytes 983048 | tf_op jit(solution)/shard_map/ppermute | solution.py:412
  50.8 12.0 %collective-permute-start.1 = (bf16[256,640]{1,0:T(8,128)(2,1)S(1)}, bf16[256,640]{1,0:T(8,128)(2,1)S(1)}, u32[]{:S(2)}, u32[]{:S(2)}) collective-permute-start(bf16[256,640]{1,0:T(8,128)(2,1)S(1)} %pad_maximum_fusion.own0), channel_id=1, source_target_pairs={{0,128},{128,256},{256,384},{384,0},{1,129},{129,257},{257,385},{3... | collective-permute-start | bytes 983048 | tf_op jit(solution)/shard_map/ppermute | solution.py:411
  52.8 23.6 %collective-permute-start.4 = (bf16[256,640]{1,0:T(8,128)(2,1)S(1)}, bf16[256,640]{1,0:T(8,128)(2,1)S(1)}, u32[]{:S(2)}, u32[]{:S(2)}) collective-permute-start(bf16[256,640]{1,0:T(8,128)(2,1)S(1)} %pad_maximum_fusion.own0), channel_id=1, source_target_pairs={{0,32},{32,0},{1,33},{33,1},{2,34},{34,2},{3,35},{35,3},{4,36},{36... | collective-permute-start | bytes 983048 | tf_op jit(solution)/shard_map/ppermute | solution.py:420
  62.9 13.5 %collective-permute-start.7 = (bf16[256,640]{1,0:T(8,128)(2,1)S(1)}, bf16[256,640]{1,0:T(8,128)(2,1)S(1)}, u32[]{:S(2)}, u32[]{:S(2)}) collective-permute-start(bf16[256,640]{1,0:T(8,128)(2,1)S(1)} %get-tuple-element.18), channel_id=1, source_target_pairs={{0,416},{32,128},{128,32},{160,256},{256,160},{288,384},{384,288},... | collective-permute-start | bytes 983048 | tf_op jit(solution)/shard_map/ppermute | solution.py:417
  64.8 11.5 %collective-permute-start.6 = (bf16[256,640]{1,0:T(8,128)(2,1)S(1)}, bf16[256,640]{1,0:T(8,128)(2,1)S(1)}, u32[]{:S(2)}, u32[]{:S(2)}) collective-permute-start(bf16[256,640]{1,0:T(8,128)(2,1)S(1)} %collective-permute-done.2.own3), channel_id=1, source_target_pairs={{0,32},{32,0},{1,33},{33,1},{2,34},{34,2},{3,35},{35,3},{4,36},{36... | collective-permute-start | bytes 983048 | tf_op jit(solution)/shard_map/ppermute | solution.py:421
  68.0 8.4 %collective-permute-start.5 = (bf16[256,640]{1,0:T(8,128)(2,1)S(1)}, bf16[256,640]{1,0:T(8,128)(2,1)S(1)}, u32[]{:S(2)}, u32[]{:S(2)}) collective-permute-start(bf16[256,640]{1,0:T(8,128)(2,1)S(1)} %collective-permute-done.1.own1), channel_id=1, source_target_pairs={{0,32},{32,0},{1,33},{33,1},{2,34},{34,2},{3,35},{35,3},{4,36},{36... | collective-permute-start | bytes 983048 | tf_op jit(solution)/shard_map/ppermute | solution.py:421
  69.9 9.0 %collective-permute-start.3 = (bf16[256,640]{1,0:T(8,128)(2,1)S(1)}, bf16[256,640]{1,0:T(8,128)(2,1)S(1)}, u32[]{:S(2)}, u32[]{:S(2)}) collective-permute-start(bf16[256,640]{1,0:T(8,128)(2,1)S(1)} %get-tuple-element.19), channel_id=1, source_target_pairs={{0,128},{32,416},{128,256},{160,32},{256,384},{288,160},{384,0},{4... | collective-permute-start | bytes 983048 | tf_op jit(solution)/shard_map/ppermute | solution.py:416
  97.7 20.6 %all-to-all-start.2 = ((f32[64,1,128]{2,1,0:T(1,128)}), f32[64,1,128]{2,1,0:T(1,128)S(1)}, u32[]{:S(2)}, u32[]{:S(2)}) async-start(f32[64,1,128]{2,1,0:T(1,128)} %bitcast.1), calls=%async_computation.2 | async-start | bytes 65536 | tf_op jit(solution)/shard_map/all_to_all | solution.py:455
  107.4 5.0 %collective-permute-start.8 = (bf16[32,640]{1,0:T(8,128)(2,1)S(1)}, bf16[32,640]{1,0:T(8,128)(2,1)S(1)}, u32[]{:S(2)}, u32[]{:S(2)}) collective-permute-start(bf16[32,640]{1,0:T(8,128)(2,1)S(1)} %get-tuple-element.17.refs_1_), channel_id=1, source_target_pairs={{0,4},{4,0},{8,12},{12,8},{16,20},{20,16},{24,28},{28,24},{1,5},{5... | collective-permute-start | bytes 122888 | tf_op jit(solution)/shard_map/ppermute | solution.py:457
